TPU v7x, 32 devices: a whole 2x2x4 slice. The times are simulated.
32 devices in a mesh: fsdp: 2 (over y), blk: 4 (over x, core), head: 4 (over z).
Axes of the slice: x: 2, y: 2, z: 4, core: 2. Of those that a mesh axis runs over, the one named last changes fastest.
Arguments:
- tokens: bfloat16 [4096, 2048], P(('fsdp', 'blk', 'head')), may hold values from -8 to 8
- w_query: bfloat16 [2048, 2048], P(('fsdp', 'blk'), 'head'), may hold values from -0.125 to 0.125
- w_key: bfloat16 [2048, 256], P(('fsdp', 'blk')), may hold values from -0.125 to 0.125
- w_value: bfloat16 [2048, 256], P(('fsdp', 'blk')), may hold values from -0.125 to 0.125
- w_out: bfloat16 [2048, 2048], P(('fsdp', 'blk'), 'head'), may hold values from -0.75 to 0.75
- w_gate: bfloat16 [2048, 5632], P(('fsdp', 'blk'), 'head'), may hold values from -0.125 to 0.125
- w_up: bfloat16 [2048, 5632], P(('fsdp', 'blk'), 'head'), may hold values from -0.125 to 0.125
- w_down: bfloat16 [2048, 5632], P(('fsdp', 'blk'), 'head'), may hold values from -0.078125 to 0.078125
- gain_attn: bfloat16 [2048], P(('fsdp', 'blk')), may hold values from 0.5 to 1.5
- gain_mlp: bfloat16 [2048], P(('fsdp', 'blk')), may hold values from 0.5 to 1.5
- stretch_order: int32 [8], replicated, may hold values from 0 to 7, each once
- cotangent: bfloat16 [4096, 2048], P(('fsdp', 'blk', 'head')), may hold values from -6 to 6
Outputs:
- layer_out: bfloat16 [4096, 2048], P(('fsdp', 'blk', 'head'))
- grad_tokens: bfloat16 [4096, 2048], P(('fsdp', 'blk', 'head'))
- grad_query: float32 [2048, 2048], P(('fsdp', 'blk'), 'head')
- grad_key: float32 [2048, 256], P(('fsdp', 'blk'))
- grad_value: float32 [2048, 256], P(('fsdp', 'blk'))
- grad_out: float32 [2048, 2048], P(('fsdp', 'blk'), 'head')
- grad_gate: float32 [2048, 5632], P(('fsdp', 'blk'), 'head')
- grad_up: float32 [2048, 5632], P(('fsdp', 'blk'), 'head')
- grad_down: float32 [2048, 5632], P(('fsdp', 'blk'), 'head')
- grad_gain_attn: float32 [2048], P(('fsdp', 'blk'))
- grad_gain_mlp: float32 [2048], P(('fsdp', 'blk'))
Inputs may be any that keep to these rules, and one draw needn't show every extreme that they name: A permutation: stored stretch c holds positions stretch_order[c] * 256 to stretch_order[c] * 256 + 255 of its sequence.
All inputs are finite; a program needn't handle non-finite values.
Results may differ from a plain program's by a relative error of at most 0.025.
Values may be sent and summed in bfloat16 or wider, within the bound.
A program may use at most 192 MiB of HBM per device.

v0:
```python
import math

import jax
import jax.numpy as jnp
from jax import lax
from jax.sharding import PartitionSpec as P

H = 32
KV = 4
HD = 64


norm_epsilon = 1e-05
rope_base = 10000.0
masked_value = -1e30


def rope_tables(positions, head_dim):
    half_dim = head_dim // 2
    frequency = rope_base ** (-(jnp.arange(half_dim, dtype=jnp.float32) * (2.0 / head_dim)))
    angles = positions.astype(jnp.float32)[:, None] * frequency[None, :]
    return (jnp.cos(angles), jnp.sin(angles))


def rotate(values, cosine, sine_table):
    half_dim = values.shape[-1] // 2
    first_half = values[..., :half_dim]
    second_half = values[..., half_dim:]
    cos_rows = cosine[:, None, :]
    sin_rows = sine_table[:, None, :]
    return jnp.concatenate(
        [
            first_half * cos_rows - second_half * sin_rows,
            second_half * cos_rows + first_half * sin_rows,
        ],
        axis=-1,
    )


def unrotate(values, cosine, sine_table):
    half_dim = values.shape[-1] // 2
    first_half = values[..., :half_dim]
    second_half = values[..., half_dim:]
    cos_rows = cosine[:, None, :]
    sin_rows = sine_table[:, None, :]
    return jnp.concatenate(
        [
            first_half * cos_rows + second_half * sin_rows,
            second_half * cos_rows - first_half * sin_rows,
        ],
        axis=-1,
    )


def stretch_positions(stretch_order, first_row, row_span, stretch_rows):
    storage = first_row + jnp.arange(row_span, dtype=jnp.int32)
    stretch_index = storage // stretch_rows
    match_table = (
        stretch_index[:, None] == jnp.arange(stretch_order.shape[0], dtype=jnp.int32)[None, :]
    )
    stretch_base = jnp.sum(jnp.where(match_table, stretch_order[None, :], 0), axis=1)
    return stretch_base * stretch_rows + storage % stretch_rows


def norm_input_grad(values, inverse, gain_vector, grad_normed):
    scaled = grad_normed * gain_vector
    inner = jnp.mean(scaled * values, axis=-1, keepdims=True)
    return inverse * scaled - values * inverse * inverse * inverse * inner


def gain_grad(values, inverse, grad_normed):
    return jnp.sum(grad_normed * values * inverse, axis=0)


def fold_block(
    state_now, keys_block, values_block, key_positions, query_heads, query_positions, score_scale
):
    running_max, running_sum, running_out = state_now
    scores = (
        jnp.einsum("qhd,kd->hqk", query_heads, keys_block, preferred_element_type=jnp.float32)
        * score_scale
    )
    allowed = (query_positions[:, None] >= key_positions[None, :])[None]
    scores = jnp.where(allowed, scores, masked_value)
    new_max = jnp.maximum(running_max, jnp.max(scores, axis=-1))
    weights = jnp.where(allowed, jnp.exp(scores - new_max[..., None]), 0.0)
    factor = jnp.exp(running_max - new_max)
    running_sum = running_sum * factor + jnp.sum(weights, axis=-1)
    running_out = running_out * factor[..., None] + jnp.einsum(
        "hqk,kd->hqd",
        weights.astype(jnp.bfloat16),
        values_block,
        preferred_element_type=jnp.float32,
    )
    return (new_max, running_sum, running_out)


def local(
    tokens,
    w_query,
    w_key,
    w_value,
    w_out,
    w_gate,
    w_up,
    w_down,
    gain_attn,
    gain_mlp,
    stretch_order,
    cotangent,
):
    row_count = tokens.shape[0]
    groups = lax.axis_size("head")
    blocks = lax.axis_size("blk")
    local_heads = H // groups
    repeats = groups // KV
    head_rows = row_count * groups
    stretch_rows = head_rows // 2
    score_scale = 1.0 / math.sqrt(HD)
    contract_last = (((1,), (1,)), ((), ()))
    contract_first = (((0,), (0,)), ((), ()))
    head_index = lax.axis_index("head")
    own_first = head_index * row_count
    block_first = lax.axis_index("blk") * head_rows
    positions = stretch_positions(stretch_order, block_first + own_first, row_count, stretch_rows)
    query_positions = stretch_positions(stretch_order, block_first, head_rows, stretch_rows)
    cos_own, sin_own = rope_tables(positions, HD)
    cos_block, sin_block = rope_tables(query_positions, HD)

    def layer_weights():
        return (
            lax.all_gather(w_query, ("fsdp", "blk"), axis=0, tiled=True),
            lax.all_gather(w_key, ("fsdp", "blk"), axis=0, tiled=True),
            lax.all_gather(w_value, ("fsdp", "blk"), axis=0, tiled=True),
            lax.all_gather(w_out, ("fsdp", "blk"), axis=0, tiled=True),
            lax.all_gather(w_gate, ("fsdp", "blk"), axis=0, tiled=True),
            lax.all_gather(w_up, ("fsdp", "blk"), axis=0, tiled=True),
            lax.all_gather(w_down, ("fsdp", "blk"), axis=0, tiled=True),
            lax.all_gather(gain_attn, ("fsdp", "blk"), axis=0, tiled=True),
            lax.all_gather(gain_mlp, ("fsdp", "blk"), axis=0, tiled=True),
        )

    def gather_query(columns):
        return lax.all_gather(columns, "head", axis=1, tiled=True)

    (
        query_cols,
        key_full,
        value_full,
        out_cols,
        gate_cols,
        up_cols,
        down_cols,
        gain_one,
        gain_two,
    ) = layer_weights()
    tokens_float = tokens.astype(jnp.float32)
    inv_attn = lax.rsqrt(
        jnp.mean(tokens_float * tokens_float, axis=-1, keepdims=True) + norm_epsilon
    )
    normed = (tokens_float * inv_attn * gain_one.astype(jnp.float32)).astype(jnp.bfloat16)
    normed_rows, cotangent_rows = (
        lax.all_gather(normed, "head", axis=0, tiled=True),
        lax.all_gather(cotangent, "head", axis=0, tiled=True),
    )
    query_all = gather_query(query_cols)
    query_lin = jnp.dot(normed, query_all, preferred_element_type=jnp.float32).reshape(
        row_count, H, HD
    )
    key_lin = jnp.dot(normed, key_full, preferred_element_type=jnp.float32).reshape(
        row_count, KV, HD
    )
    value_lin = jnp.dot(normed, value_full, preferred_element_type=jnp.float32).reshape(
        row_count, KV, HD
    )
    query_rot = rotate(query_lin, cos_own, sin_own).astype(jnp.bfloat16).reshape(row_count, H * HD)
    key_rot = rotate(key_lin, cos_own, sin_own).astype(jnp.bfloat16)
    key_slots = jnp.repeat(key_rot, repeats, axis=1).reshape(row_count, groups * HD)
    value_slots = jnp.repeat(value_lin.astype(jnp.bfloat16), repeats, axis=1).reshape(
        row_count, groups * HD
    )
    query_recv, key_own, value_own = (
        lax.all_to_all(query_rot, "head", split_axis=1, concat_axis=0, tiled=True),
        lax.all_to_all(key_slots, "head", split_axis=1, concat_axis=0, tiled=True),
        lax.all_to_all(value_slots, "head", split_axis=1, concat_axis=0, tiled=True),
    )
    query_heads = query_recv.reshape(head_rows, local_heads, HD)
    initial = (
        jnp.full((local_heads, head_rows), masked_value, jnp.float32),
        jnp.zeros((local_heads, head_rows), jnp.float32),
        jnp.zeros((local_heads, head_rows, HD), jnp.float32),
    )
    state_now = initial
    keys_piece = lax.all_gather(key_own, "blk", axis=0, tiled=True)
    values_piece = lax.all_gather(value_own, "blk", axis=0, tiled=True)
    piece_rows = keys_piece.shape[0]

    def scan_step(state_inner, step_index):
        offset = step_index * head_rows
        keys_block = lax.dynamic_slice_in_dim(keys_piece, offset, head_rows, 0)
        values_block = lax.dynamic_slice_in_dim(values_piece, offset, head_rows, 0)
        key_positions = stretch_positions(stretch_order, offset, head_rows, stretch_rows)
        return (
            fold_block(
                state_inner,
                keys_block,
                values_block,
                key_positions,
                query_heads,
                query_positions,
                score_scale,
            ),
            None,
        )

    state_now, unused = lax.scan(
        scan_step, state_now, jnp.arange(piece_rows // head_rows, dtype=jnp.int32)
    )
    running_max, running_sum, running_out = state_now
    attended_float = running_out / running_sum[..., None]
    log_sum = running_max + jnp.log(running_sum)
    attended_heads = (
        attended_float.astype(jnp.bfloat16).transpose(1, 0, 2).reshape(head_rows, local_heads * HD)
    )
    branch = lax.dot_general(
        attended_heads, out_cols, contract_last, preferred_element_type=jnp.float32
    )
    own_branch = lax.dynamic_slice_in_dim(branch, own_first, row_count, 0)
    partial_value = lax.dynamic_update_slice_in_dim(branch, own_branch + tokens_float, own_first, 0)
    hidden_rows = lax.psum(partial_value.astype(jnp.bfloat16), "head").astype(jnp.float32)
    inv_mlp = lax.rsqrt(jnp.mean(hidden_rows * hidden_rows, axis=-1, keepdims=True) + norm_epsilon)
    normed_two_rows = (hidden_rows * inv_mlp * gain_two.astype(jnp.float32)).astype(jnp.bfloat16)
    gate_proj = jnp.dot(normed_two_rows, gate_cols, preferred_element_type=jnp.float32)
    up_proj = jnp.dot(normed_two_rows, up_cols, preferred_element_type=jnp.float32)
    gate_sigmoid = jax.nn.sigmoid(gate_proj)
    gate_silu = gate_proj * gate_sigmoid
    hidden = (gate_silu * up_proj).astype(jnp.bfloat16)
    hidden_own = lax.dynamic_slice_in_dim(hidden_rows, own_first, row_count, 0)
    output_float = hidden_own + lax.psum_scatter(
        lax.dot_general(
            hidden, down_cols, contract_last, preferred_element_type=jnp.float32
        ).astype(jnp.bfloat16),
        "head",
        scatter_dimension=0,
        tiled=True,
    ).astype(jnp.float32)
    layer_low = output_float.astype(jnp.bfloat16)
    (
        query_cols,
        key_full,
        value_full,
        out_cols,
        gate_cols,
        up_cols,
        down_cols,
        gain_one,
        gain_two,
    ) = layer_weights()
    query_all = gather_query(query_cols)
    grad_hidden = jnp.dot(cotangent_rows, down_cols, preferred_element_type=jnp.float32)
    grad_gate_rows = (
        grad_hidden * up_proj * gate_sigmoid * (1.0 + gate_proj * (1.0 - gate_sigmoid))
    ).astype(jnp.bfloat16)
    grad_up_rows = (grad_hidden * gate_silu).astype(jnp.bfloat16)
    grad_w_down = lax.dot_general(
        cotangent_rows, hidden, contract_first, preferred_element_type=jnp.float32
    )
    grad_w_gate = lax.dot_general(
        normed_two_rows, grad_gate_rows, contract_first, preferred_element_type=jnp.float32
    )
    grad_w_up = lax.dot_general(
        normed_two_rows, grad_up_rows, contract_first, preferred_element_type=jnp.float32
    )
    normed_two_part = lax.dot_general(
        grad_gate_rows, gate_cols, contract_last, preferred_element_type=jnp.float32
    )
    normed_two_part = normed_two_part + lax.dot_general(
        grad_up_rows, up_cols, contract_last, preferred_element_type=jnp.float32
    )
    grad_normed_two = lax.psum(normed_two_part.astype(jnp.bfloat16), "head").astype(jnp.float32)
    gain_two_float = gain_two.astype(jnp.float32)
    grad_hidden_rows = cotangent_rows.astype(jnp.float32) + norm_input_grad(
        hidden_rows, inv_mlp, gain_two_float, grad_normed_two
    )
    own_grad_two = lax.dynamic_slice_in_dim(grad_normed_two, own_first, row_count, 0)
    own_inv_mlp = lax.dynamic_slice_in_dim(inv_mlp, own_first, row_count, 0)
    grad_gain_two = gain_grad(hidden_own, own_inv_mlp, own_grad_two)
    grad_low_rows = grad_hidden_rows.astype(jnp.bfloat16)
    grad_w_out = lax.dot_general(
        grad_low_rows, attended_heads, contract_first, preferred_element_type=jnp.float32
    )
    grad_heads = (
        jnp.dot(grad_low_rows, out_cols, preferred_element_type=jnp.float32)
        .astype(jnp.bfloat16)
        .reshape(head_rows, local_heads, HD)
    )
    keys_all, values_all = (
        lax.all_gather(key_own, "blk", axis=0, tiled=True),
        lax.all_gather(value_own, "blk", axis=0, tiled=True),
    )
    row_delta = jnp.sum(grad_heads.astype(jnp.float32).transpose(1, 0, 2) * attended_float, axis=-1)

    def back_block(grad_query_acc, block_index):
        offset = block_index * head_rows
        keys_block = lax.dynamic_slice_in_dim(keys_all, offset, head_rows, 0)
        values_block = lax.dynamic_slice_in_dim(values_all, offset, head_rows, 0)
        key_positions = stretch_positions(stretch_order, offset, head_rows, stretch_rows)
        scores = (
            jnp.einsum("qhd,kd->hqk", query_heads, keys_block, preferred_element_type=jnp.float32)
            * score_scale
        )
        allowed = (query_positions[:, None] >= key_positions[None, :])[None]
        probs_block = jnp.where(allowed, jnp.exp(scores - log_sum[..., None]), 0.0)
        grad_probs = jnp.einsum(
            "qhd,kd->hqk", grad_heads, values_block, preferred_element_type=jnp.float32
        )
        grad_scores = (probs_block * (grad_probs - row_delta[..., None])).astype(jnp.bfloat16)
        grad_query_acc = grad_query_acc + jnp.einsum(
            "hqk,kd->qhd", grad_scores, keys_block, preferred_element_type=jnp.float32
        )
        grad_key_part = (
            jnp.einsum("hqk,qhd->kd", grad_scores, query_heads, preferred_element_type=jnp.float32)
            * score_scale
        )
        grad_value_part = jnp.einsum(
            "hqk,qhd->kd",
            probs_block.astype(jnp.bfloat16),
            grad_heads,
            preferred_element_type=jnp.float32,
        )
        return (grad_query_acc, (grad_key_part, grad_value_part))

    grad_query_acc, (key_terms, value_terms) = lax.scan(
        back_block,
        jnp.zeros((head_rows, local_heads, HD), jnp.float32),
        jnp.arange(blocks, dtype=jnp.int32),
    )
    grad_key_sum, grad_value_sum = (
        lax.psum_scatter(
            key_terms.reshape(blocks * head_rows, HD).astype(jnp.bfloat16),
            "blk",
            scatter_dimension=0,
            tiled=True,
        ).astype(jnp.float32),
        lax.psum_scatter(
            value_terms.reshape(blocks * head_rows, HD).astype(jnp.bfloat16),
            "blk",
            scatter_dimension=0,
            tiled=True,
        ).astype(jnp.float32),
    )
    grad_query_rot = (grad_query_acc * score_scale).astype(jnp.bfloat16)
    grad_query_lin_heads = (
        unrotate(grad_query_rot.astype(jnp.float32), cos_block, sin_block)
        .astype(jnp.bfloat16)
        .reshape(head_rows, local_heads * HD)
    )
    key_slot_grad = grad_key_sum.astype(jnp.bfloat16)
    value_slot_grad = grad_value_sum.astype(jnp.bfloat16)
    grad_w_query = lax.dot_general(
        normed_rows, grad_query_lin_heads, contract_first, preferred_element_type=jnp.float32
    )
    query_back, key_back, value_back = (
        lax.all_to_all(grad_query_lin_heads, "head", split_axis=0, concat_axis=1, tiled=True),
        lax.all_to_all(key_slot_grad, "head", split_axis=0, concat_axis=1, tiled=True),
        lax.all_to_all(value_slot_grad, "head", split_axis=0, concat_axis=1, tiled=True),
    )
    key_slot_lin = (
        unrotate(key_back.astype(jnp.float32).reshape(row_count, groups, HD), cos_own, sin_own)
        .astype(jnp.bfloat16)
        .reshape(row_count, KV, repeats, HD)
    )
    value_slot_lin = value_back.reshape(row_count, KV, repeats, HD)
    grad_w_key = jnp.einsum(
        "td,tjrc->djc", normed, key_slot_lin, preferred_element_type=jnp.float32
    ).reshape(-1, KV * HD)
    grad_w_value = jnp.einsum(
        "td,tjrc->djc", normed, value_slot_lin, preferred_element_type=jnp.float32
    ).reshape(-1, KV * HD)
    grad_normed = lax.dot_general(
        query_back, query_all, contract_last, preferred_element_type=jnp.float32
    )
    grad_normed = grad_normed + jnp.einsum(
        "tjrc,djc->td",
        key_slot_lin,
        key_full.reshape(-1, KV, HD),
        preferred_element_type=jnp.float32,
    )
    grad_normed = grad_normed + jnp.einsum(
        "tjrc,djc->td",
        value_slot_lin,
        value_full.reshape(-1, KV, HD),
        preferred_element_type=jnp.float32,
    )
    gain_one_float = gain_one.astype(jnp.float32)
    grad_input_norm = norm_input_grad(tokens_float, inv_attn, gain_one_float, grad_normed)
    grad_gain_one = gain_grad(tokens_float, inv_attn, grad_normed)
    grad_hidden_own = lax.dynamic_slice_in_dim(grad_hidden_rows, own_first, row_count, 0)
    grad_tokens = (grad_hidden_own + grad_input_norm).astype(jnp.bfloat16)
    head_sums = (
        lax.psum(grad_w_key.astype(jnp.bfloat16), "head").astype(jnp.float32),
        lax.psum(grad_w_value.astype(jnp.bfloat16), "head").astype(jnp.float32),
        lax.psum(grad_gain_one.astype(jnp.bfloat16), "head").astype(jnp.float32),
        lax.psum(grad_gain_two.astype(jnp.bfloat16), "head").astype(jnp.float32),
    )
    reduced = (
        lax.psum_scatter(
            grad_w_query.astype(jnp.bfloat16), ("fsdp", "blk"), scatter_dimension=0, tiled=True
        ).astype(jnp.float32),
        lax.psum_scatter(
            head_sums[0].astype(jnp.bfloat16), ("fsdp", "blk"), scatter_dimension=0, tiled=True
        ).astype(jnp.float32),
        lax.psum_scatter(
            head_sums[1].astype(jnp.bfloat16), ("fsdp", "blk"), scatter_dimension=0, tiled=True
        ).astype(jnp.float32),
        lax.psum_scatter(
            grad_w_out.astype(jnp.bfloat16), ("fsdp", "blk"), scatter_dimension=0, tiled=True
        ).astype(jnp.float32),
        lax.psum_scatter(
            grad_w_gate.astype(jnp.bfloat16), ("fsdp", "blk"), scatter_dimension=0, tiled=True
        ).astype(jnp.float32),
        lax.psum_scatter(
            grad_w_up.astype(jnp.bfloat16), ("fsdp", "blk"), scatter_dimension=0, tiled=True
        ).astype(jnp.float32),
        lax.psum_scatter(
            grad_w_down.astype(jnp.bfloat16), ("fsdp", "blk"), scatter_dimension=0, tiled=True
        ).astype(jnp.float32),
        lax.psum_scatter(
            head_sums[2].astype(jnp.bfloat16), ("fsdp", "blk"), scatter_dimension=0, tiled=True
        ).astype(jnp.float32),
        lax.psum_scatter(
            head_sums[3].astype(jnp.bfloat16), ("fsdp", "blk"), scatter_dimension=0, tiled=True
        ).astype(jnp.float32),
    )
    return (
        layer_low,
        grad_tokens,
        reduced[0],
        reduced[1],
        reduced[2],
        reduced[3],
        reduced[4],
        reduced[5],
        reduced[6],
        reduced[7],
        reduced[8],
    )


def solution(mesh):
    return jax.shard_map(
        local,
        mesh=mesh,
        in_specs=(
            P(("fsdp", "blk", "head"), None),
            P(("fsdp", "blk"), "head"),
            P(("fsdp", "blk"), None),
            P(("fsdp", "blk"), None),
            P(("fsdp", "blk"), "head"),
            P(("fsdp", "blk"), "head"),
            P(("fsdp", "blk"), "head"),
            P(("fsdp", "blk"), "head"),
            P(("fsdp", "blk")),
            P(("fsdp", "blk")),
            P(),
            P(("fsdp", "blk", "head"), None),
        ),
        out_specs=(
            P(("fsdp", "blk", "head"), None),
            P(("fsdp", "blk", "head"), None),
            P(("fsdp", "blk"), "head"),
            P(("fsdp", "blk"), None),
            P(("fsdp", "blk"), None),
            P(("fsdp", "blk"), "head"),
            P(("fsdp", "blk"), "head"),
            P(("fsdp", "blk"), "head"),
            P(("fsdp", "blk"), "head"),
            P(("fsdp", "blk")),
            P(("fsdp", "blk")),
        ),
        check_vma=False,
    )
```

profile of v0, /device:TPU:0, one launch (start us, length us, event | category | flops | bytes accessed | tf_op | source)
XLA Modules:
  0.0 1346.1 jit_solution(8188463659455719253)
XLA Ops:
  9.4 31.0 %all-gather.15.cloned.1.call-done = bf16[2048,512]{1,0:T(8,128)(2,1)} async-done(((bf16[256,512]{1,0:T(8,128)(2,1)}), bf16[2048,512]{1,0:T(8,128)(2,1)}) %all-gather.15.cloned.1.call-update) | async-done | bytes 2097168 | tf_op jit(solution)/shard_map/all_gather | solution.py:132
  41.8 8.9 all-gather
  54.8 10.9 all-gather.13.cloned.1.call-done
  68.1 4.6 all-to-all-start
  72.7 18.3 %all-gather.19.cloned.1.call-done = bf16[2048,256]{1,0:T(8,128)(2,1)} async-done(((bf16[256,256]{1,0:T(8,128)(2,1)}), bf16[2048,256]{1,0:T(8,128)(2,1)}) %all-gather.19.cloned.1.call-update) | async-done | bytes 1048592 | tf_op jit(solution)/shard_map/all_gather | solution.py:134
  93.3 148.8 %all-gather.17.cloned.1.call-done = bf16[2048,2048]{1,0:T(8,128)(2,1)} async-done(((bf16[2048,512]{1,0:T(8,128)(2,1)}), bf16[2048,2048]{1,0:T(8,128)(2,1)}) %all-gather.17.cloned.1.call-update) | async-done | bytes 8388624 | tf_op jit(solution)/shard_map/all_gather | solution.py:144
  242.1 6.8 fusion.92
  253.3 4.8 all-to-all-done.2
  262.3 7.7 all_gather.56
  270.0 6.1 all_gather.60
  276.7 58.5 %while.34 = (s32[]{:T(128)}, f32[8,512]{1,0:T(8,128)S(1)}, f32[8,512]{1,0:T(8,128)S(1)}, f32[8,512,64]{1,2,0:T(8,128)S(1)}, s32[512]{0:T(512)S(1)}, /*index=5*/s...) while((s32[]{:T(128)}, f32[8,512]{1,0:T(8,128)S(1)}, ...), condition=%wide.region_7.8_spmd.clone, body=%wide.region_3.7_spmd.clone.sunk | while | flops 565230080 | bytes 62798108 | solution.py:216
  278.3 4.7 fusion.171
  283.0 4.6 fusion.172
  292.9 4.7 fusion.171
  297.6 4.6 fusion.172
  307.5 4.7 fusion.171
  312.2 4.6 fusion.172
  322.2 4.7 fusion.171
  326.9 4.6 fusion.172
  343.4 9.3 all-gather.1
  352.7 74.6 %all-reduce.9.cloned.1.call-done = bf16[512,2048]{1,0:T(8,128)(2,1)} async-done(((bf16[512,2048]{1,0:T(8,128)(2,1)}), bf16[512,2048]{1,0:T(8,128)(2,1)}) %all-reduce.9.cloned.1.call-update) | async-done | bytes 2097168 | tf_op jit(solution)/shard_map/psum | solution.py:230
  429.4 42.1 %all-gather.23.cloned.1.call-done = bf16[2048,1408]{1,0:T(8,128)(2,1)} async-done(((bf16[256,1408]{1,0:T(8,128)(2,1)}), bf16[2048,1408]{1,0:T(8,128)(2,1)}) %all-gather.23.cloned.1.call-update) | async-done | bytes 5767184 | tf_op jit(solution)/shard_map/all_gather | solution.py:136
  471.4 8.5 fusion.88
  479.9 36.6 %all-gather.25.cloned.1.call-done = bf16[2048,1408]{1,0:T(8,128)(2,1)} async-done(((bf16[256,1408]{1,0:T(8,128)(2,1)}), bf16[2048,1408]{1,0:T(8,128)(2,1)}) %all-gather.25.cloned.1.call-update) | async-done | bytes 5767184 | tf_op jit(solution)/shard_map/all_gather | solution.py:137
  516.5 7.6 fusion.87
  524.2 39.6 %all-gather.29.cloned.1.call-done = bf16[512,2048]{1,0:T(8,128)(2,1)} async-done(((bf16[128,2048]{1,0:T(8,128)(2,1)}), bf16[512,2048]{1,0:T(8,128)(2,1)}) %all-gather.29.cloned.1.call-update) | async-done | bytes 2097168 | tf_op jit(solution)/shard_map/all_gather | solution.py:164
  563.8 43.8 %all-gather.27.cloned.1.call-done = bf16[2048,1408]{1,0:T(8,128)(2,1)} async-done(((bf16[256,1408]{1,0:T(8,128)(2,1)}), bf16[2048,1408]{1,0:T(8,128)(2,1)}) %all-gather.27.cloned.1.call-update) | async-done | bytes 5767184 | tf_op jit(solution)/shard_map/all_gather | solution.py:138
  607.6 10.3 multiply_convert_fusion.1
  617.9 6.6 fusion.94
  624.5 4.7 add_convert_fusion
  629.5 86.0 %all-reduce.11.cloned.1.call-done = bf16[512,2048]{1,0:T(8,128)(2,1)} async-done(((bf16[512,2048]{1,0:T(8,128)(2,1)}), bf16[512,2048]{1,0:T(8,128)(2,1)}) %all-reduce.11.cloned.1.call-update) | async-done | bytes 2097168 | tf_op jit(solution)/shard_map/psum | solution.py:280
  724.9 76.3 %while.35 = (s32[]{:T(128)}, f32[512,8,64]{0,2,1:T(8,128)S(1)}, bf16[4,512,64]{1,2,0:T(8,128)(2,1)}, bf16[4,512,64]{1,2,0:T(8,128)(2,1)}, s32[4]{0:T(128)S(1)}, ...) while((s32[]{:T(128)}, f32[512,8,64]{0,2,1:T(8,128)S(1)}, ...), condition=%wide.region_16.17_spmd.clone, body=%wide.region_14.16_spmd.clone.sunk | while | flops 1363995136 | bytes 99875272 | solution.py:333
  727.7 5.0 fusion.187
  738.1 5.1 fusion.190
  746.8 4.9 fusion.187
  757.2 5.1 fusion.190
  765.8 4.9 fusion.187
  776.3 5.1 fusion.190
  784.9 4.9 fusion.187
  795.3 5.1 fusion.190
  802.9 19.2 %reduce-scatter.13.cloned.1.call-done = bf16[512,64]{0,1:T(8,128)(2,1)} async-done(((bf16[2048,64]{0,1:T(8,128)(2,1)}), bf16[512,64]{0,1:T(8,128)(2,1)}) %reduce-scatter.13.cloned.1.call-update) | async-done | bytes 65552 | tf_op jit(solution)/shard_map/reduce_scatter | solution.py:339
  823.6 4.6 all-to-all-start.4
  829.9 4.0 all-to-all-done.4
  837.9 14.6 %reduce-scatter.15.cloned.1.call-done = bf16[512,64]{0,1:T(8,128)(2,1)} async-done(((bf16[2048,64]{0,1:T(8,128)(2,1)}), bf16[512,64]{0,1:T(8,128)(2,1)}) %reduce-scatter.15.cloned.1.call-update) | async-done | bytes 65552 | tf_op jit(solution)/shard_map/reduce_scatter | solution.py:345
  853.4 10.2 all_to_all.93
  866.4 7.9 convolution_convert_fusion.5
  875.0 16.5 %reduce-scatter.27.cloned.1.call-done = bf16[256,256]{1,0:T(8,128)(2,1)} async-done(((bf16[2048,256]{1,0:T(8,128)(2,1)}), bf16[256,256]{1,0:T(8,128)(2,1)}) %reduce-scatter.27.cloned.1.call-update) | async-done | bytes 131088 | tf_op jit(solution)/shard_map/reduce_scatter | solution.py:410
  891.6 39.0 %reduce-scatter.29.cloned.1.call-done = bf16[256,256]{1,0:T(8,128)(2,1)} async-done(((bf16[2048,256]{1,0:T(8,128)(2,1)}), bf16[256,256]{1,0:T(8,128)(2,1)}) %reduce-scatter.29.cloned.1.call-update) | async-done | bytes 131088 | tf_op jit(solution)/shard_map/reduce_scatter | solution.py:413
  930.7 47.6 %all-gather.31.cloned.1.call-done = bf16[512,2048]{1,0:T(8,128)(2,1)} async-done(((bf16[128,2048]{1,0:T(8,128)(2,1)}), bf16[512,2048]{1,0:T(8,128)(2,1)}) %all-gather.31.cloned.1.call-update) | async-done | bytes 2097168 | tf_op jit(solution)/shard_map/all_gather | solution.py:163
  978.3 4.2 convolution_convert_fusion.4
  982.6 5.0 convolution_convert_fusion.3
  987.7 6.9 convolution_convert_fusion.2
  994.7 6.8 convolution_convert_fusion.1
  1001.8 7.7 fusion.58
  1013.5 4.1 all-to-all-start.3
  1027.3 5.9 all-to-all-done.3
  1033.3 6.6 fusion.95
  1045.6 13.8 %all-reduce.2 = (bf16[2048]{0:T(1024)(128)(2,1)S(1)}, bf16[2048]{0:T(1024)(128)(2,1)S(1)}) all-reduce(bf16[2048]{0:T(1024)(128)(2,1)S(1)} %get-tuple-element.443, bf16[2048]{0:T(1024)(128)(2,1)S(1)} %get-tuple-element.506), channel_id=12, replica_groups=mesh['fsdp'=2,'blk'=4,'head'=4] {'fsdp','blk'}, use_global_device_ids=true, to_apply=%region_31.32.clone | all-reduce | flops 4096 | bytes 16384
  1059.6 9.5 all-reduce.3
  1073.5 31.5 %reduce-scatter.17.cloned.1.call-done = bf16[256,512]{1,0:T(8,128)(2,1)} async-done(((bf16[2048,512]{1,0:T(8,128)(2,1)}), bf16[256,512]{1,0:T(8,128)(2,1)}) %reduce-scatter.17.cloned.1.call-update) | async-done | bytes 262160 | tf_op jit(solution)/shard_map/reduce_scatter | solution.py:407
  1106.9 42.5 %reduce-scatter.19.cloned.1.call-done = bf16[256,512]{1,0:T(8,128)(2,1)} async-done(((bf16[2048,512]{1,0:T(8,128)(2,1)}), bf16[256,512]{1,0:T(8,128)(2,1)}) %reduce-scatter.19.cloned.1.call-update) | async-done | bytes 262160 | tf_op jit(solution)/shard_map/reduce_scatter | solution.py:416
  1151.1 60.7 %reduce-scatter.21.cloned.1.call-done = bf16[256,1408]{1,0:T(8,128)(2,1)} async-done(((bf16[2048,1408]{1,0:T(8,128)(2,1)}), bf16[256,1408]{1,0:T(8,128)(2,1)}) %reduce-scatter.21.cloned.1.call-update) | async-done | bytes 720912 | tf_op jit(solution)/shard_map/reduce_scatter | solution.py:419
  1214.1 60.2 %reduce-scatter.23.cloned.1.call-done = bf16[256,1408]{1,0:T(8,128)(2,1)} async-done(((bf16[2048,1408]{1,0:T(8,128)(2,1)}), bf16[256,1408]{1,0:T(8,128)(2,1)}) %reduce-scatter.23.cloned.1.call-update) | async-done | bytes 720912 | tf_op jit(solution)/shard_map/reduce_scatter | solution.py:422
  1276.6 60.0 %reduce-scatter.25.cloned.1.call-done = bf16[256,1408]{0,1:T(8,128)(2,1)} async-done(((bf16[2048,1408]{0,1:T(8,128)(2,1)}), bf16[256,1408]{0,1:T(8,128)(2,1)}) %reduce-scatter.25.cloned.1.call-update) | async-done | bytes 720912 | tf_op jit(solution)/shard_map/reduce_scatter | solution.py:425
  (334 shorter events, 140.4 us)
Async XLA Ops:
  7.2 33.2 %all-gather.15.cloned.1.call-start = ((), (), s32[]{:S(2)}) async-start(), calls=%async_computation.17 | async-start | bytes 2359296 | tf_op jit(solution)/shard_map/all_gather | solution.py:132
  7.9 57.8 %all-gather.13.cloned.1.call-start = ((), (), s32[]{:S(2)}) async-start(), calls=%async_computation.16 | async-start | bytes 1179648 | tf_op jit(solution)/shard_map/all_gather | solution.py:133
  8.7 82.3 %all-gather.19.cloned.1.call-start = ((), (), s32[]{:S(2)}) async-start(), calls=%async_computation.19 | async-start | bytes 1179648 | tf_op jit(solution)/shard_map/all_gather | solution.py:134
  9.4 232.7 %all-gather.17.cloned.1.call-start = ((), (), s32[]{:S(2)}) async-start(), calls=%async_computation.18 | async-start | bytes 10485760 | tf_op jit(solution)/shard_map/all_gather | solution.py:144
  40.4 295.0 %all-gather.21.cloned.1.call-start = ((), (), s32[]{:S(2)}) async-start(), calls=%async_computation.20 | async-start | bytes 2359296 | tf_op jit(solution)/shard_map/all_gather | solution.py:135
  41.1 26.4 %copy-start.35 = (f32[32]{0:T(128)}, f32[32]{0:T(128)S(1)}, u32[]{:S(2)}) copy-start(f32[32]{0:T(128)S(1)} %negate_power_fusion) | copy-start | bytes 388
  51.9 197.0 %copy-start.33 = (f32[128]{0:T(128)}, f32[128]{0:T(128)S(1)}, u32[]{:S(2)}) copy-start(f32[128]{0:T(128)S(1)} %add_rsqrt_fusion.1) | copy-start | bytes 1540
  54.6 194.2 %copy-start.7 = (bf16[128,2048]{1,0:T(8,128)(2,1)}, bf16[128,2048]{1,0:T(8,128)(2,1)S(1)}, u32[]{:S(2)}) copy-start(bf16[128,2048]{1,0:T(8,128)(2,1)S(1)} %fusion.64) | copy-start | bytes 1572868
  54.8 194.1 %copy-start.22 = (f32[128,32]{0,1:T(8,128)}, f32[128,32]{0,1:T(8,128)S(1)}, u32[]{:S(2)}) copy-start(f32[128,32]{0,1:T(8,128)S(1)} %get-tuple-element.518) | copy-start | bytes 49156
  54.8 194.1 %copy-start.24 = (f32[128,32]{0,1:T(8,128)}, f32[128,32]{0,1:T(8,128)S(1)}, u32[]{:S(2)}) copy-start(f32[128,32]{0,1:T(8,128)S(1)} %get-tuple-element.519) | copy-start | bytes 49156
  68.1 180.9 %all-to-all-start = ((bf16[128,4,64]{0,2,1:T(8,128)(2,1)}), bf16[128,4,64]{0,2,1:T(8,128)(2,1)S(1)}, u32[]{:S(2)}, u32[]{:S(2)}) async-start(bf16[128,4,64]{0,2,1:T(8,128)(2,1)} %pad_maximum_fusion.1), calls=%async_computation | async-start | bytes 131072 | tf_op jit(solution)/shard_map/all_to_all | solution.py:184
  248.9 27.8 %copy-start.31 = (s32[8]{0:T(128)S(1)}, s32[8]{0:T(128)}, u32[]{:S(2)}) copy-start(s32[8]{0:T(128)} %param.26) | copy-start | bytes 100
  249.1 9.0 all-to-all-start.2
  258.1 17.9 %all-to-all-start.1 = ((bf16[128,4,512]{0,2,1:T(8,128)(2,1)}), bf16[128,4,512]{0,2,1:T(8,128)(2,1)S(1)}, u32[]{:S(2)}, u32[]{:S(2)}) async-start(bf16[128,4,512]{0,2,1:T(8,128)(2,1)} %bitcast.4), calls=%async_computation.1 | async-start | bytes 1048576 | tf_op jit(solution)/shard_map/all_to_all | solution.py:183
  261.6 165.7 %all-reduce.9.cloned.1.call-start = ((), (), s32[]{:S(2)}) async-start(), calls=%async_computation.21 | async-start | bytes 4194304 | tf_op jit(solution)/shard_map/psum | solution.py:230
  283.0 5.8 copy-start
  297.6 5.8 copy-start
  312.2 5.8 copy-start
  326.9 5.8 copy-start
  340.5 130.9 %all-gather.23.cloned.1.call-start = ((), (), s32[]{:S(2)}) async-start(), calls=%async_computation.22 | async-start | bytes 6488064 | tf_op jit(solution)/shard_map/all_gather | solution.py:136
  341.2 175.3 %all-gather.25.cloned.1.call-start = ((), (), s32[]{:S(2)}) async-start(), calls=%async_computation.23 | async-start | bytes 6488064 | tf_op jit(solution)/shard_map/all_gather | solution.py:137
  342.0 221.8 %all-gather.29.cloned.1.call-start = ((), (), s32[]{:S(2)}) async-start(), calls=%async_computation.26 | async-start | bytes 2621440 | tf_op jit(solution)/shard_map/all_gather | solution.py:164
  342.7 264.8 %all-gather.27.cloned.1.call-start = ((), (), s32[]{:S(2)}) async-start(), calls=%async_computation.24 | async-start | bytes 6488064 | tf_op jit(solution)/shard_map/all_gather | solution.py:138
  343.3 372.2 %all-reduce.11.cloned.1.call-start = ((), (), s32[]{:S(2)}) async-start(), calls=%async_computation.27 | async-start | bytes 4194304 | tf_op jit(solution)/shard_map/psum | solution.py:280
  471.4 45.1 %copy-start.4 = (bf16[512,2048]{1,0:T(8,128)(2,1)S(1)}, bf16[512,2048]{1,0:T(8,128)(2,1)}, u32[]{:S(2)}) copy-start(bf16[512,2048]{1,0:T(8,128)(2,1)} %all-reduce.9.cloned.1.call-done) | copy-start | bytes 6291460
  617.9 6.6 copy-start.41
  617.9 6.6 copy-start.40
  617.9 6.6 copy-start.37
  629.2 192.9 %reduce-scatter.13.cloned.1.call-start = ((), (), s32[]{:S(2)}) async-start(), calls=%async_computation.28 | async-start | bytes 327680 | tf_op jit(solution)/shard_map/reduce_scatter | solution.py:339
  724.9 109.1 %copy-start.23 = (f32[128,32]{0,1:T(8,128)S(1)}, f32[128,32]{0,1:T(8,128)}, u32[]{:S(2)}) copy-start(f32[128,32]{0,1:T(8,128)} %copy-done.22) | copy-start | bytes 49156
  724.9 109.1 %copy-start.25 = (f32[128,32]{0,1:T(8,128)S(1)}, f32[128,32]{0,1:T(8,128)}, u32[]{:S(2)}) copy-start(f32[128,32]{0,1:T(8,128)} %copy-done.24) | copy-start | bytes 49156
  724.9 109.1 %copy-start.8 = (bf16[128,2048]{1,0:T(8,128)(2,1)S(1)}, bf16[128,2048]{1,0:T(8,128)(2,1)}, u32[]{:S(2)}) copy-start(bf16[128,2048]{1,0:T(8,128)(2,1)} %copy-done.7) | copy-start | bytes 1572868
  727.3 5.3 copy-start.2
  732.7 5.5 copy-start.21
  732.7 5.5 copy-start.27
  746.4 5.3 copy-start.2
  751.7 5.5 copy-start.21
  751.7 5.5 copy-start.27
  765.5 5.3 copy-start.2
  770.8 5.5 copy-start.21
  770.8 5.5 copy-start.27
  789.9 5.5 copy-start.21
  789.9 5.5 copy-start.27
  823.6 10.4 all-to-all-start.4
  828.2 24.4 %reduce-scatter.15.cloned.1.call-start = ((), (), s32[]{:S(2)}) async-start(), calls=%async_computation.29 | async-start | bytes 327680 | tf_op jit(solution)/shard_map/reduce_scatter | solution.py:345
  829.9 61.7 %reduce-scatter.27.cloned.1.call-start = ((), (), s32[]{:S(2)}) async-start(), calls=%async_computation.36 | async-start | bytes 1179648 | tf_op jit(solution)/shard_map/reduce_scatter | solution.py:410
  837.9 92.7 %reduce-scatter.29.cloned.1.call-start = ((), (), s32[]{:S(2)}) async-start(), calls=%async_computation.37 | async-start | bytes 1179648 | tf_op jit(solution)/shard_map/reduce_scatter | solution.py:413
  865.5 112.8 %all-gather.31.cloned.1.call-start = ((), (), s32[]{:S(2)}) async-start(), calls=%async_computation.30 | async-start | bytes 2621440 | tf_op jit(solution)/shard_map/all_gather | solution.py:163
  866.1 176.9 %reduce-scatter.11.cloned.1.call-start = ((), (), s32[]{:S(2)}) async-start(), calls=%async_computation.25 | async-start | bytes 2621440 | tf_op jit(solution)/shard_map/reduce_scatter | solution.py:239
  866.3 8.0 copy-start.32
  866.3 8.0 copy-start.36
  874.3 195.9 %all-reduce.13.cloned.1.call-start = ((), (), s32[]{:S(2)}) async-start(), calls=%async_computation.38 | async-start | bytes 524288 | tf_op jit(solution)/shard_map/psum | solution.py:401
  875.0 107.5 %copy-start.17 = (bf16[512,8,64]{0,2,1:T(8,128)(2,1)}, bf16[512,8,64]{0,2,1:T(8,128)(2,1)S(1)}, u32[]{:S(2)}) copy-start(bf16[512,8,64]{0,2,1:T(8,128)(2,1)S(1)} %maximum_convert_fusion) | copy-start | bytes 1572868
  930.6 174.4 %reduce-scatter.17.cloned.1.call-start = ((), (), s32[]{:S(2)}) async-start(), calls=%async_computation.31 | async-start | bytes 2359296 | tf_op jit(solution)/shard_map/reduce_scatter | solution.py:407
  982.6 166.8 %reduce-scatter.19.cloned.1.call-start = ((), (), s32[]{:S(2)}) async-start(), calls=%async_computation.32 | async-start | bytes 2359296 | tf_op jit(solution)/shard_map/reduce_scatter | solution.py:416
  987.6 224.2 %reduce-scatter.21.cloned.1.call-start = ((), (), s32[]{:S(2)}) async-start(), calls=%async_computation.33 | async-start | bytes 6488064 | tf_op jit(solution)/shard_map/reduce_scatter | solution.py:419
  994.6 279.7 %reduce-scatter.23.cloned.1.call-start = ((), (), s32[]{:S(2)}) async-start(), calls=%async_computation.34 | async-start | bytes 6488064 | tf_op jit(solution)/shard_map/reduce_scatter | solution.py:422
  1001.5 335.1 %reduce-scatter.25.cloned.1.call-start = ((), (), s32[]{:S(2)}) async-start(), calls=%async_computation.35 | async-start | bytes 6488064 | tf_op jit(solution)/shard_map/reduce_scatter | solution.py:425
  1009.6 8.1 copy-start.39
  1009.6 9.4 copy-start.13
  1013.5 19.7 %all-to-all-start.3 = ((bf16[4,128,512]{1,2,0:T(8,128)(2,1)}), bf16[4,128,512]{1,2,0:T(8,128)(2,1)}, u32[]{:S(2)}, u32[]{:S(2)}) async-start(bf16[4,128,512]{1,2,0:T(8,128)(2,1)} %copy.105), calls=%async_computation.4 | async-start | bytes 1048576 | tf_op jit(solution)/shard_map/all_to_all | solution.py:364
  1033.3 6.6 copy-start.12
  1033.3 6.6 copy-start.30
  1033.3 6.6 copy-start.34
  (27 other events, 72.9 us)
Sparse Core Ops, SparseCore 0:
  9.9 30.4 all-gather.14
  42.3 23.3 all-gather.12
  67.6 23.3 all-gather.18
  92.4 149.5 all-gather.16
  243.8 27.2 all-gather.20
  340.6 86.6 all-reduce.8
  429.2 42.2 all-gather.22
  473.3 43.1 all-gather.24
  518.1 45.6 all-gather.28
  565.5 41.9 all-gather.26
  629.3 86.1 all-reduce.10
  803.0 19.0 reduce-scatter.12
  832.0 20.5 reduce-scatter.14
  855.6 35.9 reduce-scatter.26
  894.6 35.9 reduce-scatter.28
  932.6 45.6 all-gather.30
  980.5 42.4 reduce-scatter.10
  1025.1 35.7 all-reduce.12
  1064.2 40.8 reduce-scatter.16
  1108.2 41.0 reduce-scatter.18
  1152.8 59.0 reduce-scatter.20
  1215.3 58.9 reduce-scatter.22
  1277.7 58.8 reduce-scatter.24
where the time goes:
time: 1350 us
  waiting for transfers between devices  944 us (70%)
  matrix products  194 us (14%)
  blocking collectives  65.3 us (5%)
  other arithmetic  63.2 us (5%)
  local copies, waits for them, and re-layouts  35.6 us (3%)
  starting transfers between devices  21.7 us (2%)
  between operations  16 us (1%)
    all_gather x1, waiting for transfers between devices, gather_query(): return lax.all_gather(columns, 'head', axis=1, tiled=True)  149 us
    psum x1, waiting for transfers between devices, local(): lax.psum(normed_two_part.astype(jnp.bfloat16), 'head').astype(jnp.float32)  86 us
    psum x1, waiting for transfers between devices, local(): lax.psum(partial_value.astype(jnp.bfloat16), 'head').astype(jnp.float32)  74.6 us
    reduce_scatter x1, waiting for transfers between devices, local(): lax.psum_scatter(grad_w_gate.astype(jnp.bfloat16), ('fsdp', 'blk'), scatt...  60.7 us
    reduce_scatter x1, waiting for transfers between devices, local(): lax.psum_scatter(grad_w_up.astype(jnp.bfloat16), ('fsdp', 'blk'), scatter...  60.2 us
    reduce_scatter x1, waiting for transfers between devices, local(): lax.psum_scatter(grad_w_down.astype(jnp.bfloat16), ('fsdp', 'blk'), scatt...  60 us
    all_gather x1, waiting for transfers between devices, local(): lax.all_gather(normed, 'head', axis=0, tiled=True)  47.6 us
    all_gather x1, waiting for transfers between devices, layer_weights(): lax.all_gather(w_down, ('fsdp', 'blk'), axis=0, tiled=True)  43.8 us
  transfers between devices with their start and end apart: 28, of which 23 were waited for; matrix products, arithmetic and copies ran while one was open for 13% of the time, Pallas kernels for 0%

commit v1 on v0

--- a/solution.py
+++ b/solution.py
@@ -3,6 +3,8 @@
 import jax
 import jax.numpy as jnp
 from jax import lax
+from jax.experimental import pallas as pl
+from jax.experimental.pallas import tpu as pltpu
 from jax.sharding import PartitionSpec as P
 
 H = 32
@@ -447,9 +449,961 @@
     )
 
 
+MESH = pl.DeviceIdType.MESH
+f32, bf16 = jnp.float32, jnp.bfloat16
+VM = pl.BlockSpec(memory_space=pltpu.VMEM)
+HB = pl.BlockSpec(memory_space=pl.ANY)
+
+
+def dma_sems(n):
+    return [pltpu.SemaphoreType.DMA((n,)), pltpu.SemaphoreType.DMA((n,))]
+
+
+class Here:
+    def __init__(self, send_sem, recv_sem):
+        self.y = lax.axis_index("fsdp")
+        blk = lax.axis_index("blk")
+        self.x, self.c = blk // 2, blk % 2
+        self.z = lax.axis_index("head")
+        self.send_sem, self.recv_sem, self.used = send_sem, recv_sem, 0
+
+    def plane(self, i):
+        y = 1 - self.y if i & 4 else self.y
+        x = 1 - self.x if i & 2 else self.x
+        c = 1 - self.c if i & 1 else self.c
+        return {"fsdp": y, "blk": x * 2 + c}
+
+    def up(self):
+        return {"head": self.z + 1}
+
+    def down(self):
+        return {"head": self.z - 1}
+
+    def copy(self, src, dst, device):
+        k = self.used
+        self.used += 1
+        return self.again(k, src, dst, device)
+
+    def slot(self):
+        self.used += 1
+        return self.used - 1
+
+    def again(self, k, src, dst, device):
+        return pltpu.make_async_remote_copy(
+            src_ref=src,
+            dst_ref=dst,
+            send_sem=self.send_sem.at[k],
+            recv_sem=self.recv_sem.at[k],
+            device_id=device,
+            device_id_type=MESH,
+        )
+
+    def local(self, src, dst):
+        k = self.used
+        self.used += 1
+        return pltpu.make_async_copy(src, dst, self.send_sem.at[k])
+
+    def enter(self, offsets, along_z=True, all_z=False):
+        bar = pltpu.get_barrier_semaphore()
+        for i in offsets:
+            pl.semaphore_signal(bar, inc=1, device_id=self.plane(i), device_id_type=MESH)
+        if all_z:
+            for d in (1, 2, 3):
+                pl.semaphore_signal(
+                    bar, inc=1, device_id={"head": (self.z + d) % 4}, device_id_type=MESH
+                )
+            pl.semaphore_wait(bar, len(offsets) + 3)
+            return
+        if along_z:
+
+            @pl.when(self.z > 0)
+            def _():
+                pl.semaphore_signal(bar, inc=1, device_id=self.down(), device_id_type=MESH)
+
+            @pl.when(self.z < 3)
+            def _():
+                pl.semaphore_signal(bar, inc=1, device_id=self.up(), device_id_type=MESH)
+
+        peers = len(offsets)
+        if along_z:
+            peers = peers + jnp.where(self.z > 0, 1, 0) + jnp.where(self.z < 3, 1, 0)
+        pl.semaphore_wait(bar, peers)
+
+
+def drive(*tasks):
+    waiting = [(0.0, i, task) for i, task in enumerate(tasks)]
+    while waiting:
+        waiting.sort(key=lambda item: item[:2])
+        _, i, task = waiting.pop(0)
+        at = next(task, None)
+        if at is not None:
+            waiting.append((at, i, task))
+
+
+def z_gather(me, src, dst, unit, begin=0.0):
+    rows = src.shape[0]
+    z = me.z
+
+    def block(j):
+        return dst.at[pl.ds(pl.multiple_of(j * rows, rows), rows)]
+
+    ups = [me.slot() for _ in range(3)]
+    downs = [me.slot() for _ in range(3)]
+    if begin:
+        yield begin
+
+    @pl.when(z < 3)
+    def _():
+        me.again(ups[0], src, block(z), me.up()).start()
+
+    @pl.when(z > 0)
+    def _():
+        me.again(downs[0], src, block(z), me.down()).start()
+
+    own = me.local(src, block(z))
+    own.start()
+    for j in (1, 2, 3):
+        yield begin + unit * j
+
+        @pl.when(z >= j)
+        def _():
+            me.again(ups[j - 1], block(z - j), block(z - j), me.up()).wait_recv()
+
+        if j < 3:
+
+            @pl.when((z >= j) & (z < 3))
+            def _():
+                me.again(ups[j], block(z - j), block(z - j), me.up()).start()
+
+        @pl.when(z <= 3 - j)
+        def _():
+            me.again(downs[j - 1], block(z + j), block(z + j), me.down()).wait_recv()
+
+        if j < 3:
+
+            @pl.when((z <= 3 - j) & (z > 0))
+            def _():
+                me.again(downs[j], block(z + j), block(z + j), me.down()).start()
+
+    yield begin + unit * 3.2
+    own.wait()
+    for j in (0, 1, 2):
+
+        @pl.when((z >= j) & (z < 3))
+        def _():
+            me.again(ups[j], block(z - j), block(z - j), me.up()).wait_send()
+
+        @pl.when((z <= 3 - j) & (z > 0))
+        def _():
+            me.again(downs[j], block(z + j), block(z + j), me.down()).wait_send()
+
+
+def plane_gather(me, src, dst, unit, begin=0.0):
+    rows = src.shape[0]
+    half = rows // 2
+
+    def block(i):
+        return dst.at[pl.ds(i * rows, rows)]
+
+    def part(i, h):
+        return dst.at[pl.ds(i * rows + h * half, half)]
+
+    if begin:
+        yield begin
+    to_x = me.copy(src, block(2), me.plane(2))
+    to_y = me.copy(src, block(4), me.plane(4))
+    to_c = me.copy(src, block(1), me.plane(1))
+    own = me.local(src, block(0))
+    for copy in (to_x, to_y, to_c, own):
+        copy.start()
+    yield begin + unit
+    to_x.wait_recv()
+    x_on = me.copy(part(2, 0), part(6, 0), me.plane(4))
+    x_core = me.copy(block(2), block(3), me.plane(1))
+    x_on.start()
+    x_core.start()
+    to_y.wait_recv()
+    y_on = me.copy(part(4, 1), part(6, 1), me.plane(2))
+    y_core = me.copy(block(4), block(5), me.plane(1))
+    y_on.start()
+    y_core.start()
+    yield begin + unit * 1.5
+    x_on.wait_recv()
+    d0_core = me.copy(part(6, 0), part(7, 0), me.plane(1))
+    d0_core.start()
+    y_on.wait_recv()
+    d1_core = me.copy(part(6, 1), part(7, 1), me.plane(1))
+    d1_core.start()
+    yield begin + unit * 1.7
+    own.wait()
+    for copy in (to_c, x_core, y_core, d0_core, d1_core):
+        copy.wait_recv()
+    for copy in (to_x, to_y, to_c, x_on, x_core, y_on, y_core, d0_core, d1_core):
+        copy.wait_send()
+
+
+def add_rows(dst, a, b, step=32):
+    rows = a.shape[0]
+
+    def body(i, _):
+        at = pl.ds(pl.multiple_of(i * step, step), step)
+        dst[at, :] = (a[at, :].astype(f32) + b[at, :].astype(f32)).astype(dst.dtype)
+        return 0
+
+    lax.fori_loop(0, rows // step, body, 0)
+
+
+def z_reduce_all(me, part, total, inbox, across, partial, out, unit, chunks=8, begin=0.0):
+    rows = part.shape[0] // chunks
+    z = me.z
+    end = (z == 0) | (z == 3)
+    middle = (z == 1) | (z == 2)
+    inward = {"head": jnp.where(z < 2, z + 1, z - 1)}
+    outward = {"head": jnp.where(z < 2, z - 1, z + 1)}
+    first = [me.slot() for _ in range(chunks)]
+    second = [me.slot() for _ in range(chunks)]
+    third = [me.slot() for _ in range(chunks)]
+    store = [me.slot() for _ in range(chunks)]
+
+    def at(ref, k):
+        return ref.at[pl.ds(k * rows, rows)]
+
+    def put(k):
+        return pltpu.make_async_copy(at(total, k), at(out, k), me.send_sem.at[store[k]])
+
+    if begin:
+        yield begin
+
+    @pl.when(end)
+    def _():
+        for k in range(chunks):
+            me.again(first[k], at(part, k), at(inbox, k), inward).start()
+
+    hop = unit / chunks
+    for k in range(chunks + 2):
+        yield begin + hop * (k + 1) + 2.0
+
+        @pl.when(middle)
+        def _():
+            if k < chunks:
+                me.again(first[k], at(part, k), at(inbox, k), inward).wait_recv()
+                add_rows(at(partial, k), at(part, k), at(inbox, k))
+                me.again(second[k], at(partial, k), at(across, k), inward).start()
+            if 1 <= k <= chunks:
+                j = k - 1
+                me.again(second[j], at(partial, j), at(across, j), inward).wait_recv()
+                add_rows(at(total, j), at(partial, j), at(across, j))
+                me.again(third[j], at(total, j), at(total, j), outward).start()
+                put(j).start()
+
+        @pl.when(end)
+        def _():
+            if k >= 2:
+                j = k - 2
+                me.again(third[j], at(total, j), at(total, j), outward).wait_recv()
+                put(j).start()
+
+    yield begin + unit + hop * 3
+
+    @pl.when(end)
+    def _():
+        for k in range(chunks):
+            me.again(first[k], at(part, k), at(inbox, k), inward).wait_send()
+
+    @pl.when(middle)
+    def _():
+        for k in range(chunks):
+            me.again(second[k], at(partial, k), at(across, k), inward).wait_send()
+            me.again(third[k], at(total, k), at(total, k), outward).wait_send()
+
+    for k in range(chunks):
+        put(k).wait()
+
+
+def z_reduce_scatter(me, part, from_below, from_above, sums_up, sums_down, own, unit, begin=0.0):
+    rows = part.shape[0] // 4
+    z = me.z
+    ups = [me.slot() for _ in range(4)]
+    downs = [me.slot() for _ in range(4)]
+
+    def at(ref, j):
+        return ref.at[pl.ds(j * rows, rows)]
+
+    if begin:
+        yield begin
+
+    @pl.when(z == 0)
+    def _():
+        for j in (3, 2, 1):
+            me.again(ups[j], at(part, j), at(from_below, j), me.up()).start()
+
+    @pl.when(z == 3)
+    def _():
+        for j in (0, 1, 2):
+            me.again(downs[j], at(part, j), at(from_above, j), me.down()).start()
+
+    for step, j in enumerate((3, 2)):
+        for stop in range(1, j):
+            yield begin + unit * (3 - j + stop) + 1.0
+
+            @pl.when(z == stop)
+            def _():
+                me.again(ups[j], at(part, j), at(from_below, j), me.up()).wait_recv()
+                add_rows(at(sums_up, j), at(part, j), at(from_below, j))
+                me.again(ups[j], at(sums_up, j), at(from_below, j), me.up()).start()
+
+            @pl.when(z == 3 - stop)
+            def _():
+                i = 3 - j
+                me.again(downs[i], at(part, i), at(from_above, i), me.down()).wait_recv()
+                add_rows(at(sums_down, i), at(part, i), at(from_above, i))
+                me.again(downs[i], at(sums_down, i), at(from_above, i), me.down()).start()
+
+    yield begin + unit * 3 + 1.5
+    for j in range(4):
+
+        @pl.when(z == j)
+        def _():
+            if j > 0:
+                me.again(ups[j], at(part, j), at(from_below, j), me.up()).wait_recv()
+            if j < 3:
+                me.again(downs[j], at(part, j), at(from_above, j), me.down()).wait_recv()
+
+            def body(i, _):
+                span = pl.ds(pl.multiple_of(i * 32, 32), 32)
+                there = pl.ds(pl.multiple_of(j * rows + i * 32, 32), 32)
+                value = part[there, :].astype(f32)
+                if j > 0:
+                    value = value + from_below[there, :].astype(f32)
+                if j < 3:
+                    value = value + from_above[there, :].astype(f32)
+                own[span, :] = value
+                return 0
+
+            lax.fori_loop(0, rows // 32, body, 0)
+            for i in range(4):
+                if i > j:
+                    me.again(ups[i], at(part, i), at(from_below, i), me.up()).wait_send()
+                if i < j:
+                    me.again(downs[i], at(part, i), at(from_above, i), me.down()).wait_send()
+
+
+def plane_scatter_scratch(rows, cols):
+    half = rows // 2
+    return [
+        pltpu.VMEM((4, rows, cols), bf16),
+        pltpu.VMEM((4, rows, cols), bf16),
+        pltpu.VMEM((2, half, cols), bf16),
+        pltpu.VMEM((2, half, cols), bf16),
+        pltpu.VMEM((half, cols), bf16),
+        pltpu.VMEM((half, cols), bf16),
+    ]
+
+
+def plane_scatter(me, src, out, scratch, unit, begin=0.0):
+    held, other, over_x, over_y, last_y, last_x = scratch
+    rows = out.shape[0]
+    half = rows // 2
+
+    def block(i):
+        return src.at[pl.ds(i * rows, rows)]
+
+    first, second = pl.ds(0, half), pl.ds(half, half)
+    if begin:
+        yield begin
+    loads, cores = {}, {}
+    for i in (6, 2, 4, 0):
+        cores[i] = me.copy(block(i + 1), other.at[i // 2], me.plane(1))
+        cores[i].start()
+        loads[i] = me.local(block(i), held.at[i // 2])
+        loads[i].start()
+    yield begin + 3.0
+    for i in (6, 2, 4, 0):
+        loads[i].wait()
+        cores[i].wait_recv()
+        add_rows(held.at[i // 2], held.at[i // 2], other.at[i // 2])
+        if i == 6:
+            six_x = me.copy(held.at[3, first], over_x.at[1], me.plane(2))
+            six_y = me.copy(held.at[3, second], over_y.at[1], me.plane(4))
+            six_x.start()
+            six_y.start()
+        if i == 2:
+            two_x = me.copy(held.at[1, first], over_x.at[0], me.plane(2))
+            two_x.start()
+        if i == 4:
+            four_y = me.copy(held.at[2, second], over_y.at[0], me.plane(4))
+            four_y.start()
+    yield begin + 4.0 + unit * 0.5
+    six_x.wait_recv()
+    add_rows(held.at[2, first], held.at[2, first], over_x.at[1])
+    to_y = me.copy(held.at[2, first], last_y, me.plane(4))
+    to_y.start()
+    six_y.wait_recv()
+    add_rows(held.at[1, second], held.at[1, second], over_y.at[1])
+    to_x = me.copy(held.at[1, second], last_x, me.plane(2))
+    to_x.start()
+    yield begin + 5.0 + unit * 1.5
+    two_x.wait_recv()
+    four_y.wait_recv()
+    to_y.wait_recv()
+    to_x.wait_recv()
+
+    def body(i, _):
+        at = pl.ds(pl.multiple_of(i * 32, 32), 32)
+        low = pl.ds(pl.multiple_of(half + i * 32, 32), 32)
+        out[at, :] = (
+            held[0, at, :].astype(f32) + over_x[0, at, :].astype(f32) + last_y[at, :].astype(f32)
+        ).astype(out.dtype)
+        out[low, :] = (
+            held[0, low, :].astype(f32) + over_y[0, at, :].astype(f32) + last_x[at, :].astype(f32)
+        ).astype(out.dtype)
+        return 0
+
+    lax.fori_loop(0, half // 32, body, 0)
+    for i in (6, 2, 4, 0):
+        cores[i].wait_send()
+    for copy in (six_x, six_y, two_x, four_y, to_y, to_x):
+        copy.wait_send()
+
+
+def params(number, vmem=60 * 2**20):
+    return pltpu.CompilerParams(
+        collective_id=number, has_side_effects=True, vmem_limit_bytes=vmem
+    )
+
+
+def shape(dims, kind=bf16):
+    return jax.ShapeDtypeStruct(dims, kind)
+
+
+def first_kernel(tok, wqkv, gains, wo, wg, tok_all, wqkv_all, gains_all, wo_all, wg_all, ss, rs):
+    me = Here(ss, rs)
+    me.enter((1, 2, 4))
+    drive(
+        z_gather(me, tok, tok_all, 11.3),
+        plane_gather(me, wqkv, wqkv_all, 7.0),
+        plane_gather(me, gains, gains_all, 7.1),
+        plane_gather(me, wo, wo_all, 12.0, 0.1),
+        plane_gather(me, wg, wg_all, 27.0, 0.2),
+    )
+
+
+def first(tok, wqkv, gains, wo, wg):
+    def grown(a, n):
+        return shape((a.shape[0] * n,) + a.shape[1:])
+
+    return pl.pallas_call(
+        first_kernel,
+        out_shape=(grown(tok, 4), grown(wqkv, 8), grown(gains, 8), grown(wo, 8), grown(wg, 8)),
+        in_specs=[VM] * 5,
+        out_specs=[HB] * 5,
+        scratch_shapes=dma_sems(64),
+        compiler_params=params(1),
+        name="gather_first",
+    )(tok, wqkv, gains, wo, wg)
+
+
+def attention_forward(me, q_t, kv_own, kv, v_t, key_pos, query_pos, out_t, log_sum, kv_all, per):
+    heads, hd, rows = q_t.shape
+    blocks = kv.shape[0] // rows
+
+    def block(i):
+        return kv.at[pl.ds(i * rows, rows)]
+
+    copies = [me.copy(kv_own, block(i), me.plane(i)) for i in (1, 2, 3)]
+    for copy in copies:
+        copy.start()
+    own = me.local(kv_own, block(0))
+    own.start()
+    yield 0.2
+    own.wait()
+    for copy in copies:
+        copy.wait_recv()
+    save = me.local(kv, kv_all)
+    save.start()
+    for i in range(blocks):
+        v_t[:, i * rows : (i + 1) * rows] = kv[i * rows : (i + 1) * rows, :].astype(f32).T[hd:, :].astype(bf16)
+
+    def head(h, _):
+        q = q_t[h]
+        limit = query_pos[0:1, :]
+
+        def step(i, state):
+            top, total, acc = state
+            at = pl.ds(pl.multiple_of(i * rows, rows), rows)
+            s = jnp.dot(kv[at, 0:hd], q, preferred_element_type=f32)
+            pos = key_pos[at, :]
+            pos = jnp.concatenate([pos] * (rows // 128), axis=1)
+            s = jnp.where(pos <= limit, s, masked_value)
+            new = jnp.maximum(top, jnp.max(s, axis=0, keepdims=True))
+            p = jnp.exp(s - new)
+            factor = jnp.exp(top - new)
+            total = total * factor + jnp.sum(p, axis=0, keepdims=True)
+            acc = acc * factor + jnp.dot(v_t[:, at], p.astype(bf16), preferred_element_type=f32)
+            return new, total, acc
+
+        top, total, acc = lax.fori_loop(
+            0,
+            blocks,
+            step,
+            (
+                jnp.full((1, rows), masked_value, f32),
+                jnp.zeros((1, rows), f32),
+                jnp.zeros((hd, rows), f32),
+            ),
+        )
+        out_t[h] = acc / total
+        log_sum[h] = top + jnp.log(total)
+        return 0
+
+    for h in range(0, heads, 2):
+        yield 6.0 + per * h
+        lax.fori_loop(h, h + 2, head, 0)
+    yield 6.0 + per * heads
+    save.wait()
+    for copy in copies:
+        copy.wait_send()
+
+
+def second_kernel(q_t, kv_own, key_pos, query_pos, cot, wu, out_t, log_sum, kv_all, cot_all, wu_all, kv, v_t, ss, rs):
+    me = Here(ss, rs)
+    me.enter((1, 2, 3, 4))
+    drive(
+        attention_forward(me, q_t, kv_own, kv, v_t, key_pos, query_pos, out_t, log_sum, kv_all, 3.5),
+        z_gather(me, cot, cot_all, 11.3, 0.1),
+        plane_gather(me, wu, wu_all, 15.5, 0.3),
+    )
+
+
+def second(q_t, kv_own, key_pos, query_pos, cot, wu):
+    heads, hd, rows = q_t.shape
+    keys = key_pos.shape[0]
+    return pl.pallas_call(
+        second_kernel,
+        out_shape=(
+            shape((heads, hd, rows), f32),
+            shape((heads, 1, rows), f32),
+            shape((keys, 2 * hd)),
+            shape((cot.shape[0] * 4, cot.shape[1])),
+            shape((wu.shape[0] * 8, wu.shape[1])),
+        ),
+        in_specs=[VM] * 6,
+        out_specs=[VM, VM, HB, HB, HB],
+        scratch_shapes=[pltpu.VMEM((keys, 2 * hd), bf16), pltpu.VMEM((hd, keys), bf16)] + dma_sems(32),
+        compiler_params=params(2),
+        name="attention_forward",
+    )(q_t, kv_own, key_pos, query_pos, cot, wu)
+
+
+def third_kernel(part, wd, total_out, wd_all, total, inbox, across, partial, ss, rs):
+    me = Here(ss, rs)
+    me.enter((1, 2, 4))
+    drive(
+        z_reduce_all(me, part, total, inbox, across, partial, total_out, 45.0),
+        plane_gather(me, wd, wd_all, 15.5, 0.1),
+    )
+
+
+def third(part, wd):
+    rows = pltpu.VMEM(part.shape, bf16)
+    return pl.pallas_call(
+        third_kernel,
+        out_shape=(shape(part.shape), shape((wd.shape[0] * 8, wd.shape[1]))),
+        in_specs=[VM] * 2,
+        out_specs=[HB] * 2,
+        scratch_shapes=[rows] * 4 + dma_sems(64),
+        compiler_params=params(3),
+        name="sum_branch",
+    )(part, wd)
+
+
+def fourth_kernel(part, dwd, total_out, dwd_own, total, inbox, across, partial, *rest):
+    *scratch, ss, rs = rest
+    me = Here(ss, rs)
+    me.enter((1, 2, 4))
+    drive(
+        z_reduce_all(me, part, total, inbox, across, partial, total_out, 45.0),
+        plane_scatter(me, dwd, dwd_own, scratch, 15.5, 0.1),
+    )
+
+
+def fourth(part, dwd):
+    rows = pltpu.VMEM(part.shape, bf16)
+    own = (dwd.shape[0] // 8, dwd.shape[1])
+    return pl.pallas_call(
+        fourth_kernel,
+        out_shape=(shape(part.shape), shape(own, f32)),
+        in_specs=[VM, HB],
+        out_specs=[HB, VM],
+        scratch_shapes=[rows] * 4 + plane_scatter_scratch(*own) + dma_sems(64),
+        compiler_params=params(4),
+        name="sum_grad_normed_two",
+    )(part, dwd)
+
+
+def attention_backward(me, q_t, q_n, g_t, g_n, kv_all, log_sum, delta, key_pos, query_pos, dq_t, dkv_own, kv, k_t, dk, dv, dkv, came, per):
+    heads, hd, rows = q_t.shape
+    blocks = kv.shape[0] // rows
+    load = me.local(kv_all, kv)
+    load.start()
+    dk[...] = jnp.zeros_like(dk)
+    dv[...] = jnp.zeros_like(dv)
+    load.wait()
+    for i in range(blocks):
+        k_t[:, i * rows : (i + 1) * rows] = kv[i * rows : (i + 1) * rows, :].astype(f32).T[:hd, :].astype(bf16)
+
+    def head(h, _):
+        q, g = q_t[h], g_t[h]
+        limit = query_pos[0:1, :]
+
+        def step(i, acc):
+            at = pl.ds(pl.multiple_of(i * rows, rows), rows)
+            both = kv[at, :]
+            s = jnp.dot(both[:, 0:hd], q, preferred_element_type=f32)
+            pos = key_pos[at, :]
+            pos = jnp.concatenate([pos] * (rows // 128), axis=1)
+            s = jnp.where(pos <= limit, s, masked_value)
+            p = jnp.exp(s - log_sum[h])
+            dp = jnp.dot(both[:, hd:], g, preferred_element_type=f32)
+            ds = (p * (dp - delta[h])).astype(bf16)
+            dv[at, :] += jnp.dot(p.astype(bf16), g_n[h], preferred_element_type=f32)
+            dk[at, :] += jnp.dot(ds, q_n[h], preferred_element_type=f32)
+            return acc + jnp.dot(k_t[:, at], ds, preferred_element_type=f32)
+
+        acc = lax.fori_loop(0, blocks, step, jnp.zeros((hd, rows), f32))
+        dq_t[h] = (acc * (1.0 / math.sqrt(hd))).astype(bf16)
+        return 0
+
+    for h in range(0, heads, 2):
+        yield 0.3 + per * h
+        lax.fori_loop(h, h + 2, head, 0)
+    for i in range(blocks):
+        at = slice(i * rows, (i + 1) * rows)
+        dkv[at, :] = jnp.concatenate([dk[at, :], dv[at, :]], axis=1).astype(bf16)
+    copies = [
+        me.copy(dkv.at[pl.ds(i * rows, rows)], came.at[i - 1], me.plane(i)) for i in (1, 2, 3)
+    ]
+    for copy in copies:
+        copy.start()
+    yield 0.3 + per * heads + 8.0
+    for copy in copies:
+        copy.wait_recv()
+    value = dkv[0:rows, :].astype(f32)
+    for i in range(blocks - 1):
+        value = value + came[i].astype(f32)
+    dkv_own[...] = value
+    for copy in copies:
+        copy.wait_send()
+
+
+def fifth_kernel(
+    q_t, q_n, g_t, g_n, kv_all, log_sum, delta, key_pos, query_pos, out_part, dwg, dwu,
+    dq_t, dkv_own, out_own, dwg_own, dwu_own,
+    kv, k_t, dk, dv, dkv, came, below, above, sums_up, sums_down, *rest
+):
+    *scratch, ss, rs = rest
+    me = Here(ss, rs)
+    me.enter((1, 2, 3, 4))
+    drive(
+        plane_scatter(me, dwg, dwg_own, scratch[:6], 15.5),
+        plane_scatter(me, dwu, dwu_own, scratch[6:], 15.5, 18.0),
+        z_reduce_scatter(me, out_part, below, above, sums_up, sums_down, out_own, 11.3),
+        attention_backward(
+            me, q_t, q_n, g_t, g_n, kv_all, log_sum, delta, key_pos, query_pos,
+            dq_t, dkv_own, kv, k_t, dk, dv, dkv, came, 6.0,
+        ),
+    )
+
+
+def fifth(q_t, q_n, g_t, g_n, kv_all, log_sum, delta, key_pos, query_pos, out_part, dwg, dwu):
+    heads, hd, rows = q_t.shape
+    keys = key_pos.shape[0]
+    own = (dwg.shape[0] // 8, dwg.shape[1])
+    part = pltpu.VMEM(out_part.shape, bf16)
+    return pl.pallas_call(
+        fifth_kernel,
+        out_shape=(
+            shape((heads, hd, rows)),
+            shape((rows, 2 * hd), f32),
+            shape((out_part.shape[0] // 4, out_part.shape[1]), f32),
+            shape(own, f32),
+            shape(own, f32),
+        ),
+        in_specs=[VM] * 4 + [HB] + [VM] * 5 + [HB] * 2,
+        out_specs=[VM] * 5,
+        scratch_shapes=[
+            pltpu.VMEM((keys, 2 * hd), bf16),
+            pltpu.VMEM((hd, keys), bf16),
+            pltpu.VMEM((keys, hd), f32),
+            pltpu.VMEM((keys, hd), f32),
+            pltpu.VMEM((keys, 2 * hd), bf16),
+            pltpu.VMEM((keys // rows - 1, rows, 2 * hd), bf16),
+            part, part, part, part,
+        ]
+        + plane_scatter_scratch(*own) * 2
+        + dma_sems(64),
+        compiler_params=params(5),
+        name="attention_backward",
+    )(q_t, q_n, g_t, g_n, kv_all, log_sum, delta, key_pos, query_pos, out_part, dwg, dwu)
+
+
+def gain_sums(me, src, out, came, mine, came_z):
+    n = src.shape[0] // 8
+    copies = [me.copy(src.at[pl.ds(i * 8, 8)], came.at[i - 1], me.plane(i)) for i in range(1, n)]
+    for copy in copies:
+        copy.start()
+    yield 4.0
+    value = src[0:8, :]
+    for i, copy in enumerate(copies):
+        copy.wait_recv()
+        value = value + came[i]
+    mine[...] = value
+    again = [
+        me.copy(mine, came_z.at[d - 1], {"head": (me.z + d) % 4}) for d in (1, 2, 3)
+    ]
+    for copy in again:
+        copy.start()
+    yield 8.0
+    for d, copy in enumerate(again):
+        copy.wait_recv()
+        value = value + came_z[d]
+    out[...] = value
+    for copy in copies + again:
+        copy.wait_send()
+
+
+def sixth_kernel(
+    part, dwqkv, dwo, gains,
+    own, dwq_own, dwkv_all, dwo_own, gains_out,
+    below, above, sums_up, sums_down, dwqkv_own, dwkv_own, came_kv, came, mine, came_z, *rest
+):
+    *scratch, ss, rs = rest
+    me = Here(ss, rs)
+    me.enter(tuple(range(1, 8)), all_z=True)
+    wide = dwq_own.shape[1]
+
+    def weights():
+        yield from plane_scatter(me, dwqkv, dwqkv_own, scratch[:6], 7.0, 0.1)
+        dwq_own[...] = dwqkv_own[:, :wide]
+        dwkv_own[...] = dwqkv_own[:, wide:].astype(bf16)
+        copies = [
+            me.copy(dwkv_own, came_kv.at[d - 1], {"head": (me.z + d) % 4}) for d in (1, 2, 3)
+        ]
+        for copy in copies:
+            copy.start()
+        yield 30.0
+        for copy in copies:
+            copy.wait_recv()
+        dwkv_all[0] = dwkv_own[...]
+        for d in (1, 2, 3):
+            dwkv_all[d] = came_kv[d - 1]
+        for copy in copies:
+            copy.wait_send()
+
+    drive(
+        gain_sums(me, gains, gains_out, came, mine, came_z),
+        z_reduce_scatter(me, part, below, above, sums_up, sums_down, own, 11.3),
+        weights(),
+        plane_scatter(me, dwo, dwo_own, scratch[6:], 6.0, 9.0),
+    )
+
+
+def sixth(part, dwqkv, dwo, gains):
+    rows, cols = dwqkv.shape[0] // 8, dwqkv.shape[1]
+    wide = dwo.shape[1]
+    whole = pltpu.VMEM(part.shape, bf16)
+    return pl.pallas_call(
+        sixth_kernel,
+        out_shape=(
+            shape((part.shape[0] // 4, part.shape[1]), f32),
+            shape((rows, wide), f32),
+            shape((4, rows, cols - wide)),
+            shape((rows, wide), f32),
+            shape((8, gains.shape[1]), f32),
+        ),
+        in_specs=[VM, HB, HB, VM],
+        out_specs=[VM] * 5,
+        scratch_shapes=[
+            whole, whole, whole, whole,
+            pltpu.VMEM((rows, cols), f32),
+            pltpu.VMEM((rows, cols - wide), bf16),
+            pltpu.VMEM((3, rows, cols - wide), bf16),
+            pltpu.VMEM((7, 8, gains.shape[1]), f32),
+            pltpu.VMEM((8, gains.shape[1]), f32),
+            pltpu.VMEM((3, 8, gains.shape[1]), f32),
+        ]
+        + plane_scatter_scratch(rows, cols)
+        + plane_scatter_scratch(rows, wide)
+        + dma_sems(64),
+        compiler_params=params(6),
+        name="scatter_last",
+    )(part, dwqkv, dwo, gains)
+
+
+def local_fast(
+    tokens, w_query, w_key, w_value, w_out, w_gate, w_up, w_down, gain_attn, gain_mlp, stretch_order, cotangent
+):
+    row_count, width = tokens.shape
+    groups = 4
+    heads = H // groups
+    head_rows = row_count * groups
+    stretch_rows = head_rows // 2
+    cols = width // 8
+    contract_last = (((1,), (1,)), ((), ()))
+    contract_first = (((0,), (0,)), ((), ()))
+    z = lax.axis_index("head")
+    b = lax.axis_index("blk")
+    place = lax.axis_index("fsdp") * 4 + b
+    own_first = z * row_count
+
+    def turn(values):
+        return jnp.concatenate(
+            [
+                lax.dynamic_slice_in_dim(values, jnp.bitwise_xor(place, i) * cols, cols, values.ndim - 1)
+                for i in range(8)
+            ],
+            axis=-1,
+        )
+
+    def own_rows(values):
+        return lax.dynamic_slice_in_dim(values, own_first, row_count, 0)
+
+    query_positions = stretch_positions(stretch_order, b * head_rows, head_rows, stretch_rows)
+    key_positions = jnp.concatenate(
+        [
+            stretch_positions(stretch_order, jnp.bitwise_xor(b, i) * head_rows, head_rows, stretch_rows)
+            for i in range(4)
+        ]
+    )
+    key_pos = jnp.broadcast_to(key_positions[:, None], (key_positions.shape[0], 128))
+    query_pos = jnp.broadcast_to(query_positions[None, :], (8, head_rows))
+    cos_rows, sin_rows = rope_tables(query_positions, HD)
+    cos_t, sin_t = cos_rows.T, sin_rows.T
+
+    def rotate_t(values):
+        a, c = values[..., : HD // 2, :], values[..., HD // 2 :, :]
+        return jnp.concatenate([a * cos_t - c * sin_t, c * cos_t + a * sin_t], axis=-2)
+
+    def unrotate_t(values):
+        a, c = values[..., : HD // 2, :], values[..., HD // 2 :, :]
+        return jnp.concatenate([a * cos_t + c * sin_t, c * cos_t - a * sin_t], axis=-2)
+
+    slot_first = z * HD
+    w_qkv = jnp.concatenate(
+        [
+            w_query,
+            lax.dynamic_slice_in_dim(w_key, slot_first, HD, 1),
+            lax.dynamic_slice_in_dim(w_value, slot_first, HD, 1),
+        ],
+        axis=1,
+    )
+    gains = jnp.concatenate([gain_attn[None], gain_mlp[None], jnp.zeros((30, cols), bf16)])
+    tok_all, wqkv_all, gains_all, wo_all, wg_all = first(tokens, w_qkv, gains, w_out, w_gate)
+    gains_all = gains_all.reshape(8, 32, cols)
+    gain_one = gains_all[:, 0].reshape(width).astype(f32)
+    gain_two = gains_all[:, 1].reshape(width).astype(f32)
+
+    x_rows = turn(tok_all).astype(f32)
+    inv_attn = lax.rsqrt(jnp.mean(x_rows * x_rows, axis=-1, keepdims=True) + norm_epsilon)
+    normed = (x_rows * inv_attn * gain_one).astype(bf16)
+    qkv_t = lax.dot_general(wqkv_all, normed, (((0,), (1,)), ((), ())), preferred_element_type=f32)
+    wide = heads * HD
+    q_t = rotate_t(qkv_t[:wide].reshape(heads, HD, head_rows)).astype(bf16) * bf16(1.0 / math.sqrt(HD))
+    k_t = rotate_t(qkv_t[wide : wide + HD]).astype(bf16)
+    v_t = qkv_t[wide + HD :].astype(bf16)
+    kv_own = jnp.concatenate([k_t, v_t], axis=0).T
+    out_t, log_sum, kv_all, cot_all, wu_all = second(q_t, kv_own, key_pos, query_pos, cotangent, w_up)
+    attended_t = out_t.astype(bf16).reshape(wide, head_rows)
+    branch_part = lax.dot_general(
+        attended_t, wo_all, (((0,), (1,)), ((), ())), preferred_element_type=f32
+    ).astype(bf16)
+    branch, wd_all = third(branch_part, w_down)
+
+    hidden_rows = x_rows + branch.astype(f32)
+    inv_mlp = lax.rsqrt(jnp.mean(hidden_rows * hidden_rows, axis=-1, keepdims=True) + norm_epsilon)
+    normed_two = (hidden_rows * inv_mlp * gain_two).astype(bf16)
+    gate = jnp.dot(normed_two, wg_all, preferred_element_type=f32)
+    up = jnp.dot(normed_two, wu_all, preferred_element_type=f32)
+    gate_sigmoid = jax.nn.sigmoid(gate)
+    gate_silu = gate * gate_sigmoid
+    hidden = (gate_silu * up).astype(bf16)
+    out_part = lax.dot_general(hidden, wd_all, contract_last, preferred_element_type=f32).astype(bf16)
+
+    cot_rows = turn(cot_all)
+    grad_hidden = jnp.dot(cot_rows, wd_all, preferred_element_type=f32)
+    d_gate = (grad_hidden * up * gate_sigmoid * (1.0 + gate * (1.0 - gate_sigmoid))).astype(bf16)
+    d_up = (grad_hidden * gate_silu).astype(bf16)
+    two_part = lax.dot_general(d_gate, wg_all, contract_last, preferred_element_type=f32)
+    two_part = two_part + lax.dot_general(d_up, wu_all, contract_last, preferred_element_type=f32)
+    dwd = lax.dot_general(cot_rows, hidden, contract_first, preferred_element_type=f32).astype(bf16)
+    dwg = lax.dot_general(normed_two, d_gate, contract_first, preferred_element_type=f32).astype(bf16)
+    dwu = lax.dot_general(normed_two, d_up, contract_first, preferred_element_type=f32).astype(bf16)
+    grad_two, dwd_own = fourth(two_part.astype(bf16), dwd)
+
+    grad_two = grad_two.astype(f32)
+    grad_hidden_rows = cot_rows.astype(f32) + norm_input_grad(hidden_rows, inv_mlp, gain_two, grad_two)
+    grad_low = grad_hidden_rows.astype(bf16)
+    g_t = lax.dot_general(wo_all, grad_low, (((0,), (1,)), ((), ())), preferred_element_type=f32)
+    g_t = g_t.astype(bf16).reshape(heads, HD, head_rows)
+    dwo = lax.dot_general(
+        grad_low, attended_t, (((0,), (1,)), ((), ())), preferred_element_type=f32
+    ).astype(bf16)
+    delta = jnp.sum(g_t.astype(f32) * out_t, axis=1, keepdims=True)
+    q_n = q_t.transpose(0, 2, 1)
+    g_n = g_t.transpose(0, 2, 1)
+    dq_t, dkv, out_own, dwg_own, dwu_own = fifth(
+        q_t, q_n, g_t, g_n, kv_all, log_sum, delta, key_pos, query_pos, out_part, dwg, dwu
+    )
+
+    dkv_t = dkv.T.astype(bf16).astype(f32)
+    dqkv_t = jnp.concatenate(
+        [
+            unrotate_t(dq_t.astype(f32)).reshape(wide, head_rows).astype(bf16),
+            unrotate_t(dkv_t[:HD]).astype(bf16),
+            dkv_t[HD:].astype(bf16),
+        ]
+    )
+    one_part = lax.dot_general(dqkv_t, wqkv_all, (((0,), (1,)), ((), ())), preferred_element_type=f32)
+    dwqkv = lax.dot_general(
+        normed, dqkv_t, (((0,), (1,)), ((), ())), preferred_element_type=f32
+    ).astype(bf16)
+    gain_one_part = jnp.sum(one_part * (x_rows * inv_attn), axis=0).reshape(8, 1, cols)
+    gain_two_part = jnp.sum(
+        own_rows(grad_two) * own_rows(hidden_rows) * own_rows(inv_mlp), axis=0
+    ).reshape(8, 1, cols)
+    gain_parts = jnp.concatenate(
+        [gain_one_part, gain_two_part, jnp.zeros((8, 6, cols), f32)], axis=1
+    ).reshape(64, cols)
+    grad_one, dwq_own, dwkv_all, dwo_own, gain_grads = sixth(one_part.astype(bf16), dwqkv, dwo, gain_parts)
+
+    layer_low = turn((own_rows(hidden_rows) + out_own).astype(bf16))
+    x_own = own_rows(x_rows)
+    grad_tokens = own_rows(grad_hidden_rows) + norm_input_grad(x_own, own_rows(inv_attn), gain_one, grad_one)
+    grad_tokens = turn(grad_tokens.astype(bf16))
+    slots = jnp.concatenate(
+        [lax.dynamic_slice_in_dim(dwkv_all, (z - j) % 4, 1, 0) for j in range(4)], axis=0
+    ).astype(f32)
+    grad_key = slots[:, :, :HD].transpose(1, 0, 2).reshape(cols, groups * HD)
+    grad_value = slots[:, :, HD:].transpose(1, 0, 2).reshape(cols, groups * HD)
+    return (
+        layer_low,
+        grad_tokens,
+        dwq_own,
+        grad_key,
+        grad_value,
+        dwo_own,
+        dwg_own,
+        dwu_own,
+        dwd_own,
+        gain_grads[0],
+        gain_grads[1],
+    )
+
+
 def solution(mesh):
+    sizes = (mesh.shape["fsdp"], mesh.shape["blk"], mesh.shape["head"])
     return jax.shard_map(
-        local,
+        local_fast if sizes == (2, 4, 4) else local,
         mesh=mesh,
         in_specs=(
             P(("fsdp", "blk", "head"), None),

time: 1350 us -> 570 us (0.42)
  waiting for transfers between devices: 944 us -> 0 us
  Pallas kernels: 0 us -> 392 us
  matrix products: 194 us -> 77 us
  blocking collectives: 65.3 us -> 0 us
  starting transfers between devices: 21.7 us -> 0 us
  other arithmetic: 63.2 us -> 42.9 us
  between operations: 16 us -> 2.2 us
    all_gather x10 -> x0, waiting for transfers between devices: 419 us -> none  [the longest x1 149 us: gather_query(): return lax.all_gather(columns, 'head', axis=1, tiled=True)]
    pallas_call x0 -> x6, Pallas kernels: none -> 392 us  [the longest x1 74.6 us: sixth(): pl.pallas_call(sixth_kernel, out_shape=(shape((part.shape[0] // 4, part.s...]
    reduce_scatter x10 -> x0, waiting for transfers between devices: 344 us -> none  [the longest x1 60.7 us: local(): lax.psum_scatter(grad_w_gate.astype(jnp.bfloat16), ('fsdp', 'blk'), scatt...]
    psum x3 -> x0, waiting for transfers between devices: 161 us -> none  [the longest x1 86 us: local(): lax.psum(normed_two_part.astype(jnp.bfloat16), 'head').astype(jnp.float32)]
    dot_general x47 -> x15, matrix products: 194 us -> 77 us  [the longest x1 17 us: local_fast(): lax.dot_general(cot_rows, hidden, contract_first, preferred_element_type=...]
    all_gather x4 -> x0, blocking collectives: 31.9 us -> none  [the longest x1 9.27 us: layer_weights(): lax.all_gather(gain_mlp, ('fsdp', 'blk'), axis=0, tiled=True)]
    unnamed x76 -> x136, local copies, waits for them, and re-layouts: 5.06 us -> 28.3 us
    reduce_sum x8 -> x2, other arithmetic: 24.7 us -> 2.68 us  [the longest x1 2.19 us: local_fast(): jnp.sum(own_rows(grad_two) * own_rows(hidden_rows) * own_rows(inv_mlp), a...]
  transfers between devices with their start and end apart: 28 -> 0, of which waited for: 23 -> 0; matrix products, arithmetic and copies ran while one was open for 13% -> 0% of each run, Pallas kernels for 0% -> 0%
where the time goes in v1:
time: 570 us; the launch traced here: 561 us
  Pallas kernels  392 us (69%)
  matrix products  77 us (14%)
  local copies, waits for them, and re-layouts  46.5 us (8%)
  other arithmetic  42.9 us (8%)
    pallas_call x1, Pallas kernels, sixth(): pl.pallas_call(sixth_kernel, out_shape=(shape((part.shape[0] // 4, part.s...  74.6 us
    pallas_call x1, Pallas kernels, fifth(): pl.pallas_call(fifth_kernel, out_shape=(shape((heads, hd, rows)), shape((...  69.6 us
    pallas_call x1, Pallas kernels, first(): pl.pallas_call(first_kernel, out_shape=(grown(tok, 4), grown(wqkv, 8), gr...  67.3 us
    pallas_call x1, Pallas kernels, fourth(): pl.pallas_call(fourth_kernel, out_shape=(shape(part.shape), shape(own, f3...  66.2 us
    pallas_call x1, Pallas kernels, third(): pl.pallas_call(third_kernel, out_shape=(shape(part.shape), shape((wd.shap...  66.2 us
    pallas_call x1, Pallas kernels, second(): pl.pallas_call(second_kernel, out_shape=(shape((heads, hd, rows), f32), s...  48.2 us
    unnamed x136, local copies, waits for them, and re-layouts  28.3 us
    dot_general x1, matrix products, local_fast(): lax.dot_general(cot_rows, hidden, contract_first, preferred_element_type=...  17 us

profile of v1, /device:TPU:0, one launch (start us, length us, event | category | flops | bytes accessed | tf_op | source)
XLA Modules:
  0.0 560.7 jit_solution(10770460236934609920)
XLA Ops:
  0.6 1.0 constant_dynamic-slice_fusion.4
  1.6 1.8 pad_maximum_fusion.2.wqkv
  5.5 67.3 %gather_first.1 = (bf16[512,2048]{1,0:T(8,128)(2,1)}, bf16[2048,640]{1,0:T(8,128)(2,1)}, bf16[256,256]{1,0:T(8,128)(2,1)}, bf16[2048,512]{1,0:T(8,128)(2,1)}, bf16[2048,1408]{1,0:T(8,128)(2,1)}) custom-call(bf16[128,2048]{1,0:T(8,128)(2,1)} %tok.1, bf16[256,640]{1,0:T(8,128)(2,1)} %pad_maximum_fusion.2.wqkv, bf16[32,256]{1,0:T(8,128)(2,1)} %maximum_maximum_fusion.gains, ...), custom_call_target="tpu_custom_call" | custom-call | tf_op jit(solution)/shard_map/gather_first/pallas_call | solution.py:895
  72.8 0.8 slice_convert_fusion
  73.7 1.0 dynamic-slice_dynamic-update-slice_fusion.15
  74.7 1.0 dynamic-slice_dynamic-update-slice_fusion.14
  75.7 1.0 dynamic-slice_dynamic-update-slice_fusion.13
  76.7 1.0 dynamic-slice_dynamic-update-slice_fusion.12
  77.6 1.0 dynamic-slice_dynamic-update-slice_fusion.11
  78.6 1.0 dynamic-slice_dynamic-update-slice_fusion.10
  79.6 1.0 dynamic-slice_dynamic-update-slice_fusion.9
  80.6 1.1 dynamic-slice_dynamic-update-slice_fusion.8
  82.5 1.7 fusion.3
  84.3 0.9 copy-done.22
  85.2 2.0 copy.88
  87.2 2.0 copy.87
  89.2 0.9 fusion.42
  91.7 1.8 fusion.13
  93.5 2.9 subtract_convert_fusion.1
  96.4 1.0 copy-done.5
  97.4 1.6 maximum_multiply_fusion
  99.1 2.3 copy.75.q_t
  101.4 1.5 slice.82
  102.9 1.6 copy.91
  104.5 1.8 maximum_bitcast_fusion.kv_own
  109.1 1.3 broadcast_in_dim.47.key_pos
  110.4 1.3 broadcast_in_dim.48.query_pos
  111.7 48.2 %attention_forward.1 = (f32[8,64,512]{2,1,0:T(8,128)}, f32[8,1,512]{2,1,0:T(1,128)}, bf16[2048,128]{1,0:T(8,128)(2,1)}, bf16[512,2048]{1,0:T(8,128)(2,1)}, bf16[2048,1408]{1,0:T(8,128)(2,1)}) custom-call(bf16[8,64,512]{2,1,0:T(8,128)(2,1)} %copy.75.q_t, bf16[512,128]{1,0:T(8,128)(2,1)} %maximum_bitcast_fusion.kv_own, s32[2048,128]{1,0:T(8,128)} %broadcast_in_dim.47.key_pos, ...), custom_call_target="tpu_custom_call" | custom-call | tf_op jit(solution)/shard_map/attention_forward/pallas_call | solution.py:981
  159.9 1.3 convert_element_type.129
  162.0 4.3 convolution_convert_fusion.5.part
  166.3 66.2 %sum_branch.1 = (bf16[512,2048]{1,0:T(8,128)(2,1)}, bf16[2048,1408]{1,0:T(8,128)(2,1)}) custom-call(bf16[512,2048]{1,0:T(8,128)(2,1)} %convolution_convert_fusion.5.part, bf16[256,1408]{1,0:T(8,128)(2,1)} %wd.1), custom_call_target="tpu_custom_call" | custom-call | tf_op jit(solution)/shard_map/sum_branch/pallas_call | solution.py:1009
  232.5 4.4 convert_add_fusion
  237.0 1.0 multiply_convert_fusion
  238.1 6.6 %fusion.46 = f32[512,1408]{1,0:T(8,128)S(1)} fusion(bf16[512,2048]{1,0:T(8,128)(2,1)S(1)} %multiply_convert_fusion, bf16[2048,1408]{1,0:T(8,128)(2,1)} %get-tuple-element.44), kind=kOutput, calls=%fused_computation.170 | convolution fusion | flops 2952790016 | bytes 10747904 | tf_op jit(solution)/shard_map/dot_general | solution.py:1325
  245.1 3.4 fusion.45
  248.6 4.3 multiply_convert_fusion.2
  253.0 3.4 fusion.47
  256.5 4.7 add_convert_fusion.part
  261.2 17.0 %convolution_convert_fusion.2.dwd = bf16[2048,1408]{1,0:T(8,128)(2,1)} fusion(bf16[512,2048]{1,0:T(8,128)(2,1)S(1)} %dynamic-slice_dynamic-update-slice_fusion, bf16[512,1408]{1,0:T(8,128)(2,1)S(1)} %get-tuple-element.100), kind=kOutput, calls=%fused_computation.2 | convolution fusion | flops 2955673600 | bytes 9306112 | tf_op jit(solution)/shard_map/dot_general | solution.py:1338
  278.2 66.2 %sum_grad_normed_two.1 = (bf16[512,2048]{1,0:T(8,128)(2,1)}, f32[256,1408]{1,0:T(8,128)}) custom-call(bf16[512,2048]{1,0:T(8,128)(2,1)} %add_convert_fusion.part, bf16[2048,1408]{1,0:T(8,128)(2,1)} %convolution_convert_fusion.2.dwd), custom_call_target="tpu_custom_call" | custom-call | tf_op jit(solution)/shard_map/sum_grad_normed_two/pallas_call | solution.py:1033
  344.4 4.1 convert_element_type.141
  348.6 3.0 fusion.72.q_n
  351.6 2.8 multiply_reduce_fusion.1
  354.5 2.3 subtract_add_fusion
  356.8 1.3 multiply_reduce_fusion.6
  358.7 1.3 copy.76
  360.7 8.0 %convolution_convert_fusion.6.out_part = bf16[512,2048]{1,0:T(8,128)(2,1)} fusion(bf16[512,1408]{1,0:T(8,128)(2,1)} %copy-done.41, bf16[2048,1408]{1,0:T(8,128)(2,1)} %get-tuple-element.42), kind=kOutput, calls=%fused_computation.15 | convolution fusion | flops 2953838592 | bytes 9306112 | tf_op jit(solution)/shard_map/dot_general | solution.py:1330
  368.7 5.3 convolution_convert_fusion.1.dwg
  374.0 5.3 convolution_convert_fusion.dwu
  379.2 69.6 %attention_backward.1 = (bf16[8,64,512]{2,1,0:T(8,128)(2,1)}, f32[512,128]{1,0:T(8,128)}, f32[128,2048]{1,0:T(8,128)}, f32[256,1408]{1,0:T(8,128)}, f32[256,1408]{1,0:T(8,128)}) custom-call(bf16[8,64,512]{2,1,0:T(8,128)(2,1)} %copy.75.q_t, bf16[8,512,64]{2,1,0:T(8,128)(2,1)} %fusion.72.q_n, bf16[8,64,512]{2,1,0:T(8,128)(2,1)} %bitcast.53, ...), custom_call_target="tpu_custom_call" | custom-call | tf_op jit(solution)/shard_map/attention_backward/pallas_call | solution.py:1123
  448.9 2.2 multiply_reduce_fusion.5
  452.3 1.2 fusion.17
  453.7 1.5 copy.78
  457.6 1.1 copy.79
  458.7 5.4 multiply_reduce_fusion
  464.1 3.6 convolution_convert_fusion.3.dwqkv
  467.7 2.6 convolution_convert_fusion.4.dwo
  471.1 74.6 %scatter_last.1 = (f32[128,2048]{1,0:T(8,128)}, f32[256,512]{1,0:T(8,128)}, bf16[4,256,128]{2,1,0:T(8,128)(2,1)}, f32[256,512]{1,0:T(8,128)}, f32[8,256]{1,0:T(8,128)}) custom-call(bf16[512,2048]{1,0:T(8,128)(2,1)} %get-tuple-element.106.part, bf16[2048,640]{1,0:T(8,128)(2,1)} %convolution_convert_fusion.3.dwqkv, ...), custom_call_target="tpu_custom_call" | custom-call | tf_op jit(solution)/shard_map/scatter_last/pallas_call | solution.py:1215
  547.3 1.6 add_convert_fusion.3
  552.2 1.3 fusion.44
  553.6 1.9 copy.125
  556.3 1.1 copy.127
  557.4 1.1 copy.128
  559.2 1.1 copy.129
  (168 shorter events, 20.5 us)
Async XLA Ops:
  80.6 1.8 copy-start.36
  82.4 1.7 copy-start.31
  84.1 1.1 copy-start.22
  87.2 3.2 copy-start.35
  91.7 1.8 copy-start.27
  91.7 1.8 copy-start.33
  93.5 2.9 copy-start.11
  96.4 1.0 copy-start.5
  161.2 0.8 copy-start.16
  232.5 4.4 copy-start.2
  238.0 10.6 %copy-start.13 = (bf16[512,2048]{1,0:T(8,128)(2,1)}, bf16[512,2048]{1,0:T(8,128)(2,1)S(1)}, u32[]{:S(2)}) copy-start(bf16[512,2048]{1,0:T(8,128)(2,1)S(1)} %multiply_convert_fusion) | copy-start | bytes 6291460
  238.0 7.1 %slice-start.2 = ((s8[5767168]{0:T(1024)(128)(4,1)}), s8[4194304]{0:T(1024)(128)(4,1)S(1)}, s32[]{:S(2)}) async-start(s8[5767168]{0:T(1024)(128)(4,1)} %bitcast.76), calls=%async_computation.2 | async-start | bytes 8388608
  238.0 6.6 %copy-start.15 = (bf16[512,2048]{1,0:T(8,128)(2,1)S(1)}, bf16[512,2048]{1,0:T(8,128)(2,1)}, u32[]{:S(2)}) copy-start(bf16[512,2048]{1,0:T(8,128)(2,1)} %get-tuple-element.41) | copy-start | bytes 6291460
  238.1 7.1 %slice-start.3 = ((s8[5767168]{0:T(1024)(128)(4,1)}), s8[1572864]{0:T(1024)(128)(4,1)S(1)}, s32[]{:S(2)}) async-start(s8[5767168]{0:T(1024)(128)(4,1)} %bitcast.76), calls=%async_computation.3 | async-start | bytes 3145728
  245.0 3.6 slice-start.4
  245.1 16.1 %copy-start.9 = (bf16[512,2048]{1,0:T(8,128)(2,1)}, bf16[512,2048]{1,0:T(8,128)(2,1)S(1)}, u32[]{:S(2)}) copy-start(bf16[512,2048]{1,0:T(8,128)(2,1)S(1)} %dynamic-slice_dynamic-update-slice_fusion) | copy-start | bytes 6291460
  245.1 3.5 slice-start.5
  245.1 7.8 %slice-start = ((s8[5767168]{0:T(1024)(128)(4,1)}), s8[4194304]{0:T(1024)(128)(4,1)S(1)}, s32[]{:S(2)}) async-start(s8[5767168]{0:T(1024)(128)(4,1)} %bitcast.74), calls=%async_computation | async-start | bytes 8388608
  248.6 4.4 slice-start.1
  252.9 3.5 copy-start.39
  253.0 3.5 copy-start.37
  253.0 8.2 %copy-start.41 = (bf16[512,1408]{1,0:T(8,128)(2,1)}, bf16[512,1408]{1,0:T(8,128)(2,1)S(1)}, u32[]{:S(2)}) copy-start(bf16[512,1408]{1,0:T(8,128)(2,1)S(1)} %get-tuple-element.100) | copy-start | bytes 4325380
  348.5 3.1 copy-start.3
  351.6 2.8 copy-start.4
  351.6 2.9 copy-start.10
  354.5 2.3 copy-start.7
  354.5 2.3 copy-start.18
  356.8 1.9 copy-start
  358.7 9.9 %copy-start.6 = (bf16[512,512]{1,0:T(8,128)(2,1)}, bf16[512,512]{1,0:T(8,128)(2,1)S(1)}, u32[]{:S(2)}) copy-start(bf16[512,512]{1,0:T(8,128)(2,1)S(1)} %get-tuple-element.134) | copy-start | bytes 1572868
  360.7 8.0 %copy-start.14 = (bf16[512,2048]{1,0:T(8,128)(2,1)S(1)}, bf16[512,2048]{1,0:T(8,128)(2,1)}, u32[]{:S(2)}) copy-start(bf16[512,2048]{1,0:T(8,128)(2,1)} %copy-done.13) | copy-start | bytes 6291460
  360.7 8.0 %copy-start.40 = (bf16[512,1408]{1,0:T(8,128)(2,1)S(1)}, bf16[512,1408]{1,0:T(8,128)(2,1)}, u32[]{:S(2)}) copy-start(bf16[512,1408]{1,0:T(8,128)(2,1)} %copy-done.39) | copy-start | bytes 4325380
  368.6 5.3 copy-start.38
  448.8 2.5 copy-start.26
  448.9 3.4 copy-start.28
  448.9 3.4 copy-start.34
  451.3 0.8 copy-start.30
  455.2 1.0 copy-start.12
  457.0 1.7 copy-start.32
  458.7 5.4 copy-start.23
  464.1 3.6 copy-start.1
  464.1 3.6 copy-start.17
  545.8 1.2 copy-start.8
  547.3 2.7 copy-start.25
  549.1 0.8 copy-start.29
  550.2 5.3 copy-start.24
  550.4 5.9 %copy-start.21 = (f32[256,1408]{1,0:T(8,128)S(1)}, f32[256,1408]{1,0:T(8,128)}, u32[]{:S(2)}) copy-start(f32[256,1408]{1,0:T(8,128)} %get-tuple-element.159) | copy-start | bytes 4325380
  555.5 1.9 copy-start.20
  557.4 1.9 copy-start.19

commit v2 on v1

--- a/solution.py
+++ b/solution.py
@@ -473,6 +473,10 @@
         c = 1 - self.c if i & 1 else self.c
         return {"fsdp": y, "blk": x * 2 + c}
 
+    def number(self, i):
+        at = self.plane(i)
+        return at["fsdp"] * 4 + at["blk"]
+
     def up(self):
         return {"head": self.z + 1}
 
@@ -603,42 +607,50 @@
     half = rows // 2
 
     def block(i):
-        return dst.at[pl.ds(i * rows, rows)]
+        return dst.at[pl.ds(pl.multiple_of(me.number(i) * rows, rows), rows)]
 
     def part(i, h):
-        return dst.at[pl.ds(i * rows + h * half, half)]
+        return dst.at[pl.ds(pl.multiple_of(me.number(i) * rows + h * half, half), half)]
 
     if begin:
         yield begin
-    to_x = me.copy(src, block(2), me.plane(2))
-    to_y = me.copy(src, block(4), me.plane(4))
-    to_c = me.copy(src, block(1), me.plane(1))
+    heads = src.at[pl.ds(0, half)], src.at[pl.ds(half, half)]
+    x_in, y_in = [], []
+    for h in (0, 1):
+        x_in.append(me.copy(heads[h], part(0, h), me.plane(2)))
+        x_in[h].start()
+        y_in.append(me.copy(heads[1 - h], part(0, 1 - h), me.plane(4)))
+        y_in[h].start()
+    to_c = me.copy(src, block(0), me.plane(1))
     own = me.local(src, block(0))
-    for copy in (to_x, to_y, to_c, own):
-        copy.start()
+    to_c.start()
+    own.start()
+    yield begin + unit * 0.5
+    x_in[0].wait_recv()
+    x_on = me.copy(part(2, 0), part(2, 0), me.plane(4))
+    x_on.start()
+    y_in[0].wait_recv()
+    y_on = me.copy(part(4, 1), part(4, 1), me.plane(2))
+    y_on.start()
     yield begin + unit
-    to_x.wait_recv()
-    x_on = me.copy(part(2, 0), part(6, 0), me.plane(4))
-    x_core = me.copy(block(2), block(3), me.plane(1))
-    x_on.start()
+    x_in[1].wait_recv()
+    x_core = me.copy(block(2), block(2), me.plane(1))
     x_core.start()
-    to_y.wait_recv()
-    y_on = me.copy(part(4, 1), part(6, 1), me.plane(2))
-    y_core = me.copy(block(4), block(5), me.plane(1))
-    y_on.start()
+    y_in[1].wait_recv()
+    y_core = me.copy(block(4), block(4), me.plane(1))
     y_core.start()
     yield begin + unit * 1.5
     x_on.wait_recv()
-    d0_core = me.copy(part(6, 0), part(7, 0), me.plane(1))
+    d0_core = me.copy(part(6, 0), part(6, 0), me.plane(1))
     d0_core.start()
     y_on.wait_recv()
-    d1_core = me.copy(part(6, 1), part(7, 1), me.plane(1))
+    d1_core = me.copy(part(6, 1), part(6, 1), me.plane(1))
     d1_core.start()
-    yield begin + unit * 1.7
+    yield begin + unit * 1.5 + 2.0
     own.wait()
     for copy in (to_c, x_core, y_core, d0_core, d1_core):
         copy.wait_recv()
-    for copy in (to_x, to_y, to_c, x_on, x_core, y_on, y_core, d0_core, d1_core):
+    for copy in (*x_in, *y_in, to_c, x_on, x_core, y_on, y_core, d0_core, d1_core):
         copy.wait_send()
 
 
@@ -729,45 +741,55 @@
     def at(ref, j):
         return ref.at[pl.ds(j * rows, rows)]
 
-    if begin:
-        yield begin
-
-    @pl.when(z == 0)
-    def _():
-        for j in (3, 2, 1):
-            me.again(ups[j], at(part, j), at(from_below, j), me.up()).start()
-
-    @pl.when(z == 3)
-    def _():
-        for j in (0, 1, 2):
-            me.again(downs[j], at(part, j), at(from_above, j), me.down()).start()
-
-    for step, j in enumerate((3, 2)):
-        for stop in range(1, j):
-            yield begin + unit * (3 - j + stop) + 1.0
-
-            @pl.when(z == stop)
-            def _():
-                me.again(ups[j], at(part, j), at(from_below, j), me.up()).wait_recv()
-                add_rows(at(sums_up, j), at(part, j), at(from_below, j))
-                me.again(ups[j], at(sums_up, j), at(from_below, j), me.up()).start()
-
-            @pl.when(z == 3 - stop)
-            def _():
-                i = 3 - j
-                me.again(downs[i], at(part, i), at(from_above, i), me.down()).wait_recv()
-                add_rows(at(sums_down, i), at(part, i), at(from_above, i))
-                me.again(downs[i], at(sums_down, i), at(from_above, i), me.down()).start()
-
+    def up(j, source):
+        return me.again(ups[j], at(source, j), at(from_below, j), me.up())
+
+    def down(j, source):
+        return me.again(downs[j], at(source, j), at(from_above, j), me.down())
+
+    def start(j):
+        @pl.when(z == 0)
+        def _():
+            up(j, part).start()
+
+        @pl.when(z == 3)
+        def _():
+            down(3 - j, part).start()
+
+    def relay(j, stop):
+        @pl.when(z == stop)
+        def _():
+            up(j, part).wait_recv()
+            add_rows(at(sums_up, j), at(part, j), at(from_below, j))
+            up(j, sums_up).start()
+
+        @pl.when(z == 3 - stop)
+        def _():
+            i = 3 - j
+            down(i, part).wait_recv()
+            add_rows(at(sums_down, i), at(part, i), at(from_above, i))
+            down(i, sums_down).start()
+
+    yield begin
+    start(3)
+    yield begin + unit * 0.6
+    start(2)
+    yield begin + unit + 1.0
+    relay(3, 1)
+    yield begin + unit * 1.6
+    start(1)
+    yield begin + unit * 2 + 1.0
+    relay(3, 2)
+    relay(2, 1)
     yield begin + unit * 3 + 1.5
     for j in range(4):
 
         @pl.when(z == j)
         def _():
             if j > 0:
-                me.again(ups[j], at(part, j), at(from_below, j), me.up()).wait_recv()
+                up(j, part).wait_recv()
             if j < 3:
-                me.again(downs[j], at(part, j), at(from_above, j), me.down()).wait_recv()
+                down(j, part).wait_recv()
 
             def body(i, _):
                 span = pl.ds(pl.multiple_of(i * 32, 32), 32)
@@ -783,9 +805,9 @@
             lax.fori_loop(0, rows // 32, body, 0)
             for i in range(4):
                 if i > j:
-                    me.again(ups[i], at(part, i), at(from_below, i), me.up()).wait_send()
+                    up(i, part).wait_send()
                 if i < j:
-                    me.again(downs[i], at(part, i), at(from_above, i), me.down()).wait_send()
+                    down(i, part).wait_send()
 
 
 def plane_scatter_scratch(rows, cols):
@@ -806,7 +828,7 @@
     half = rows // 2
 
     def block(i):
-        return src.at[pl.ds(i * rows, rows)]
+        return src.at[pl.ds(pl.multiple_of(me.number(i) * rows, rows), rows)]
 
     first, second = pl.ds(0, half), pl.ds(half, half)
     if begin:
@@ -876,34 +898,101 @@
     return jax.ShapeDtypeStruct(dims, kind)
 
 
-def first_kernel(tok, wqkv, gains, wo, wg, tok_all, wqkv_all, gains_all, wo_all, wg_all, ss, rs):
+def first_kernel(tok, wqkv, gains, tok_all, wqkv_all, gains_all, ss, rs):
     me = Here(ss, rs)
     me.enter((1, 2, 4))
     drive(
         z_gather(me, tok, tok_all, 11.3),
+        plane_gather(me, gains, gains_all, 2.0),
         plane_gather(me, wqkv, wqkv_all, 7.0),
-        plane_gather(me, gains, gains_all, 7.1),
-        plane_gather(me, wo, wo_all, 12.0, 0.1),
-        plane_gather(me, wg, wg_all, 27.0, 0.2),
-    )
-
-
-def first(tok, wqkv, gains, wo, wg):
+    )
+
+
+def first(tok, wqkv, gains):
     def grown(a, n):
         return shape((a.shape[0] * n,) + a.shape[1:])
 
     return pl.pallas_call(
         first_kernel,
-        out_shape=(grown(tok, 4), grown(wqkv, 8), grown(gains, 8), grown(wo, 8), grown(wg, 8)),
-        in_specs=[VM] * 5,
-        out_specs=[HB] * 5,
+        out_shape=(grown(tok, 4), grown(wqkv, 8), grown(gains, 8)),
+        in_specs=[VM] * 3,
+        out_specs=[HB] * 3,
         scratch_shapes=dma_sems(64),
         compiler_params=params(1),
         name="gather_first",
-    )(tok, wqkv, gains, wo, wg)
-
-
-def attention_forward(me, q_t, kv_own, kv, v_t, key_pos, query_pos, out_t, log_sum, kv_all, per):
+    )(tok, wqkv, gains)
+
+
+def alone(flops, vmem=60 * 2**20):
+    return dict(
+        compiler_params=pltpu.CompilerParams(vmem_limit_bytes=vmem),
+        cost_estimate=pl.CostEstimate(flops=int(flops), bytes_accessed=2**23, transcendentals=0),
+    )
+
+
+def gain_row(gains, which):
+    return jnp.concatenate(
+        [gains[i * 32 : i * 32 + 16, :].astype(f32)[which : which + 1] for i in range(8)], axis=1
+    )
+
+
+def rotate_heads(values, cos, sin, inverse=False):
+    out = []
+    for h in range(values.shape[0] // HD):
+        a = values[h * HD : h * HD + HD // 2]
+        b = values[h * HD + HD // 2 : (h + 1) * HD]
+        if inverse:
+            out += [a * cos + b * sin, b * cos - a * sin]
+        else:
+            out += [a * cos - b * sin, b * cos + a * sin]
+    return jnp.concatenate(out, axis=0)
+
+
+def project_kernel(tok, wqkv, gains, cos_t, sin_t, normed, q_t, q_n, kv_own):
+    heads = q_t.shape[0]
+    wide = heads * HD
+    gain = gain_row(gains, 0)
+
+    def body(i, _):
+        at = pl.ds(pl.multiple_of(i * 128, 128), 128)
+        x = tok[at, :].astype(f32)
+        inv = lax.rsqrt(jnp.mean(x * x, axis=1, keepdims=True) + norm_epsilon)
+        low = (x * inv * gain).astype(bf16)
+        normed[at, :] = low
+        lin = jnp.dot(low, wqkv[...], preferred_element_type=f32).T
+        cos, sin = cos_t[:, at], sin_t[:, at]
+        turned = rotate_heads(lin[: wide + HD], cos, sin)
+        query = turned[:wide].astype(bf16) * bf16(1.0 / math.sqrt(HD))
+        for h in range(heads):
+            q_t[h, :, at] = query[h * HD : (h + 1) * HD]
+        natural = query.astype(f32).T
+        for h in range(heads):
+            q_n[h, at, :] = natural[:, h * HD : (h + 1) * HD].astype(bf16)
+        kv_own[at, :] = jnp.concatenate([turned[wide:], lin[wide + HD :]], axis=0).T.astype(bf16)
+        return 0
+
+    lax.fori_loop(0, tok.shape[0] // 128, body, 0)
+
+
+def project(tok, wqkv, gains, cos_t, sin_t):
+    rows = tok.shape[0]
+    heads = (wqkv.shape[1] - 2 * HD) // HD
+    return pl.pallas_call(
+        project_kernel,
+        out_shape=(
+            shape(tok.shape),
+            shape((heads, HD, rows)),
+            shape((heads, rows, HD)),
+            shape((rows, 2 * HD)),
+        ),
+        in_specs=[VM] * 5,
+        out_specs=[VM] * 4,
+        name="project",
+        **alone(2 * rows * wqkv.shape[0] * wqkv.shape[1]),
+    )(tok, wqkv, gains, cos_t, sin_t)
+
+
+def attention_forward(me, q_t, kv_own, kv, v_t, key_pos, query_pos, out_t, attended, log_sum, kv_all, per):
     heads, hd, rows = q_t.shape
     blocks = kv.shape[0] // rows
 
@@ -924,7 +1013,7 @@
     for i in range(blocks):
         v_t[:, i * rows : (i + 1) * rows] = kv[i * rows : (i + 1) * rows, :].astype(f32).T[hd:, :].astype(bf16)
 
-    def head(h, _):
+    def one_head(h):
         q = q_t[h]
         limit = query_pos[0:1, :]
 
@@ -952,93 +1041,239 @@
                 jnp.zeros((hd, rows), f32),
             ),
         )
-        out_t[h] = acc / total
+        acc = acc / total
+        out_t[h] = acc
         log_sum[h] = top + jnp.log(total)
-        return 0
+        return acc
 
     for h in range(0, heads, 2):
         yield 6.0 + per * h
-        lax.fori_loop(h, h + 2, head, 0)
+        pair = jnp.concatenate([one_head(h), one_head(h + 1)], axis=0)
+        attended[:, h * hd : (h + 2) * hd] = pair.T.astype(bf16)
     yield 6.0 + per * heads
     save.wait()
     for copy in copies:
         copy.wait_send()
 
 
-def second_kernel(q_t, kv_own, key_pos, query_pos, cot, wu, out_t, log_sum, kv_all, cot_all, wu_all, kv, v_t, ss, rs):
+def second_kernel(
+    q_t, kv_own, key_pos, query_pos, cot, wo, wu,
+    out_t, attended, log_sum, kv_all, cot_all, wo_all, wu_all, kv, v_t, ss, rs
+):
     me = Here(ss, rs)
     me.enter((1, 2, 3, 4))
     drive(
-        attention_forward(me, q_t, kv_own, kv, v_t, key_pos, query_pos, out_t, log_sum, kv_all, 3.5),
+        attention_forward(
+            me, q_t, kv_own, kv, v_t, key_pos, query_pos, out_t, attended, log_sum, kv_all, 4.0
+        ),
         z_gather(me, cot, cot_all, 11.3, 0.1),
-        plane_gather(me, wu, wu_all, 15.5, 0.3),
-    )
-
-
-def second(q_t, kv_own, key_pos, query_pos, cot, wu):
+        plane_gather(me, wo, wo_all, 6.0, 0.3),
+        plane_gather(me, wu, wu_all, 15.5, 6.0),
+    )
+
+
+def second(q_t, kv_own, key_pos, query_pos, cot, wo, wu):
     heads, hd, rows = q_t.shape
     keys = key_pos.shape[0]
     return pl.pallas_call(
         second_kernel,
         out_shape=(
             shape((heads, hd, rows), f32),
+            shape((rows, heads * hd)),
             shape((heads, 1, rows), f32),
             shape((keys, 2 * hd)),
             shape((cot.shape[0] * 4, cot.shape[1])),
+            shape((wo.shape[0] * 8, wo.shape[1])),
             shape((wu.shape[0] * 8, wu.shape[1])),
         ),
-        in_specs=[VM] * 6,
-        out_specs=[VM, VM, HB, HB, HB],
-        scratch_shapes=[pltpu.VMEM((keys, 2 * hd), bf16), pltpu.VMEM((hd, keys), bf16)] + dma_sems(32),
+        in_specs=[VM] * 7,
+        out_specs=[VM] * 3 + [HB] * 4,
+        scratch_shapes=[pltpu.VMEM((keys, 2 * hd), bf16), pltpu.VMEM((hd, keys), bf16)] + dma_sems(64),
         compiler_params=params(2),
         name="attention_forward",
-    )(q_t, kv_own, key_pos, query_pos, cot, wu)
-
-
-def third_kernel(part, wd, total_out, wd_all, total, inbox, across, partial, ss, rs):
+    )(q_t, kv_own, key_pos, query_pos, cot, wo, wu)
+
+
+def third_kernel(part, wg, wd, total_out, wg_all, wd_all, total, inbox, across, partial, ss, rs):
     me = Here(ss, rs)
     me.enter((1, 2, 4))
     drive(
-        z_reduce_all(me, part, total, inbox, across, partial, total_out, 45.0),
-        plane_gather(me, wd, wd_all, 15.5, 0.1),
-    )
-
-
-def third(part, wd):
+        z_reduce_all(me, part, total, inbox, across, partial, total_out, 45.0, 16),
+        plane_gather(me, wg, wg_all, 15.5, 0.1),
+        plane_gather(me, wd, wd_all, 15.5, 15.0),
+    )
+
+
+def third(part, wg, wd):
     rows = pltpu.VMEM(part.shape, bf16)
+
+    def grown(a):
+        return shape((a.shape[0] * 8, a.shape[1]))
+
     return pl.pallas_call(
         third_kernel,
-        out_shape=(shape(part.shape), shape((wd.shape[0] * 8, wd.shape[1]))),
-        in_specs=[VM] * 2,
-        out_specs=[HB] * 2,
-        scratch_shapes=[rows] * 4 + dma_sems(64),
+        out_shape=(shape(part.shape), grown(wg), grown(wd)),
+        in_specs=[VM] * 3,
+        out_specs=[HB] * 3,
+        scratch_shapes=[rows] * 4 + dma_sems(96),
         compiler_params=params(3),
         name="sum_branch",
-    )(part, wd)
-
-
-def fourth_kernel(part, dwd, total_out, dwd_own, total, inbox, across, partial, *rest):
+    )(part, wg, wd)
+
+
+def contract_rows(left, right):
+    return lax.dot_general(left, right, (((0,), (0,)), ((), ())), preferred_element_type=f32)
+
+
+def contract_last_dims(left, right):
+    return lax.dot_general(left, right, (((1,), (1,)), ((), ())), preferred_element_type=f32)
+
+
+def fourth_kernel(
+    part, cot_all, hidden, normed_two, d_gate, d_up, wd_all,
+    total_out, dwd_own, dwg, dwu, out_part,
+    total, inbox, across, partial, left_a, left_b, right_a, right_b, right_c, wd, dwd, stage, *rest
+):
     *scratch, ss, rs = rest
     me = Here(ss, rs)
     me.enter((1, 2, 4))
+    blocks = left_a.shape[1] // 256
+    pairs = ((cot_all, left_a), (hidden, right_a), (normed_two, left_b), (d_gate, right_b), (d_up, right_c), (wd_all, wd))
+    loads = [me.local(src, dst) for src, dst in pairs]
+
+    def block(ref, i):
+        return ref[:, i * 256 : (i + 1) * 256]
+
+    def down():
+        yield 0.2
+        for load in loads:
+            load.start()
+        loads[0].wait()
+        loads[1].wait()
+        for i in range(blocks):
+            yield 2.5 + i
+            dwd[i * 256 : (i + 1) * 256, :] = contract_rows(block(left_a, i), right_a[...]).astype(bf16)
+        yield from plane_scatter(me, dwd, dwd_own, scratch, 15.5, 2.6 + blocks)
+
+    puts = [me.slot(), me.slot()]
+    busy = [None, None]
+
+    def put(n, value, dst):
+        k = n % 2
+        if busy[k] is not None:
+            busy[k].wait()
+        view = stage.at[k, pl.ds(0, value.shape[0]), pl.ds(0, value.shape[1])]
+        stage[k, : value.shape[0], : value.shape[1]] = value.astype(bf16)
+        busy[k] = pltpu.make_async_copy(view, dst, me.send_sem.at[puts[k]])
+        busy[k].start()
+
+    def others():
+        n = 0
+        yield 11.0
+        loads[2].wait()
+        for load, right, dst in ((loads[3], right_b, dwg), (loads[4], right_c, dwu)):
+            load.wait()
+            for i in range(blocks):
+                yield 12.0 + n
+                value = contract_rows(block(left_b, i), right[...])
+                put(n, value, dst.at[pl.ds(i * 256, 256)])
+                n += 1
+        loads[5].wait()
+        for i in range(hidden.shape[0] // 128):
+            for h in (0, 1):
+                yield 12.0 + n
+                at = slice(i * 128, (i + 1) * 128)
+                half = wd.shape[0] // 2
+                value = contract_last_dims(right_a[at, :], wd[h * half : (h + 1) * half, :])
+                put(n, value, out_part.at[pl.ds(i * 128, 128), pl.ds(h * half, half)])
+                n += 1
+        for copy in busy:
+            copy.wait()
+
     drive(
-        z_reduce_all(me, part, total, inbox, across, partial, total_out, 45.0),
-        plane_scatter(me, dwd, dwd_own, scratch, 15.5, 0.1),
-    )
-
-
-def fourth(part, dwd):
+        z_reduce_all(me, part, total, inbox, across, partial, total_out, 45.0, 16),
+        down(),
+        others(),
+    )
+
+
+def fourth(part, cot_all, hidden, normed_two, d_gate, d_up, wd_all):
     rows = pltpu.VMEM(part.shape, bf16)
-    own = (dwd.shape[0] // 8, dwd.shape[1])
+    units = pltpu.VMEM(hidden.shape, bf16)
+    weight = pltpu.VMEM(wd_all.shape, bf16)
+    own = (wd_all.shape[0] // 8, wd_all.shape[1])
     return pl.pallas_call(
         fourth_kernel,
-        out_shape=(shape(part.shape), shape(own, f32)),
-        in_specs=[VM, HB],
-        out_specs=[HB, VM],
-        scratch_shapes=[rows] * 4 + plane_scatter_scratch(*own) + dma_sems(64),
-        compiler_params=params(4),
+        out_shape=(
+            shape(part.shape), shape(own, f32), shape(wd_all.shape), shape(wd_all.shape), shape(part.shape)
+        ),
+        in_specs=[VM] + [HB] * 6,
+        out_specs=[HB, VM, HB, HB, HB],
+        scratch_shapes=[rows] * 6 + [units] * 3 + [weight] * 2
+        + [pltpu.VMEM((2, 256, max(own[1], wd_all.shape[0] // 2)), bf16)]
+        + plane_scatter_scratch(*own) + dma_sems(128),
+        compiler_params=params(4, 63 * 2**20),
         name="sum_grad_normed_two",
-    )(part, dwd)
+    )(part, cot_all, hidden, normed_two, d_gate, d_up, wd_all)
+
+
+def prepare_kernel(cot, tok, branch, grad_two, gains, wo, out_t, attended, g_t, g_n, delta, own, gain_part, dwo, low):
+    heads = g_t.shape[0]
+    gain = gain_row(gains, 1)
+    z = lax.axis_index("head")
+
+    def body(i, _):
+        at = pl.ds(pl.multiple_of(i * 128, 128), 128)
+        h = tok[at, :].astype(f32) + branch[at, :].astype(f32)
+        e = grad_two[at, :].astype(f32)
+        inv = lax.rsqrt(jnp.mean(h * h, axis=1, keepdims=True) + norm_epsilon)
+        u = e * gain
+        inner = jnp.mean(u * h, axis=1, keepdims=True)
+        grad = cot[at, :].astype(f32) + (inv * u - h * (inv * inv * inv * inner))
+
+        @pl.when(i == z)
+        def _():
+            own[...] = grad
+            gain_part[...] = jnp.broadcast_to(
+                jnp.sum(e * h * inv, axis=0, keepdims=True), gain_part.shape
+            )
+
+        small = grad.astype(bf16)
+        low[at, :] = small
+        g = jnp.dot(small, wo[...], preferred_element_type=f32).astype(bf16)
+        turned = g.astype(f32).T
+        for head in range(heads):
+            g_n[head, at, :] = g[:, head * HD : (head + 1) * HD]
+            mine = turned[head * HD : (head + 1) * HD]
+            g_t[head, :, at] = mine.astype(bf16)
+            delta[head, :, at] = jnp.sum(mine * out_t[head, :, at], axis=0, keepdims=True)
+        return 0
+
+    lax.fori_loop(0, tok.shape[0] // 128, body, 0)
+    for i in range(dwo.shape[0] // 256):
+        span = slice(i * 256, (i + 1) * 256)
+        dwo[span, :] = contract_rows(low[:, span], attended[...]).astype(bf16)
+
+
+def prepare(cot, tok, branch, grad_two, gains, wo, out_t, attended):
+    heads, hd, rows = out_t.shape
+    width = tok.shape[1]
+    return pl.pallas_call(
+        prepare_kernel,
+        out_shape=(
+            shape((heads, hd, rows)),
+            shape((heads, rows, hd)),
+            shape((heads, 1, rows), f32),
+            shape((rows // 4, width), f32),
+            shape((8, width), f32),
+            shape(wo.shape),
+        ),
+        in_specs=[VM] * 8,
+        out_specs=[VM] * 6,
+        scratch_shapes=[pltpu.VMEM(tok.shape, bf16)],
+        name="prepare_backward",
+        **alone(4 * rows * width * heads * hd),
+    )(cot, tok, branch, grad_two, gains, wo, out_t, attended)
 
 
 def attention_backward(me, q_t, q_n, g_t, g_n, kv_all, log_sum, delta, key_pos, query_pos, dq_t, dkv_own, kv, k_t, dk, dv, dkv, came, per):
@@ -1147,13 +1382,57 @@
     )(q_t, q_n, g_t, g_n, kv_all, log_sum, delta, key_pos, query_pos, out_part, dwg, dwu)
 
 
+def finish_kernel(dq_t, dkv, cos_t, sin_t, wqkv, normed, tok, gain_two, one_part, dwqkv, gain_parts, lin):
+    heads = dq_t.shape[0]
+    wide = heads * HD
+    width = tok.shape[1]
+    cols = width // 8
+
+    def body(i, total):
+        at = pl.ds(pl.multiple_of(i * 128, 128), 128)
+        cos, sin = cos_t[:, at], sin_t[:, at]
+        kv = dkv[at, :].astype(bf16).astype(f32).T
+        grads = jnp.concatenate([dq_t[h, :, at].astype(f32) for h in range(heads)] + [kv[:HD]], axis=0)
+        grads = rotate_heads(grads, cos, sin, inverse=True)
+        natural = jnp.concatenate([grads, kv[HD:]], axis=0).T.astype(bf16)
+        lin[at, :] = natural
+        one = contract_last_dims(natural, wqkv[...])
+        one_part[at, :] = one.astype(bf16)
+        x = tok[at, :].astype(f32)
+        inv = lax.rsqrt(jnp.mean(x * x, axis=1, keepdims=True) + norm_epsilon)
+        return total + jnp.sum(one * x * inv, axis=0, keepdims=True)
+
+    total = lax.fori_loop(0, tok.shape[0] // 128, body, jnp.zeros((1, width), f32))
+    for i in range(8):
+        span = slice(i * cols, (i + 1) * cols)
+        gain_parts[i * 8 : (i + 1) * 8, :] = jnp.concatenate(
+            [total[:, span], gain_two[0:1, span], jnp.zeros((6, cols), f32)], axis=0
+        )
+        dwqkv[span, :] = contract_rows(normed[:, span], lin[...]).astype(bf16)
+
+
+def finish(dq_t, dkv, cos_t, sin_t, wqkv, normed, tok, gain_two):
+    width = tok.shape[1]
+    return pl.pallas_call(
+        finish_kernel,
+        out_shape=(shape(tok.shape), shape(wqkv.shape), shape((64, width // 8), f32)),
+        in_specs=[VM] * 8,
+        out_specs=[VM] * 3,
+        scratch_shapes=[pltpu.VMEM((tok.shape[0], wqkv.shape[1]), bf16)],
+        name="finish_attention",
+        **alone(4 * tok.shape[0] * width * wqkv.shape[1]),
+    )(dq_t, dkv, cos_t, sin_t, wqkv, normed, tok, gain_two)
+
+
 def gain_sums(me, src, out, came, mine, came_z):
-    n = src.shape[0] // 8
-    copies = [me.copy(src.at[pl.ds(i * 8, 8)], came.at[i - 1], me.plane(i)) for i in range(1, n)]
+    def block(i):
+        return pl.ds(pl.multiple_of(me.number(i) * 8, 8), 8)
+
+    copies = [me.copy(src.at[block(i)], came.at[i - 1], me.plane(i)) for i in range(1, 8)]
     for copy in copies:
         copy.start()
     yield 4.0
-    value = src[0:8, :]
+    value = src[block(0), :]
     for i, copy in enumerate(copies):
         copy.wait_recv()
         value = value + came[i]
@@ -1163,7 +1442,7 @@
     ]
     for copy in again:
         copy.start()
-    yield 8.0
+    yield 20.0
     for d, copy in enumerate(again):
         copy.wait_recv()
         value = value + came_z[d]
@@ -1191,7 +1470,7 @@
         ]
         for copy in copies:
             copy.start()
-        yield 30.0
+        yield 37.0
         for copy in copies:
             copy.wait_recv()
         dwkv_all[0] = dwkv_own[...]
@@ -1245,25 +1524,13 @@
 ):
     row_count, width = tokens.shape
     groups = 4
-    heads = H // groups
     head_rows = row_count * groups
     stretch_rows = head_rows // 2
     cols = width // 8
     contract_last = (((1,), (1,)), ((), ()))
-    contract_first = (((0,), (0,)), ((), ()))
     z = lax.axis_index("head")
     b = lax.axis_index("blk")
-    place = lax.axis_index("fsdp") * 4 + b
     own_first = z * row_count
-
-    def turn(values):
-        return jnp.concatenate(
-            [
-                lax.dynamic_slice_in_dim(values, jnp.bitwise_xor(place, i) * cols, cols, values.ndim - 1)
-                for i in range(8)
-            ],
-            axis=-1,
-        )
 
     def own_rows(values):
         return lax.dynamic_slice_in_dim(values, own_first, row_count, 0)
@@ -1277,16 +1544,10 @@
     )
     key_pos = jnp.broadcast_to(key_positions[:, None], (key_positions.shape[0], 128))
     query_pos = jnp.broadcast_to(query_positions[None, :], (8, head_rows))
-    cos_rows, sin_rows = rope_tables(query_positions, HD)
-    cos_t, sin_t = cos_rows.T, sin_rows.T
-
-    def rotate_t(values):
-        a, c = values[..., : HD // 2, :], values[..., HD // 2 :, :]
-        return jnp.concatenate([a * cos_t - c * sin_t, c * cos_t + a * sin_t], axis=-2)
-
-    def unrotate_t(values):
-        a, c = values[..., : HD // 2, :], values[..., HD // 2 :, :]
-        return jnp.concatenate([a * cos_t + c * sin_t, c * cos_t - a * sin_t], axis=-2)
+    half = HD // 2
+    frequency = rope_base ** (-(jnp.arange(half, dtype=f32) * (2.0 / HD)))
+    angles = frequency[:, None] * query_positions.astype(f32)[None, :]
+    cos_t, sin_t = jnp.cos(angles), jnp.sin(angles)
 
     slot_first = z * HD
     w_qkv = jnp.concatenate(
@@ -1298,28 +1559,18 @@
         axis=1,
     )
     gains = jnp.concatenate([gain_attn[None], gain_mlp[None], jnp.zeros((30, cols), bf16)])
-    tok_all, wqkv_all, gains_all, wo_all, wg_all = first(tokens, w_qkv, gains, w_out, w_gate)
-    gains_all = gains_all.reshape(8, 32, cols)
-    gain_one = gains_all[:, 0].reshape(width).astype(f32)
-    gain_two = gains_all[:, 1].reshape(width).astype(f32)
-
-    x_rows = turn(tok_all).astype(f32)
-    inv_attn = lax.rsqrt(jnp.mean(x_rows * x_rows, axis=-1, keepdims=True) + norm_epsilon)
-    normed = (x_rows * inv_attn * gain_one).astype(bf16)
-    qkv_t = lax.dot_general(wqkv_all, normed, (((0,), (1,)), ((), ())), preferred_element_type=f32)
-    wide = heads * HD
-    q_t = rotate_t(qkv_t[:wide].reshape(heads, HD, head_rows)).astype(bf16) * bf16(1.0 / math.sqrt(HD))
-    k_t = rotate_t(qkv_t[wide : wide + HD]).astype(bf16)
-    v_t = qkv_t[wide + HD :].astype(bf16)
-    kv_own = jnp.concatenate([k_t, v_t], axis=0).T
-    out_t, log_sum, kv_all, cot_all, wu_all = second(q_t, kv_own, key_pos, query_pos, cotangent, w_up)
-    attended_t = out_t.astype(bf16).reshape(wide, head_rows)
-    branch_part = lax.dot_general(
-        attended_t, wo_all, (((0,), (1,)), ((), ())), preferred_element_type=f32
-    ).astype(bf16)
-    branch, wd_all = third(branch_part, w_down)
-
-    hidden_rows = x_rows + branch.astype(f32)
+    tok_all, wqkv_all, gains_all = first(tokens, w_qkv, gains)
+    normed, q_t, q_n, kv_own = project(tok_all, wqkv_all, gains_all, cos_t, sin_t)
+    out_t, attended, log_sum, kv_all, cot_all, wo_all, wu_all = second(
+        q_t, kv_own, key_pos, query_pos, cotangent, w_out, w_up
+    )
+    branch_part = lax.dot_general(attended, wo_all, contract_last, preferred_element_type=f32).astype(bf16)
+    branch, wg_all, wd_all = third(branch_part, w_gate, w_down)
+
+    gain_rows = gains_all.reshape(8, 32, cols)
+    gain_one = gain_rows[:, 0].reshape(width).astype(f32)
+    gain_two = gain_rows[:, 1].reshape(width).astype(f32)
+    hidden_rows = tok_all.astype(f32) + branch.astype(f32)
     inv_mlp = lax.rsqrt(jnp.mean(hidden_rows * hidden_rows, axis=-1, keepdims=True) + norm_epsilon)
     normed_two = (hidden_rows * inv_mlp * gain_two).astype(bf16)
     gate = jnp.dot(normed_two, wg_all, preferred_element_type=f32)
@@ -1327,59 +1578,30 @@
     gate_sigmoid = jax.nn.sigmoid(gate)
     gate_silu = gate * gate_sigmoid
     hidden = (gate_silu * up).astype(bf16)
-    out_part = lax.dot_general(hidden, wd_all, contract_last, preferred_element_type=f32).astype(bf16)
-
-    cot_rows = turn(cot_all)
-    grad_hidden = jnp.dot(cot_rows, wd_all, preferred_element_type=f32)
+    grad_hidden = jnp.dot(cot_all, wd_all, preferred_element_type=f32)
     d_gate = (grad_hidden * up * gate_sigmoid * (1.0 + gate * (1.0 - gate_sigmoid))).astype(bf16)
     d_up = (grad_hidden * gate_silu).astype(bf16)
     two_part = lax.dot_general(d_gate, wg_all, contract_last, preferred_element_type=f32)
     two_part = two_part + lax.dot_general(d_up, wu_all, contract_last, preferred_element_type=f32)
-    dwd = lax.dot_general(cot_rows, hidden, contract_first, preferred_element_type=f32).astype(bf16)
-    dwg = lax.dot_general(normed_two, d_gate, contract_first, preferred_element_type=f32).astype(bf16)
-    dwu = lax.dot_general(normed_two, d_up, contract_first, preferred_element_type=f32).astype(bf16)
-    grad_two, dwd_own = fourth(two_part.astype(bf16), dwd)
-
-    grad_two = grad_two.astype(f32)
-    grad_hidden_rows = cot_rows.astype(f32) + norm_input_grad(hidden_rows, inv_mlp, gain_two, grad_two)
-    grad_low = grad_hidden_rows.astype(bf16)
-    g_t = lax.dot_general(wo_all, grad_low, (((0,), (1,)), ((), ())), preferred_element_type=f32)
-    g_t = g_t.astype(bf16).reshape(heads, HD, head_rows)
-    dwo = lax.dot_general(
-        grad_low, attended_t, (((0,), (1,)), ((), ())), preferred_element_type=f32
-    ).astype(bf16)
-    delta = jnp.sum(g_t.astype(f32) * out_t, axis=1, keepdims=True)
-    q_n = q_t.transpose(0, 2, 1)
-    g_n = g_t.transpose(0, 2, 1)
+    grad_two, dwd_own, dwg, dwu, out_part = fourth(
+        two_part.astype(bf16), cot_all, hidden, normed_two, d_gate, d_up, wd_all
+    )
+
+    g_t, g_n, delta, grad_hidden_own, gain_two_part, dwo = prepare(
+        cot_all, tok_all, branch, grad_two, gains_all, wo_all, out_t, attended
+    )
     dq_t, dkv, out_own, dwg_own, dwu_own = fifth(
         q_t, q_n, g_t, g_n, kv_all, log_sum, delta, key_pos, query_pos, out_part, dwg, dwu
     )
-
-    dkv_t = dkv.T.astype(bf16).astype(f32)
-    dqkv_t = jnp.concatenate(
-        [
-            unrotate_t(dq_t.astype(f32)).reshape(wide, head_rows).astype(bf16),
-            unrotate_t(dkv_t[:HD]).astype(bf16),
-            dkv_t[HD:].astype(bf16),
-        ]
-    )
-    one_part = lax.dot_general(dqkv_t, wqkv_all, (((0,), (1,)), ((), ())), preferred_element_type=f32)
-    dwqkv = lax.dot_general(
-        normed, dqkv_t, (((0,), (1,)), ((), ())), preferred_element_type=f32
-    ).astype(bf16)
-    gain_one_part = jnp.sum(one_part * (x_rows * inv_attn), axis=0).reshape(8, 1, cols)
-    gain_two_part = jnp.sum(
-        own_rows(grad_two) * own_rows(hidden_rows) * own_rows(inv_mlp), axis=0
-    ).reshape(8, 1, cols)
-    gain_parts = jnp.concatenate(
-        [gain_one_part, gain_two_part, jnp.zeros((8, 6, cols), f32)], axis=1
-    ).reshape(64, cols)
-    grad_one, dwq_own, dwkv_all, dwo_own, gain_grads = sixth(one_part.astype(bf16), dwqkv, dwo, gain_parts)
-
-    layer_low = turn((own_rows(hidden_rows) + out_own).astype(bf16))
-    x_own = own_rows(x_rows)
-    grad_tokens = own_rows(grad_hidden_rows) + norm_input_grad(x_own, own_rows(inv_attn), gain_one, grad_one)
-    grad_tokens = turn(grad_tokens.astype(bf16))
+    one_part, dwqkv, gain_parts = finish(
+        dq_t, dkv, cos_t, sin_t, wqkv_all, normed, tok_all, gain_two_part
+    )
+    grad_one, dwq_own, dwkv_all, dwo_own, gain_grads = sixth(one_part, dwqkv, dwo, gain_parts)
+
+    x_own = tokens.astype(f32)
+    layer_low = (x_own + own_rows(branch).astype(f32) + out_own).astype(bf16)
+    inv_own = lax.rsqrt(jnp.mean(x_own * x_own, axis=-1, keepdims=True) + norm_epsilon)
+    grad_tokens = (grad_hidden_own + norm_input_grad(x_own, inv_own, gain_one, grad_one)).astype(bf16)
     slots = jnp.concatenate(
         [lax.dynamic_slice_in_dim(dwkv_all, (z - j) % 4, 1, 0) for j in range(4)], axis=0
     ).astype(f32)

time: 570 us -> 451 us (0.79)
  matrix products: 77 us -> 27 us
  local copies, waits for them, and re-layouts: 46.5 us -> 13.9 us
  other arithmetic: 42.9 us -> 10.6 us
    dot_general x11 -> x2, matrix products: 57.9 us -> 10.3 us  [the longest x1 5.88 us: local_fast(): grad_hidden = jnp.dot(cot_all, wd_all, preferred_element_type=f32)]
    pallas_call x1 -> x4, Pallas kernels: 66.2 us -> 102 us  [the longest x1 71.6 us: third(): pl.pallas_call(third_kernel, out_shape=(shape(part.shape), grown(wg), gro...]
    pallas_call x1, Pallas kernels: 74.6 us -> 45.6 us  [sixth(): pl.pallas_call(sixth_kernel, out_shape=(shape((part.shape[0] // 4, part.s...]
    pallas_call x1, Pallas kernels: 67.3 us -> 44.3 us  [first(): pl.pallas_call(first_kernel, out_shape=(grown(tok, 4), grown(wqkv, 8), gr...]
    unnamed x136 -> x41, local copies, waits for them, and re-layouts: 28.3 us -> 6.63 us
    pallas_call x1, Pallas kernels: 66.2 us -> 73.9 us  [fourth(): pl.pallas_call(fourth_kernel, out_shape=(shape(part.shape), shape(own, f3...]
    another operation x4 -> x0, other arithmetic: 6.69 us -> none
    add x2 -> x0, other arithmetic: 6.68 us -> none  [the longest x1 4.41 us: local_fast(): hidden_rows = x_rows + branch.astype(f32)]
where the time goes in v2:
time: 451 us; the launch traced here: 443 us
  Pallas kernels  390 us (86%)
  matrix products  27 us (6%)
  local copies, waits for them, and re-layouts  13.9 us (3%)
  other arithmetic  10.6 us (2%)
    pallas_call x1, Pallas kernels, fourth(): pl.pallas_call(fourth_kernel, out_shape=(shape(part.shape), shape(own, f3...  73.9 us
    pallas_call x1, Pallas kernels, third(): pl.pallas_call(third_kernel, out_shape=(shape(part.shape), grown(wg), gro...  71.6 us
    pallas_call x1, Pallas kernels, fifth(): pl.pallas_call(fifth_kernel, out_shape=(shape((heads, hd, rows)), shape((...  69.5 us
    pallas_call x1, Pallas kernels, second(): pl.pallas_call(second_kernel, out_shape=(shape((heads, hd, rows), f32), s...  53.8 us
    pallas_call x1, Pallas kernels, sixth(): pl.pallas_call(sixth_kernel, out_shape=(shape((part.shape[0] // 4, part.s...  45.6 us
    pallas_call x1, Pallas kernels, first(): pl.pallas_call(first_kernel, out_shape=(grown(tok, 4), grown(wqkv, 8), gr...  44.3 us
    pallas_call x1, Pallas kernels, prepare(): pl.pallas_call(prepare_kernel, out_shape=(shape((heads, hd, rows)), shape...  12.7 us
    pallas_call x1, Pallas kernels, finish(): pl.pallas_call(finish_kernel, out_shape=(shape(tok.shape), shape(wqkv.sha...  10.7 us

profile of v2, /device:TPU:0, one launch (start us, length us, event | category | flops | bytes accessed | tf_op | source)
XLA Modules:
  0.0 442.5 jit_solution(1044167892024176762)
XLA Ops:
  0.6 1.0 constant_dynamic-slice_fusion.4
  1.6 1.8 pad_maximum_fusion.wqkv
  3.4 0.7 broadcast_in_dim.38
  4.1 0.7 broadcast_in_dim.39
  4.7 0.1 pad.10.clone
  4.8 0.7 maximum_maximum_fusion.gains
  5.5 44.3 %gather_first.1 = (bf16[512,2048]{1,0:T(8,128)(2,1)}, bf16[2048,640]{1,0:T(8,128)(2,1)}, bf16[256,256]{1,0:T(8,128)(2,1)}) custom-call(bf16[128,2048]{1,0:T(8,128)(2,1)} %tok.1, bf16[256,640]{1,0:T(8,128)(2,1)} %pad_maximum_fusion.wqkv, bf16[32,256]{1,0:T(8,128)(2,1)} %maximum_maximum_fusion.gains), custom_call_target="tpu_custom_call" | custom-call | tf_op jit(solution)/shard_map/gather_first/pallas_call | solution.py:915
  49.8 0.8 select_reduce_fusion.2
  50.6 1.0 multiply_sine_fusion
  51.6 7.4 %project.1 = (bf16[512,2048]{1,0:T(8,128)(2,1)}, bf16[8,64,512]{2,1,0:T(8,128)(2,1)}, bf16[8,512,64]{2,1,0:T(8,128)(2,1)}, bf16[512,128]{1,0:T(8,128)(2,1)}) custom-call(bf16[512,2048]{1,0:T(8,128)(2,1)} %get-tuple-element.52.tok, bf16[2048,640]{1,0:T(8,128)(2,1)} %get-tuple-element.53.wqkv, bf16[256,256]{1,0:T(8,128)(2,1)} %get-tuple-element.54.gains, ...), custom_call_target="tpu_custom_call" | custom-call | flops 1342177280 | bytes 8388608 | tf_op jit(solution)/shard_map/project/pallas_call | solution.py:980
  59.0 1.3 broadcast_in_dim.76.key_pos
  60.4 0.6 broadcast_in_dim.77.query_pos
  61.0 53.8 %attention_forward.1 = (f32[8,64,512]{2,1,0:T(8,128)}, bf16[512,512]{1,0:T(8,128)(2,1)}, f32[8,1,512]{2,1,0:T(1,128)}, bf16[2048,128]{1,0:T(8,128)(2,1)}, bf16[5...) custom-call(bf16[8,64,512]{2,1,0:T(8,128)(2,1)} %get-tuple-element.55.q_t, ...), custom_call_target="tpu_custom_call" | custom-call | tf_op jit(solution)/shard_map/attention_forward/pallas_call | solution.py:1078
  114.8 4.4 convolution_convert_fusion.part
  119.2 71.6 %sum_branch.1 = (bf16[512,2048]{1,0:T(8,128)(2,1)}, bf16[2048,1408]{1,0:T(8,128)(2,1)}, bf16[2048,1408]{1,0:T(8,128)(2,1)}) custom-call(bf16[512,2048]{1,0:T(8,128)(2,1)} %convolution_convert_fusion.part, bf16[256,1408]{1,0:T(8,128)(2,1)} %wg.1, bf16[256,1408]{1,0:T(8,128)(2,1)} %wd.1), custom_call_target="tpu_custom_call" | custom-call | tf_op jit(solution)/shard_map/sum_branch/pallas_call | solution.py:1113
  190.8 0.0 copy-done.3
  190.8 0.0 copy-start
  190.8 0.0 copy-start.1
  190.8 5.9 %fusion.30 = f32[512,1408]{1,0:T(8,128)S(1)} fusion(bf16[512,2048]{1,0:T(8,128)(2,1)S(1)} %copy-done.3, bf16[2048,1408]{1,0:T(8,128)(2,1)} %get-tuple-element.62.wd_all), kind=kOutput, calls=%fused_computation.98 | convolution fusion | flops 2952790016 | bytes 10747904 | tf_op jit(solution)/shard_map/dot_general | solution.py:1581
  196.7 0.0 copy-done
  196.7 0.0 copy-done.1
  196.8 0.0 copy-start.14
  196.8 0.8 multiply_reduce_fusion
  197.5 1.1 slice_convert_fusion
  198.7 0.0 slice-start
  198.7 1.1 multiply_convert_fusion.normed_two
  199.7 0.0 copy-start.2
  199.8 0.0 copy-done.14
  199.8 0.0 slice-start.1
  199.8 3.4 fusion.31
  203.2 0.0 copy-done.2
  203.2 0.0 slice-done
  203.2 0.0 slice-done.1
  203.2 5.2 %multiply_convert_fusion.1 = (bf16[512,1408]{1,0:T(8,128)(2,1)}, bf16[512,1408]{1,0:T(8,128)(2,1)S(1)}, bf16[512,1408]{1,0:T(8,128)(2,1)S(1)}) fusion(f32[512,1408]{1,0:T(8,128)S(1)} %fusion.31, f32[512,1408]{1,0:T(8,128)S(1)} %fusion.30, bf16[512,2048]{1,0:T(8,128)(2,1)S(1)} %multiply_convert_fusion.normed_two, bf16[2048,1408]{1,0:T(8,128)(2,1)S(1)} %bitcast.32), kind=kOutput, calls=%fused_computation.5 | convolution fusion | flops 2963603456 | bytes 17956864 | tf_op jit(solution)/shard_map/dot_general | solution.py:1577
  208.4 3.4 fusion.32
  211.9 0.0 copy-done.9
  211.9 0.0 copy-done.10
  211.9 4.7 %add_convert_fusion.part = bf16[512,2048]{1,0:T(8,128)(2,1)} fusion(f32[512,2048]{1,0:T(8,128)S(1)} %fusion.32, bf16[512,1408]{1,0:T(8,128)(2,1)S(1)} %get-tuple-element.125.d_up, bf16[2048,1408]{1,0:T(8,128)(2,1)S(1)} %bitcast.32), kind=kOutput, calls=%fused_computation | convolution fusion | flops 2954887168 | bytes 13500416 | tf_op jit(solution)/shard_map/dot_general | solution.py:1585
  216.6 73.9 %sum_grad_normed_two.1 = (bf16[512,2048]{1,0:T(8,128)(2,1)}, f32[256,1408]{1,0:T(8,128)}, bf16[2048,1408]{1,0:T(8,128)(2,1)}, bf16[2048,1408]{1,0:T(8,128)(2,1)}, bf16[512,2048]{1,0:T(8,128)(2,1)}) custom-call(bf16[512,2048]{1,0:T(8,128)(2,1)} %add_convert_fusion.part, bf16[512,2048]{1,0:T(8,128)(2,1)} %get-tuple-element.61.cot_all.cot, ...), custom_call_target="tpu_custom_call" | custom-call | tf_op jit(solution)/shard_map/sum_grad_normed_two/pallas_call | solution.py:1205
  290.5 12.7 %prepare_backward.1 = (bf16[8,64,512]{2,1,0:T(8,128)(2,1)}, bf16[8,512,64]{2,1,0:T(8,128)(2,1)}, f32[8,1,512]{2,1,0:T(1,128)}, f32[128,2048]{1,0:T(8,128)}, f32[...) custom-call(bf16[512,2048]{1,0:T(8,128)(2,1)} %get-tuple-element.61.cot_all.cot, bf16[512,2048]{1,0:T(8,128)(2,1)} %get-tuple-element.52.tok, ...), custom_call_target="tpu_custom_call" | custom-call | flops 2147483648 | bytes 8388608 | tf_op jit(solution)/shard_map/prepare_backward/pallas_call | solution.py:1261
  303.2 69.5 %attention_backward.1 = (bf16[8,64,512]{2,1,0:T(8,128)(2,1)}, f32[512,128]{1,0:T(8,128)}, f32[128,2048]{1,0:T(8,128)}, f32[256,1408]{1,0:T(8,128)}, f32[256,1408]{1,0:T(8,128)}) custom-call(bf16[8,64,512]{2,1,0:T(8,128)(2,1)} %get-tuple-element.55.q_t, bf16[8,512,64]{2,1,0:T(8,128)(2,1)} %get-tuple-element.60.q_n, ...), custom_call_target="tpu_custom_call" | custom-call | tf_op jit(solution)/shard_map/attention_backward/pallas_call | solution.py:1358
  372.8 10.7 %finish_attention.1 = (bf16[512,2048]{1,0:T(8,128)(2,1)}, bf16[2048,640]{1,0:T(8,128)(2,1)}, f32[64,256]{1,0:T(8,128)}) custom-call(bf16[8,64,512]{2,1,0:T(8,128)(2,1)} %get-tuple-element.77.dq_t, f32[512,128]{1,0:T(8,128)} %get-tuple-element.78.dkv, f32[32,512]{1,0:T(8,128)} %get-tuple-element.139.cos_t, f32[32,512]{1,0:T(8,128)} %get-tuple-element.138.sin_t, ...), custom_call_target="tpu_custom_call" | custom-call | flops 2684354560 | bytes 8388608 | tf_op jit(solution)/shard_map/finish_attention/pallas_call | solution.py:1416
  383.5 45.6 %scatter_last.1 = (f32[128,2048]{1,0:T(8,128)}, f32[256,512]{1,0:T(8,128)}, bf16[4,256,128]{2,1,0:T(8,128)(2,1)}, f32[256,512]{1,0:T(8,128)}, f32[8,256]{1,0:T(8,128)}) custom-call(bf16[512,2048]{1,0:T(8,128)(2,1)} %get-tuple-element.81.part, bf16[2048,640]{1,0:T(8,128)(2,1)} %get-tuple-element.82.dwqkv, bf16[2048,512]{1,0:T(8,128)(2,1)} %get-tuple-element.83.dwo, ...), custom_call_target="tpu_custom_call" | custom-call | tf_op jit(solution)/shard_map/scatter_last/pallas_call | solution.py:1494
  429.1 1.0 constant_dynamic-slice_fusion.3
  430.1 0.0 copy-start.4
  430.1 0.0 copy-start.5
  430.2 0.2 slice_bitcast_fusion
  430.4 0.2 copy.27
  430.6 0.8 copy.29
  431.4 0.2 copy.28
  431.6 0.8 copy.30
  432.4 0.0 copy-done.4
  432.4 0.3 fusion.3
  432.8 0.0 copy-done.11
  432.8 0.0 copy-start.12
  432.8 0.0 copy-start.8
  432.8 3.0 fusion.9
  435.8 1.4 fusion.29
  437.2 0.8 copy.36
  438.0 0.0 copy-done.12
  438.0 0.8 copy.37
  438.8 1.1 copy.38
  439.9 1.1 copy.39
  441.0 1.1 copy.40
  (26 shorter events, 0.2 us)
Async XLA Ops:
  119.2 71.7 %copy-start.3 = (bf16[512,2048]{1,0:T(8,128)(2,1)S(1)}, bf16[512,2048]{1,0:T(8,128)(2,1)}, u32[]{:S(2)}) copy-start(bf16[512,2048]{1,0:T(8,128)(2,1)} %get-tuple-element.61.cot_all.cot) | copy-start | bytes 6291460
  190.8 5.9 %copy-start = (bf16[512,2048]{1,0:T(8,128)(2,1)S(1)}, bf16[512,2048]{1,0:T(8,128)(2,1)}, u32[]{:S(2)}) copy-start(bf16[512,2048]{1,0:T(8,128)(2,1)} %get-tuple-element.52.tok) | copy-start | bytes 6291460
  190.8 5.9 %copy-start.1 = (bf16[512,2048]{1,0:T(8,128)(2,1)S(1)}, bf16[512,2048]{1,0:T(8,128)(2,1)}, u32[]{:S(2)}) copy-start(bf16[512,2048]{1,0:T(8,128)(2,1)} %get-tuple-element.59.branch) | copy-start | bytes 6291460
  196.8 3.0 copy-start.14
  198.7 4.5 %slice-start = ((s8[5767168]{0:T(1024)(128)(4,1)}), s8[4194304]{0:T(1024)(128)(4,1)S(1)}, s32[]{:S(2)}) async-start(s8[5767168]{0:T(1024)(128)(4,1)} %bitcast.31), calls=%async_computation | async-start | bytes 8388608
  199.7 3.5 copy-start.2
  199.8 3.5 slice-start.1
  208.4 3.5 copy-start.9
  208.4 3.5 copy-start.10
  430.1 2.3 copy-start.4
  430.1 2.3 copy-start.5
  431.4 1.4 copy-start.11
  432.7 4.5 %copy-start.13 = (f32[256,512]{1,0:T(8,128)S(1)}, f32[256,512]{1,0:T(8,128)}, u32[]{:S(2)}) copy-start(f32[256,512]{1,0:T(8,128)} %get-tuple-element.159) | copy-start | bytes 1572868
  432.8 5.2 %copy-start.12 = (f32[256,512]{1,0:T(8,128)S(1)}, f32[256,512]{1,0:T(8,128)}, u32[]{:S(2)}) copy-start(f32[256,512]{1,0:T(8,128)} %get-tuple-element.162) | copy-start | bytes 1572868
  432.8 6.0 %copy-start.8 = (f32[256,1408]{1,0:T(8,128)S(1)}, f32[256,1408]{1,0:T(8,128)}, u32[]{:S(2)}) copy-start(f32[256,1408]{1,0:T(8,128)} %get-tuple-element.163) | copy-start | bytes 4325380
  435.8 4.1 copy-start.7
  438.8 2.2 copy-start.6

commit v3 on v2

--- a/solution.py
+++ b/solution.py
@@ -465,6 +465,10 @@
         blk = lax.axis_index("blk")
         self.x, self.c = blk // 2, blk % 2
         self.z = lax.axis_index("head")
+        self.end = (self.z == 0) | (self.z == 3)
+        self.middle = (self.z == 1) | (self.z == 2)
+        self.inward = {"head": jnp.where(self.z < 2, self.z + 1, self.z - 1)}
+        self.outward = {"head": jnp.where(self.z < 2, self.z - 1, self.z + 1)}
         self.send_sem, self.recv_sem, self.used = send_sem, recv_sem, 0
 
     def plane(self, i):
@@ -534,14 +538,57 @@
         pl.semaphore_wait(bar, peers)
 
 
+class Order:
+    def __init__(self, *tasks):
+        self.now, self.count, self.waiting = 0.0, 0, []
+        for task in tasks:
+            self.add(task)
+
+    def add(self, task, at=None):
+        self.waiting.append((self.now if at is None else at, self.count, task))
+        self.count += 1
+
+    def next_at(self):
+        return min(self.waiting, default=(math.inf,))[0]
+
+    def step(self):
+        item = min(self.waiting, key=lambda entry: entry[:2])
+        self.waiting.remove(item)
+        at = next(item[2], None)
+        if at is not None:
+            self.waiting.append((max(at, item[0]), item[1], item[2]))
+
+    def pump(self, until):
+        while self.next_at() <= until:
+            self.step()
+        self.now = max(self.now, until)
+
+    def finish(self):
+        while self.waiting:
+            self.step()
+
+    def loop(self, n, each, item, before=None):
+        start = self.now
+
+        def body(i, _):
+            for k in range(n):
+                while self.waiting and (
+                    self.next_at() <= start + k * each or (before is not None and before(k))
+                ):
+
+                    @pl.when(i == k)
+                    def _():
+                        self.step()
+
+            item(i)
+            return 0
+
+        lax.fori_loop(0, n, body, 0)
+        self.now = start + n * each
+
+
 def drive(*tasks):
-    waiting = [(0.0, i, task) for i, task in enumerate(tasks)]
-    while waiting:
-        waiting.sort(key=lambda item: item[:2])
-        _, i, task = waiting.pop(0)
-        at = next(task, None)
-        if at is not None:
-            waiting.append((at, i, task))
+    Order(*tasks).finish()
 
 
 def z_gather(me, src, dst, unit, begin=0.0):
@@ -665,13 +712,14 @@
     lax.fori_loop(0, rows // step, body, 0)
 
 
-def z_reduce_all(me, part, total, inbox, across, partial, out, unit, chunks=8, begin=0.0):
+class Progress:
+    def __init__(self, parts):
+        self.parts, self.whole = parts, 0
+
+
+def z_reduce_all(me, part, total, inbox, across, out, unit, chunks, progress, begin=0.0):
     rows = part.shape[0] // chunks
-    z = me.z
-    end = (z == 0) | (z == 3)
-    middle = (z == 1) | (z == 2)
-    inward = {"head": jnp.where(z < 2, z + 1, z - 1)}
-    outward = {"head": jnp.where(z < 2, z - 1, z + 1)}
+    end, middle = me.end, me.middle
     first = [me.slot() for _ in range(chunks)]
     second = [me.slot() for _ in range(chunks)]
     third = [me.slot() for _ in range(chunks)]
@@ -680,59 +728,78 @@
     def at(ref, k):
         return ref.at[pl.ds(k * rows, rows)]
 
+    def send_in(k):
+        return me.again(first[k], at(part, k), at(inbox, k), me.inward)
+
+    def send_across(k):
+        return me.again(second[k], at(inbox, k), at(across, k), me.inward)
+
+    def send_out(k):
+        return me.again(third[k], at(total, k), at(total, k), me.outward)
+
     def put(k):
-        return pltpu.make_async_copy(at(total, k), at(out, k), me.send_sem.at[store[k]])
-
-    if begin:
-        yield begin
+        if out is not None:
+            return pltpu.make_async_copy(at(total, k), at(out, k), me.send_sem.at[store[k]])
+
+    yield begin
+    hop = unit / chunks
+    time, sent = begin, 0
+    for k in range(chunks + 2):
+        while min(k, chunks - 1) >= progress.parts:
+            time += 1.0
+            yield time
+        new = range(sent, min(progress.parts, chunks))
+        sent = max(sent, min(progress.parts, chunks))
+        if len(new):
+
+            @pl.when(end)
+            def _():
+                for j in new:
+                    send_in(j).start()
+
+        time = max(time + hop, begin + hop * (k + 1) + 2.0)
+        yield time
+
+        @pl.when(middle)
+        def _():
+            if k < chunks:
+                send_in(k).wait_recv()
+                add_rows(at(inbox, k), at(part, k), at(inbox, k))
+                send_across(k).start()
+            if 1 <= k <= chunks:
+                send_across(k - 1).wait_recv()
+                add_rows(at(total, k - 1), at(inbox, k - 1), at(across, k - 1))
+                send_out(k - 1).start()
+                if out is not None:
+                    put(k - 1).start()
+
+        @pl.when(end)
+        def _():
+            if k >= 2:
+                send_out(k - 2).wait_recv()
+                if out is not None:
+                    put(k - 2).start()
+
+        progress.whole = max(0, k - 1)
+    yield time + 1.0
 
     @pl.when(end)
     def _():
         for k in range(chunks):
-            me.again(first[k], at(part, k), at(inbox, k), inward).start()
-
-    hop = unit / chunks
-    for k in range(chunks + 2):
-        yield begin + hop * (k + 1) + 2.0
-
-        @pl.when(middle)
-        def _():
-            if k < chunks:
-                me.again(first[k], at(part, k), at(inbox, k), inward).wait_recv()
-                add_rows(at(partial, k), at(part, k), at(inbox, k))
-                me.again(second[k], at(partial, k), at(across, k), inward).start()
-            if 1 <= k <= chunks:
-                j = k - 1
-                me.again(second[j], at(partial, j), at(across, j), inward).wait_recv()
-                add_rows(at(total, j), at(partial, j), at(across, j))
-                me.again(third[j], at(total, j), at(total, j), outward).start()
-                put(j).start()
-
-        @pl.when(end)
-        def _():
-            if k >= 2:
-                j = k - 2
-                me.again(third[j], at(total, j), at(total, j), outward).wait_recv()
-                put(j).start()
-
-    yield begin + unit + hop * 3
-
-    @pl.when(end)
-    def _():
-        for k in range(chunks):
-            me.again(first[k], at(part, k), at(inbox, k), inward).wait_send()
+            send_in(k).wait_send()
 
     @pl.when(middle)
     def _():
         for k in range(chunks):
-            me.again(second[k], at(partial, k), at(across, k), inward).wait_send()
-            me.again(third[k], at(total, k), at(total, k), outward).wait_send()
-
-    for k in range(chunks):
-        put(k).wait()
-
-
-def z_reduce_scatter(me, part, from_below, from_above, sums_up, sums_down, own, unit, begin=0.0):
+            send_across(k).wait_send()
+            send_out(k).wait_send()
+
+    if out is not None:
+        for k in range(chunks):
+            put(k).wait()
+
+
+def z_reduce_scatter(me, part, from_below, from_above, own, unit, begin=0.0):
     rows = part.shape[0] // 4
     z = me.z
     ups = [me.slot() for _ in range(4)]
@@ -760,15 +827,15 @@
         @pl.when(z == stop)
         def _():
             up(j, part).wait_recv()
-            add_rows(at(sums_up, j), at(part, j), at(from_below, j))
-            up(j, sums_up).start()
+            add_rows(at(from_below, j), at(part, j), at(from_below, j))
+            up(j, from_below).start()
 
         @pl.when(z == 3 - stop)
         def _():
             i = 3 - j
             down(i, part).wait_recv()
-            add_rows(at(sums_down, i), at(part, i), at(from_above, i))
-            down(i, sums_down).start()
+            add_rows(at(from_above, i), at(part, i), at(from_above, i))
+            down(i, from_above).start()
 
     yield begin
     start(3)
@@ -810,10 +877,18 @@
                     down(i, part).wait_send()
 
 
+def offsets_of(me, j):
+    dx, dy, dc = 1 - (j % 4) // 2, 1 - j % 2, 1 - j // 4
+    y = me.y + dy - 2 * me.y * dy
+    x = me.x + dx - 2 * me.x * dx
+    c = me.c + dc - 2 * me.c * dc
+    return y * 4 + x * 2 + c
+
+
 def plane_scatter_scratch(rows, cols):
     half = rows // 2
     return [
-        pltpu.VMEM((4, rows, cols), bf16),
+        pltpu.VMEM((8, rows, cols), bf16),
         pltpu.VMEM((4, rows, cols), bf16),
         pltpu.VMEM((2, half, cols), bf16),
         pltpu.VMEM((2, half, cols), bf16),
@@ -822,70 +897,77 @@
     ]
 
 
+class PlaneScatter:
+    def __init__(self, me, scratch):
+        self.blocks, self.other, self.over_x, self.over_y, self.last_y, self.last_x = scratch
+        blocks, rows = self.blocks, self.blocks.shape[1]
+        half = rows // 2
+        self.half, self.first, self.second = half, pl.ds(0, half), pl.ds(half, half)
+        first, second = self.first, self.second
+        self.core = [me.copy(blocks.at[j], self.other.at[j], me.plane(1)) for j in range(4)]
+        self.far_x = me.copy(blocks.at[4, first], self.over_x.at[1], me.plane(2))
+        self.far_y = me.copy(blocks.at[4, second], self.over_y.at[1], me.plane(4))
+        self.near_x = me.copy(blocks.at[5, first], self.over_x.at[0], me.plane(2))
+        self.near_y = me.copy(blocks.at[6, second], self.over_y.at[0], me.plane(4))
+        self.to_y = me.copy(blocks.at[6, first], self.last_y, me.plane(4))
+        self.to_x = me.copy(blocks.at[5, second], self.last_x, me.plane(2))
+
+    def steps(self, out, unit, begin):
+        blocks, half, first, second = self.blocks, self.half, self.first, self.second
+        for j in range(4):
+            yield begin + 0.3 * j
+            self.core[j].wait_recv()
+            add_rows(blocks.at[4 + j], blocks.at[4 + j], self.other.at[j])
+            if j == 0:
+                self.far_x.start()
+                self.far_y.start()
+            if j == 1:
+                self.near_x.start()
+            if j == 2:
+                self.near_y.start()
+        yield begin + 3.0 + unit * 0.5
+        self.far_x.wait_recv()
+        add_rows(blocks.at[6, first], blocks.at[6, first], self.over_x.at[1])
+        self.to_y.start()
+        self.far_y.wait_recv()
+        add_rows(blocks.at[5, second], blocks.at[5, second], self.over_y.at[1])
+        self.to_x.start()
+        yield begin + 4.0 + unit * 1.5
+        for copy in (self.near_x, self.near_y, self.to_y, self.to_x):
+            copy.wait_recv()
+
+        def body(i, _):
+            at = pl.ds(pl.multiple_of(i * 32, 32), 32)
+            low = pl.ds(pl.multiple_of(half + i * 32, 32), 32)
+            for rows, near, last in ((at, self.over_x, self.last_y), (low, self.over_y, self.last_x)):
+                value = blocks[7, rows, :].astype(f32) + near[0, at, :].astype(f32)
+                out[rows, :] = (value + last[at, :].astype(f32)).astype(out.dtype)
+            return 0
+
+        lax.fori_loop(0, half // 32, body, 0)
+        for copy in (*self.core, self.far_x, self.far_y, self.near_x, self.near_y, self.to_y, self.to_x):
+            copy.wait_send()
+
+
 def plane_scatter(me, src, out, scratch, unit, begin=0.0):
-    held, other, over_x, over_y, last_y, last_x = scratch
+    scatter = PlaneScatter(me, scratch)
     rows = out.shape[0]
-    half = rows // 2
-
-    def block(i):
-        return src.at[pl.ds(pl.multiple_of(me.number(i) * rows, rows), rows)]
-
-    first, second = pl.ds(0, half), pl.ds(half, half)
-    if begin:
-        yield begin
-    loads, cores = {}, {}
-    for i in (6, 2, 4, 0):
-        cores[i] = me.copy(block(i + 1), other.at[i // 2], me.plane(1))
-        cores[i].start()
-        loads[i] = me.local(block(i), held.at[i // 2])
-        loads[i].start()
-    yield begin + 3.0
-    for i in (6, 2, 4, 0):
-        loads[i].wait()
-        cores[i].wait_recv()
-        add_rows(held.at[i // 2], held.at[i // 2], other.at[i // 2])
-        if i == 6:
-            six_x = me.copy(held.at[3, first], over_x.at[1], me.plane(2))
-            six_y = me.copy(held.at[3, second], over_y.at[1], me.plane(4))
-            six_x.start()
-            six_y.start()
-        if i == 2:
-            two_x = me.copy(held.at[1, first], over_x.at[0], me.plane(2))
-            two_x.start()
-        if i == 4:
-            four_y = me.copy(held.at[2, second], over_y.at[0], me.plane(4))
-            four_y.start()
-    yield begin + 4.0 + unit * 0.5
-    six_x.wait_recv()
-    add_rows(held.at[2, first], held.at[2, first], over_x.at[1])
-    to_y = me.copy(held.at[2, first], last_y, me.plane(4))
-    to_y.start()
-    six_y.wait_recv()
-    add_rows(held.at[1, second], held.at[1, second], over_y.at[1])
-    to_x = me.copy(held.at[1, second], last_x, me.plane(2))
-    to_x.start()
-    yield begin + 5.0 + unit * 1.5
-    two_x.wait_recv()
-    four_y.wait_recv()
-    to_y.wait_recv()
-    to_x.wait_recv()
-
-    def body(i, _):
-        at = pl.ds(pl.multiple_of(i * 32, 32), 32)
-        low = pl.ds(pl.multiple_of(half + i * 32, 32), 32)
-        out[at, :] = (
-            held[0, at, :].astype(f32) + over_x[0, at, :].astype(f32) + last_y[at, :].astype(f32)
-        ).astype(out.dtype)
-        out[low, :] = (
-            held[0, low, :].astype(f32) + over_y[0, at, :].astype(f32) + last_x[at, :].astype(f32)
-        ).astype(out.dtype)
-        return 0
-
-    lax.fori_loop(0, half // 32, body, 0)
-    for i in (6, 2, 4, 0):
-        cores[i].wait_send()
-    for copy in (six_x, six_y, two_x, four_y, to_y, to_x):
-        copy.wait_send()
+    loads = [
+        me.local(
+            src.at[pl.ds(pl.multiple_of(offsets_of(me, j) * rows, rows), rows)], scatter.blocks.at[j]
+        )
+        for j in range(8)
+    ]
+    yield begin
+    for load in loads:
+        load.start()
+    for j in range(4):
+        loads[j].wait()
+        scatter.core[j].start()
+    yield begin + 1.0
+    for j in range(4, 8):
+        loads[j].wait()
+    yield from scatter.steps(out, unit, begin + 2.5)
 
 
 def params(number, vmem=60 * 2**20):
@@ -1094,11 +1176,11 @@
     )(q_t, kv_own, key_pos, query_pos, cot, wo, wu)
 
 
-def third_kernel(part, wg, wd, total_out, wg_all, wd_all, total, inbox, across, partial, ss, rs):
+def third_kernel(part, wg, wd, total_out, wg_all, wd_all, total, inbox, across, ss, rs):
     me = Here(ss, rs)
     me.enter((1, 2, 4))
     drive(
-        z_reduce_all(me, part, total, inbox, across, partial, total_out, 45.0, 16),
+        z_reduce_all(me, part, total, inbox, across, total_out, 45.0, 16, Progress(16)),
         plane_gather(me, wg, wg_all, 15.5, 0.1),
         plane_gather(me, wd, wd_all, 15.5, 15.0),
     )
@@ -1115,7 +1197,7 @@
         out_shape=(shape(part.shape), grown(wg), grown(wd)),
         in_specs=[VM] * 3,
         out_specs=[HB] * 3,
-        scratch_shapes=[rows] * 4 + dma_sems(96),
+        scratch_shapes=[rows] * 3 + dma_sems(96),
         compiler_params=params(3),
         name="sum_branch",
     )(part, wg, wd)
@@ -1129,257 +1211,268 @@
     return lax.dot_general(left, right, (((1,), (1,)), ((), ())), preferred_element_type=f32)
 
 
-def fourth_kernel(
-    part, cot_all, hidden, normed_two, d_gate, d_up, wd_all,
-    total_out, dwd_own, dwg, dwu, out_part,
-    total, inbox, across, partial, left_a, left_b, right_a, right_b, right_c, wd, dwd, stage, *rest
+def backward_kernel(
+    part, cot_all, hidden, normed_two, d_gate, d_up, wd_all, tok_all, branch, gains, wo_all,
+    out_t_all, attended_all, q_t_all, q_n_all, kv_all, log_sum, key_pos, query_pos,
+    dwd_own, dwg_own, dwu, out_own, dwo, own, gain_part, dq_t, dkv_own,
+    total, inbox, across, cot, out_part, below, above, q_t, q_n, kv, k_t, came, *rest
 ):
-    *scratch, ss, rs = rest
+    scratch_d, scratch_g, (ss, rs) = rest[:6], rest[6:12], rest[12:]
     me = Here(ss, rs)
-    me.enter((1, 2, 4))
-    blocks = left_a.shape[1] // 256
-    pairs = ((cot_all, left_a), (hidden, right_a), (normed_two, left_b), (d_gate, right_b), (d_up, right_c), (wd_all, wd))
-    loads = [me.local(src, dst) for src, dst in pairs]
-
-    def block(ref, i):
-        return ref[:, i * 256 : (i + 1) * 256]
-
-    def down():
-        yield 0.2
+    me.enter((1, 2, 3, 4))
+    z = me.z
+    rows, width = part.shape
+    heads, hd, _ = q_t.shape
+    keys = kv.shape[0]
+    cols = width // 8
+    progress = Progress(16)
+    order = Order(z_reduce_all(me, part, total, inbox, across, None, 45.0, 16, progress))
+    down, gate = PlaneScatter(me, scratch_d), PlaneScatter(me, scratch_g)
+    cot_load = me.local(cot_all, cot)
+    cot_load.start()
+    later = [me.local(src, dst) for src, dst in ((kv_all, kv), (q_t_all, q_t), (q_n_all, q_n))]
+    stores = [me.slot() for _ in range(4)]
+
+    def weights(left, right_h, right_g, right_u, stage, wd):
+        pairs = ((hidden, right_h), (normed_two, left), (d_gate, right_g), (d_up, right_u))
+        loads = [me.local(src, dst) for src, dst in pairs]
         for load in loads:
             load.start()
+        for load in later:
+            load.start()
+        cot_load.wait()
         loads[0].wait()
+        order.pump(2.0)
+
+        def columns(j):
+            return pl.ds(pl.multiple_of(offsets_of(me, j) * cols, cols), cols)
+
+        def send(scatter, j):
+            for k in range(4):
+
+                @pl.when(j == k)
+                def _():
+                    scatter.core[k].start()
+
+        def down_item(j):
+            down.blocks[j] = contract_rows(cot[:, columns(j)], right_h[...]).astype(bf16)
+            send(down, j)
+
+        order.loop(8, 0.9, down_item)
+        order.add(down.steps(dwd_own, 15.5, order.now + 0.1))
         loads[1].wait()
-        for i in range(blocks):
-            yield 2.5 + i
-            dwd[i * 256 : (i + 1) * 256, :] = contract_rows(block(left_a, i), right_a[...]).astype(bf16)
-        yield from plane_scatter(me, dwd, dwd_own, scratch, 15.5, 2.6 + blocks)
-
-    puts = [me.slot(), me.slot()]
-    busy = [None, None]
-
-    def put(n, value, dst):
-        k = n % 2
-        if busy[k] is not None:
-            busy[k].wait()
-        view = stage.at[k, pl.ds(0, value.shape[0]), pl.ds(0, value.shape[1])]
-        stage[k, : value.shape[0], : value.shape[1]] = value.astype(bf16)
-        busy[k] = pltpu.make_async_copy(view, dst, me.send_sem.at[puts[k]])
-        busy[k].start()
-
-    def others():
-        n = 0
-        yield 11.0
         loads[2].wait()
-        for load, right, dst in ((loads[3], right_b, dwg), (loads[4], right_c, dwu)):
+
+        def gate_item(j):
+            gate.blocks[j] = contract_rows(left[:, columns(j)], right_g[...]).astype(bf16)
+            send(gate, j)
+
+        order.loop(8, 0.9, gate_item)
+        order.add(gate.steps(dwg_own, 15.5, order.now + 15.0))
+        loads[3].wait()
+
+        def put(j):
+            at = pl.ds(pl.multiple_of(j * cols, cols), cols)
+            return pltpu.make_async_copy(stage.at[j % 2], dwu.at[at], ss.at[stores[0]])
+
+        def up_item(j):
+            @pl.when(j >= 1)
+            def _():
+                put(j - 1).wait()
+
+            at = pl.ds(pl.multiple_of(j * cols, cols), cols)
+            stage[j % 2] = contract_rows(left[:, at], right_u[...]).astype(bf16)
+            put(j).start()
+
+        order.loop(8, 0.9, up_item)
+        put(7).wait()
+
+        def fetch(j):
+            at = pl.ds(pl.multiple_of(j * cols, cols), cols)
+            return pltpu.make_async_copy(wd_all.at[at], wd.at[j % 2], ss.at[stores[1]])
+
+        fetch(0).start()
+
+        def out_item(j):
+            fetch(j).wait()
+
+            @pl.when(j < 7)
+            def _():
+                fetch(j + 1).start()
+
+            at = pl.ds(pl.multiple_of(j * cols, cols), cols)
+            out_part[:, at] = contract_last_dims(right_h[...], wd[j % 2]).astype(bf16)
+
+        order.loop(8, 0.7, out_item)
+
+    units = pltpu.VMEM(hidden.shape, bf16)
+    weight = pltpu.VMEM((2, cols, hidden.shape[1]), bf16)
+    pl.run_scoped(weights, pltpu.VMEM(part.shape, bf16), units, units, units, weight, weight)
+
+    def attention(tok, summed, wo, out_t, attended, g_t, g_n, delta, dk, dv):
+        gain = gain_row(gains, 1)
+
+        def fetch(r):
+            at = pl.ds(pl.multiple_of(r * 128, 128), 128)
+            return (
+                pltpu.make_async_copy(tok_all.at[at], tok, ss.at[stores[2]]),
+                pltpu.make_async_copy(branch.at[at], summed, ss.at[stores[3]]),
+            )
+
+        for copy in fetch(0):
+            copy.start()
+        loads = [
+            me.local(src, dst)
+            for src, dst in ((wo_all, wo), (out_t_all, out_t), (attended_all, attended))
+        ]
+        for load in loads:
+            load.start()
+        dk[...] = jnp.zeros_like(dk)
+        dv[...] = jnp.zeros_like(dv)
+        for load in later:
             load.wait()
-            for i in range(blocks):
-                yield 12.0 + n
-                value = contract_rows(block(left_b, i), right[...])
-                put(n, value, dst.at[pl.ds(i * 256, 256)])
-                n += 1
-        loads[5].wait()
-        for i in range(hidden.shape[0] // 128):
-            for h in (0, 1):
-                yield 12.0 + n
-                at = slice(i * 128, (i + 1) * 128)
-                half = wd.shape[0] // 2
-                value = contract_last_dims(right_a[at, :], wd[h * half : (h + 1) * half, :])
-                put(n, value, out_part.at[pl.ds(i * 128, 128), pl.ds(h * half, half)])
-                n += 1
-        for copy in busy:
-            copy.wait()
-
-    drive(
-        z_reduce_all(me, part, total, inbox, across, partial, total_out, 45.0, 16),
-        down(),
-        others(),
-    )
-
-
-def fourth(part, cot_all, hidden, normed_two, d_gate, d_up, wd_all):
-    rows = pltpu.VMEM(part.shape, bf16)
-    units = pltpu.VMEM(hidden.shape, bf16)
-    weight = pltpu.VMEM(wd_all.shape, bf16)
+        for i in range(keys // rows):
+            span = slice(i * rows, (i + 1) * rows)
+            k_t[:, span] = kv[span, :].astype(f32).T[:hd, :].astype(bf16)
+        for load in loads:
+            load.wait()
+        order.add(z_reduce_scatter(me, out_part, below, above, out_own, 11.3, 47.0), 47.0)
+
+        def prepare(r):
+            for copy in fetch(r):
+                copy.wait()
+            at = pl.ds(pl.multiple_of(r * 128, 128), 128)
+            h = tok[...].astype(f32) + summed[...].astype(f32)
+            e = total[at, :].astype(f32)
+            inv = lax.rsqrt(jnp.mean(h * h, axis=1, keepdims=True) + norm_epsilon)
+            u = e * gain
+            inner = jnp.mean(u * h, axis=1, keepdims=True)
+            grad = cot[at, :].astype(f32) + (inv * u - h * (inv * inv * inv * inner))
+
+            @pl.when(r == z)
+            def _():
+                own[...] = grad
+                gain_part[...] = jnp.broadcast_to(
+                    jnp.sum(e * h * inv, axis=0, keepdims=True), gain_part.shape
+                )
+
+            small = grad.astype(bf16)
+            cot[at, :] = small
+            g = jnp.dot(small, wo[...], preferred_element_type=f32).astype(bf16)
+            turned = g.astype(f32).T
+            for head in range(heads):
+                g_n[head] = g[:, head * hd : (head + 1) * hd]
+                mine = turned[head * hd : (head + 1) * hd]
+                g_t[head] = mine.astype(bf16)
+                delta[head] = jnp.sum(mine * out_t[head, :, at], axis=0, keepdims=True)
+
+            @pl.when(r < rows // 128 - 1)
+            def _():
+                for copy in fetch(r + 1):
+                    copy.start()
+
+        def item(i):
+            r, h = i // heads, i % heads
+
+            @pl.when(h == 0)
+            def _():
+                prepare(r)
+
+            at = pl.ds(pl.multiple_of(r * 128, 128), 128)
+            s = jnp.dot(kv[:, 0:hd], q_t[h, :, at], preferred_element_type=f32)
+            s = jnp.where(key_pos[...] <= query_pos[0:1, at], s, masked_value)
+            p = jnp.exp(s - log_sum[h, :, at])
+            dp = jnp.dot(kv[:, hd:], g_t[h], preferred_element_type=f32)
+            ds = (p * (dp - delta[h])).astype(bf16)
+            dv[...] += jnp.dot(p.astype(bf16), g_n[h], preferred_element_type=f32)
+            dk[...] += jnp.dot(ds, q_n[h, at, :], preferred_element_type=f32)
+            grad = jnp.dot(k_t[...], ds, preferred_element_type=f32)
+            dq_t[h, :, at] = (grad * (1.0 / math.sqrt(hd))).astype(bf16)
+
+        def before(k):
+            return progress.whole < (k // heads + 1) * 4
+
+        order.loop(heads * rows // 128, 1.2, item, before)
+        for i in range(keys // rows):
+            span = slice(i * rows, (i + 1) * rows)
+            kv[span, :] = jnp.concatenate([dk[span, :], dv[span, :]], axis=1).astype(bf16)
+        copies = [
+            me.copy(kv.at[pl.ds(i * rows, rows)], came.at[i - 1], me.plane(i)) for i in (1, 2, 3)
+        ]
+        for copy in copies:
+            copy.start()
+
+        def out_item(i):
+            span = pl.ds(pl.multiple_of(i * cols, cols), cols)
+            dwo[span, :] = contract_rows(cot[:, span], attended[...]).astype(bf16)
+
+        order.loop(8, 0.4, out_item)
+        order.pump(order.now + 2.0)
+        value = kv[0:rows, :].astype(f32)
+        for i, copy in enumerate(copies):
+            copy.wait_recv()
+            value = value + came[i].astype(f32)
+        dkv_own[...] = value
+        for copy in copies:
+            copy.wait_send()
+
+    slots = pltpu.VMEM((128, width), bf16)
+    pl.run_scoped(
+        attention,
+        slots,
+        slots,
+        pltpu.VMEM(wo_all.shape, bf16),
+        pltpu.VMEM(out_t_all.shape, f32),
+        pltpu.VMEM(attended_all.shape, bf16),
+        pltpu.VMEM((heads, hd, 128), bf16),
+        pltpu.VMEM((heads, 128, hd), bf16),
+        pltpu.VMEM((heads, 1, 128), f32),
+        pltpu.VMEM((keys, hd), f32),
+        pltpu.VMEM((keys, hd), f32),
+    )
+    order.finish()
+
+
+def backward(
+    part, cot_all, hidden, normed_two, d_gate, d_up, wd_all, tok_all, branch, gains, wo_all,
+    out_t, attended, q_t, q_n, kv_all, log_sum, key_pos, query_pos
+):
+    heads, hd, rows = q_t.shape
+    keys = key_pos.shape[0]
+    width = part.shape[1]
+    whole = pltpu.VMEM(part.shape, bf16)
     own = (wd_all.shape[0] // 8, wd_all.shape[1])
     return pl.pallas_call(
-        fourth_kernel,
+        backward_kernel,
         out_shape=(
-            shape(part.shape), shape(own, f32), shape(wd_all.shape), shape(wd_all.shape), shape(part.shape)
-        ),
-        in_specs=[VM] + [HB] * 6,
-        out_specs=[HB, VM, HB, HB, HB],
-        scratch_shapes=[rows] * 6 + [units] * 3 + [weight] * 2
-        + [pltpu.VMEM((2, 256, max(own[1], wd_all.shape[0] // 2)), bf16)]
-        + plane_scatter_scratch(*own) + dma_sems(128),
-        compiler_params=params(4, 63 * 2**20),
-        name="sum_grad_normed_two",
-    )(part, cot_all, hidden, normed_two, d_gate, d_up, wd_all)
-
-
-def prepare_kernel(cot, tok, branch, grad_two, gains, wo, out_t, attended, g_t, g_n, delta, own, gain_part, dwo, low):
-    heads = g_t.shape[0]
-    gain = gain_row(gains, 1)
-    z = lax.axis_index("head")
-
-    def body(i, _):
-        at = pl.ds(pl.multiple_of(i * 128, 128), 128)
-        h = tok[at, :].astype(f32) + branch[at, :].astype(f32)
-        e = grad_two[at, :].astype(f32)
-        inv = lax.rsqrt(jnp.mean(h * h, axis=1, keepdims=True) + norm_epsilon)
-        u = e * gain
-        inner = jnp.mean(u * h, axis=1, keepdims=True)
-        grad = cot[at, :].astype(f32) + (inv * u - h * (inv * inv * inv * inner))
-
-        @pl.when(i == z)
-        def _():
-            own[...] = grad
-            gain_part[...] = jnp.broadcast_to(
-                jnp.sum(e * h * inv, axis=0, keepdims=True), gain_part.shape
-            )
-
-        small = grad.astype(bf16)
-        low[at, :] = small
-        g = jnp.dot(small, wo[...], preferred_element_type=f32).astype(bf16)
-        turned = g.astype(f32).T
-        for head in range(heads):
-            g_n[head, at, :] = g[:, head * HD : (head + 1) * HD]
-            mine = turned[head * HD : (head + 1) * HD]
-            g_t[head, :, at] = mine.astype(bf16)
-            delta[head, :, at] = jnp.sum(mine * out_t[head, :, at], axis=0, keepdims=True)
-        return 0
-
-    lax.fori_loop(0, tok.shape[0] // 128, body, 0)
-    for i in range(dwo.shape[0] // 256):
-        span = slice(i * 256, (i + 1) * 256)
-        dwo[span, :] = contract_rows(low[:, span], attended[...]).astype(bf16)
-
-
-def prepare(cot, tok, branch, grad_two, gains, wo, out_t, attended):
-    heads, hd, rows = out_t.shape
-    width = tok.shape[1]
-    return pl.pallas_call(
-        prepare_kernel,
-        out_shape=(
-            shape((heads, hd, rows)),
-            shape((heads, rows, hd)),
-            shape((heads, 1, rows), f32),
+            shape(own, f32),
+            shape(own, f32),
+            shape(wd_all.shape),
+            shape((rows // 4, width), f32),
+            shape(wo_all.shape),
             shape((rows // 4, width), f32),
             shape((8, width), f32),
-            shape(wo.shape),
-        ),
-        in_specs=[VM] * 8,
-        out_specs=[VM] * 6,
-        scratch_shapes=[pltpu.VMEM(tok.shape, bf16)],
-        name="prepare_backward",
-        **alone(4 * rows * width * heads * hd),
-    )(cot, tok, branch, grad_two, gains, wo, out_t, attended)
-
-
-def attention_backward(me, q_t, q_n, g_t, g_n, kv_all, log_sum, delta, key_pos, query_pos, dq_t, dkv_own, kv, k_t, dk, dv, dkv, came, per):
-    heads, hd, rows = q_t.shape
-    blocks = kv.shape[0] // rows
-    load = me.local(kv_all, kv)
-    load.start()
-    dk[...] = jnp.zeros_like(dk)
-    dv[...] = jnp.zeros_like(dv)
-    load.wait()
-    for i in range(blocks):
-        k_t[:, i * rows : (i + 1) * rows] = kv[i * rows : (i + 1) * rows, :].astype(f32).T[:hd, :].astype(bf16)
-
-    def head(h, _):
-        q, g = q_t[h], g_t[h]
-        limit = query_pos[0:1, :]
-
-        def step(i, acc):
-            at = pl.ds(pl.multiple_of(i * rows, rows), rows)
-            both = kv[at, :]
-            s = jnp.dot(both[:, 0:hd], q, preferred_element_type=f32)
-            pos = key_pos[at, :]
-            pos = jnp.concatenate([pos] * (rows // 128), axis=1)
-            s = jnp.where(pos <= limit, s, masked_value)
-            p = jnp.exp(s - log_sum[h])
-            dp = jnp.dot(both[:, hd:], g, preferred_element_type=f32)
-            ds = (p * (dp - delta[h])).astype(bf16)
-            dv[at, :] += jnp.dot(p.astype(bf16), g_n[h], preferred_element_type=f32)
-            dk[at, :] += jnp.dot(ds, q_n[h], preferred_element_type=f32)
-            return acc + jnp.dot(k_t[:, at], ds, preferred_element_type=f32)
-
-        acc = lax.fori_loop(0, blocks, step, jnp.zeros((hd, rows), f32))
-        dq_t[h] = (acc * (1.0 / math.sqrt(hd))).astype(bf16)
-        return 0
-
-    for h in range(0, heads, 2):
-        yield 0.3 + per * h
-        lax.fori_loop(h, h + 2, head, 0)
-    for i in range(blocks):
-        at = slice(i * rows, (i + 1) * rows)
-        dkv[at, :] = jnp.concatenate([dk[at, :], dv[at, :]], axis=1).astype(bf16)
-    copies = [
-        me.copy(dkv.at[pl.ds(i * rows, rows)], came.at[i - 1], me.plane(i)) for i in (1, 2, 3)
-    ]
-    for copy in copies:
-        copy.start()
-    yield 0.3 + per * heads + 8.0
-    for copy in copies:
-        copy.wait_recv()
-    value = dkv[0:rows, :].astype(f32)
-    for i in range(blocks - 1):
-        value = value + came[i].astype(f32)
-    dkv_own[...] = value
-    for copy in copies:
-        copy.wait_send()
-
-
-def fifth_kernel(
-    q_t, q_n, g_t, g_n, kv_all, log_sum, delta, key_pos, query_pos, out_part, dwg, dwu,
-    dq_t, dkv_own, out_own, dwg_own, dwu_own,
-    kv, k_t, dk, dv, dkv, came, below, above, sums_up, sums_down, *rest
-):
-    *scratch, ss, rs = rest
-    me = Here(ss, rs)
-    me.enter((1, 2, 3, 4))
-    drive(
-        plane_scatter(me, dwg, dwg_own, scratch[:6], 15.5),
-        plane_scatter(me, dwu, dwu_own, scratch[6:], 15.5, 18.0),
-        z_reduce_scatter(me, out_part, below, above, sums_up, sums_down, out_own, 11.3),
-        attention_backward(
-            me, q_t, q_n, g_t, g_n, kv_all, log_sum, delta, key_pos, query_pos,
-            dq_t, dkv_own, kv, k_t, dk, dv, dkv, came, 6.0,
-        ),
-    )
-
-
-def fifth(q_t, q_n, g_t, g_n, kv_all, log_sum, delta, key_pos, query_pos, out_part, dwg, dwu):
-    heads, hd, rows = q_t.shape
-    keys = key_pos.shape[0]
-    own = (dwg.shape[0] // 8, dwg.shape[1])
-    part = pltpu.VMEM(out_part.shape, bf16)
-    return pl.pallas_call(
-        fifth_kernel,
-        out_shape=(
             shape((heads, hd, rows)),
             shape((rows, 2 * hd), f32),
-            shape((out_part.shape[0] // 4, out_part.shape[1]), f32),
-            shape(own, f32),
-            shape(own, f32),
         ),
-        in_specs=[VM] * 4 + [HB] + [VM] * 5 + [HB] * 2,
-        out_specs=[VM] * 5,
-        scratch_shapes=[
+        in_specs=[VM] + [HB] * 8 + [VM] + [HB] * 6 + [VM] * 3,
+        out_specs=[VM, VM, HB] + [VM] * 6,
+        scratch_shapes=[whole] * 7
+        + [
+            pltpu.VMEM(q_t.shape, bf16),
+            pltpu.VMEM(q_n.shape, bf16),
             pltpu.VMEM((keys, 2 * hd), bf16),
             pltpu.VMEM((hd, keys), bf16),
-            pltpu.VMEM((keys, hd), f32),
-            pltpu.VMEM((keys, hd), f32),
-            pltpu.VMEM((keys, 2 * hd), bf16),
             pltpu.VMEM((keys // rows - 1, rows, 2 * hd), bf16),
-            part, part, part, part,
         ]
         + plane_scatter_scratch(*own) * 2
-        + dma_sems(64),
-        compiler_params=params(5),
-        name="attention_backward",
-    )(q_t, q_n, g_t, g_n, kv_all, log_sum, delta, key_pos, query_pos, out_part, dwg, dwu)
+        + dma_sems(160),
+        compiler_params=params(4, 67043328),
+        name="backward",
+    )(
+        part, cot_all, hidden, normed_two, d_gate, d_up, wd_all, tok_all, branch, gains, wo_all,
+        out_t, attended, q_t, q_n, kv_all, log_sum, key_pos, query_pos
+    )
 
 
 def finish_kernel(dq_t, dkv, cos_t, sin_t, wqkv, normed, tok, gain_two, one_part, dwqkv, gain_parts, lin):
@@ -1452,9 +1545,9 @@
 
 
 def sixth_kernel(
-    part, dwqkv, dwo, gains,
-    own, dwq_own, dwkv_all, dwo_own, gains_out,
-    below, above, sums_up, sums_down, dwqkv_own, dwkv_own, came_kv, came, mine, came_z, *rest
+    part, dwqkv, dwo, dwu, gains,
+    own, dwq_own, dwkv_all, dwo_own, dwu_own, gains_out,
+    below, above, dwqkv_own, dwkv_own, came_kv, came, mine, came_z, *rest
 ):
     *scratch, ss, rs = rest
     me = Here(ss, rs)
@@ -1462,7 +1555,7 @@
     wide = dwq_own.shape[1]
 
     def weights():
-        yield from plane_scatter(me, dwqkv, dwqkv_own, scratch[:6], 7.0, 0.1)
+        yield from plane_scatter(me, dwqkv, dwqkv_own, scratch[:6], 7.0, 18.0)
         dwq_own[...] = dwqkv_own[:, :wide]
         dwkv_own[...] = dwqkv_own[:, wide:].astype(bf16)
         copies = [
@@ -1470,7 +1563,7 @@
         ]
         for copy in copies:
             copy.start()
-        yield 37.0
+        yield 45.0
         for copy in copies:
             copy.wait_recv()
         dwkv_all[0] = dwkv_own[...]
@@ -1481,13 +1574,14 @@
 
     drive(
         gain_sums(me, gains, gains_out, came, mine, came_z),
-        z_reduce_scatter(me, part, below, above, sums_up, sums_down, own, 11.3),
+        z_reduce_scatter(me, part, below, above, own, 11.3),
+        plane_scatter(me, dwu, dwu_own, scratch[12:], 15.5, 0.1),
+        plane_scatter(me, dwo, dwo_own, scratch[6:12], 8.0, 9.0),
         weights(),
-        plane_scatter(me, dwo, dwo_own, scratch[6:], 6.0, 9.0),
-    )
-
-
-def sixth(part, dwqkv, dwo, gains):
+    )
+
+
+def sixth(part, dwqkv, dwo, dwu, gains):
     rows, cols = dwqkv.shape[0] // 8, dwqkv.shape[1]
     wide = dwo.shape[1]
     whole = pltpu.VMEM(part.shape, bf16)
@@ -1498,12 +1592,13 @@
             shape((rows, wide), f32),
             shape((4, rows, cols - wide)),
             shape((rows, wide), f32),
+            shape((rows, dwu.shape[1]), f32),
             shape((8, gains.shape[1]), f32),
         ),
-        in_specs=[VM, HB, HB, VM],
-        out_specs=[VM] * 5,
+        in_specs=[VM, HB, HB, HB, VM],
+        out_specs=[VM] * 6,
         scratch_shapes=[
-            whole, whole, whole, whole,
+            whole, whole,
             pltpu.VMEM((rows, cols), f32),
             pltpu.VMEM((rows, cols - wide), bf16),
             pltpu.VMEM((3, rows, cols - wide), bf16),
@@ -1513,10 +1608,11 @@
         ]
         + plane_scatter_scratch(rows, cols)
         + plane_scatter_scratch(rows, wide)
-        + dma_sems(64),
+        + plane_scatter_scratch(rows, dwu.shape[1])
+        + dma_sems(96),
         compiler_params=params(6),
         name="scatter_last",
-    )(part, dwqkv, dwo, gains)
+    )(part, dwqkv, dwo, dwu, gains)
 
 
 def local_fast(
@@ -1583,20 +1679,16 @@
     d_up = (grad_hidden * gate_silu).astype(bf16)
     two_part = lax.dot_general(d_gate, wg_all, contract_last, preferred_element_type=f32)
     two_part = two_part + lax.dot_general(d_up, wu_all, contract_last, preferred_element_type=f32)
-    grad_two, dwd_own, dwg, dwu, out_part = fourth(
-        two_part.astype(bf16), cot_all, hidden, normed_two, d_gate, d_up, wd_all
-    )
-
-    g_t, g_n, delta, grad_hidden_own, gain_two_part, dwo = prepare(
-        cot_all, tok_all, branch, grad_two, gains_all, wo_all, out_t, attended
-    )
-    dq_t, dkv, out_own, dwg_own, dwu_own = fifth(
-        q_t, q_n, g_t, g_n, kv_all, log_sum, delta, key_pos, query_pos, out_part, dwg, dwu
+    dwd_own, dwg_own, dwu, out_own, dwo, grad_hidden_own, gain_two_part, dq_t, dkv = backward(
+        two_part.astype(bf16), cot_all, hidden, normed_two, d_gate, d_up, wd_all, tok_all, branch,
+        gains_all, wo_all, out_t, attended, q_t, q_n, kv_all, log_sum, key_pos, query_pos,
     )
     one_part, dwqkv, gain_parts = finish(
         dq_t, dkv, cos_t, sin_t, wqkv_all, normed, tok_all, gain_two_part
     )
-    grad_one, dwq_own, dwkv_all, dwo_own, gain_grads = sixth(one_part, dwqkv, dwo, gain_parts)
+    grad_one, dwq_own, dwkv_all, dwo_own, dwu_own, gain_grads = sixth(
+        one_part, dwqkv, dwo, dwu, gain_parts
+    )
 
     x_own = tokens.astype(f32)
     layer_low = (x_own + own_rows(branch).astype(f32) + out_own).astype(bf16)

time: 451 us -> 420 us (0.931); the launches traced: 443 us -> 419 us
  Pallas kernels: 390 us -> 366 us
    pallas_call x3 -> x1, Pallas kernels: 156 us -> 115 us  [backward(): pl.pallas_call(backward_kernel, out_shape=(shape(own, f32), shape(own, f3...]
    pallas_call x1, Pallas kernels: 45.6 us -> 62.9 us  [sixth(): pl.pallas_call(sixth_kernel, out_shape=(shape((part.shape[0] // 4, part.s...]
where the time goes in v3:
time: 420 us; the launch traced here: 419 us
  Pallas kernels  366 us (87%)
  matrix products  27 us (6%)
  local copies, waits for them, and re-layouts  13.9 us (3%)
  other arithmetic  11.2 us (3%)
    pallas_call x1, Pallas kernels, backward(): pl.pallas_call(backward_kernel, out_shape=(shape(own, f32), shape(own, f3...  115 us
    pallas_call x1, Pallas kernels, third(): pl.pallas_call(third_kernel, out_shape=(shape(part.shape), grown(wg), gro...  71.6 us
    pallas_call x1, Pallas kernels, sixth(): pl.pallas_call(sixth_kernel, out_shape=(shape((part.shape[0] // 4, part.s...  62.9 us
    pallas_call x1, Pallas kernels, second(): pl.pallas_call(second_kernel, out_shape=(shape((heads, hd, rows), f32), s...  53.8 us
    pallas_call x1, Pallas kernels, first(): pl.pallas_call(first_kernel, out_shape=(grown(tok, 4), grown(wqkv, 8), gr...  44.3 us
    pallas_call x1, Pallas kernels, finish(): pl.pallas_call(finish_kernel, out_shape=(shape(tok.shape), shape(wqkv.sha...  10.7 us

profile of v3, /device:TPU:0, one launch (start us, length us, event | category | flops | bytes accessed | tf_op | source)
XLA Modules:
  0.0 418.8 jit_solution(14292080837856792578)
XLA Ops:
  0.6 1.0 constant_dynamic-slice_fusion.4
  1.6 1.8 pad_maximum_fusion.wqkv
  3.4 0.7 broadcast_in_dim.38
  4.1 0.7 broadcast_in_dim.39
  4.7 0.1 pad.10.clone
  4.8 0.7 maximum_maximum_fusion.gains
  5.5 44.3 %gather_first.1 = (bf16[512,2048]{1,0:T(8,128)(2,1)}, bf16[2048,640]{1,0:T(8,128)(2,1)}, bf16[256,256]{1,0:T(8,128)(2,1)}) custom-call(bf16[128,2048]{1,0:T(8,128)(2,1)} %tok.1, bf16[256,640]{1,0:T(8,128)(2,1)} %pad_maximum_fusion.wqkv, bf16[32,256]{1,0:T(8,128)(2,1)} %maximum_maximum_fusion.gains), custom_call_target="tpu_custom_call" | custom-call | tf_op jit(solution)/shard_map/gather_first/pallas_call | solution.py:997
  49.8 0.8 select_reduce_fusion.2
  50.6 1.0 multiply_sine_fusion
  51.6 7.4 %project.1 = (bf16[512,2048]{1,0:T(8,128)(2,1)}, bf16[8,64,512]{2,1,0:T(8,128)(2,1)}, bf16[8,512,64]{2,1,0:T(8,128)(2,1)}, bf16[512,128]{1,0:T(8,128)(2,1)}) custom-call(bf16[512,2048]{1,0:T(8,128)(2,1)} %get-tuple-element.46.tok.tok_all, bf16[2048,640]{1,0:T(8,128)(2,1)} %get-tuple-element.47.wqkv, bf16[256,256]{1,0:T(8,128)(2,1)} %get-tuple-element.48.gains, ...), custom_call_target="tpu_custom_call" | custom-call | flops 1342177280 | bytes 8388608 | tf_op jit(solution)/shard_map/project/pallas_call | solution.py:1062
  59.0 1.3 broadcast_in_dim.76.key_pos
  60.4 0.6 broadcast_in_dim.77.query_pos
  61.0 53.8 %attention_forward.1 = (f32[8,64,512]{2,1,0:T(8,128)}, bf16[512,512]{1,0:T(8,128)(2,1)}, f32[8,1,512]{2,1,0:T(1,128)}, bf16[2048,128]{1,0:T(8,128)(2,1)}, bf16[5...) custom-call(bf16[8,64,512]{2,1,0:T(8,128)(2,1)} %get-tuple-element.49.q_t.q_t_all, ...), custom_call_target="tpu_custom_call" | custom-call | tf_op jit(solution)/shard_map/attention_forward/pallas_call | solution.py:1160
  114.8 4.4 %convolution_convert_fusion.part = bf16[512,2048]{1,0:T(8,128)(2,1)} fusion(bf16[512,512]{1,0:T(8,128)(2,1)} %get-tuple-element.51.attended_all, bf16[2048,512]{1,0:T(8,128)(2,1)} %get-tuple-element.52.wo_all), kind=kOutput, calls=%fused_computation.4 | convolution fusion | flops 1074790400 | bytes 4718592 | tf_op jit(solution)/shard_map/dot_general | solution.py:1663
  119.2 71.6 %sum_branch.1 = (bf16[512,2048]{1,0:T(8,128)(2,1)}, bf16[2048,1408]{1,0:T(8,128)(2,1)}, bf16[2048,1408]{1,0:T(8,128)(2,1)}) custom-call(bf16[512,2048]{1,0:T(8,128)(2,1)} %convolution_convert_fusion.part, bf16[256,1408]{1,0:T(8,128)(2,1)} %wg.1, bf16[256,1408]{1,0:T(8,128)(2,1)} %wd.1), custom_call_target="tpu_custom_call" | custom-call | tf_op jit(solution)/shard_map/sum_branch/pallas_call | solution.py:1195
  190.8 0.0 copy-done.5
  190.8 0.0 copy-start
  190.8 0.0 copy-start.1
  190.8 5.9 %fusion.30 = f32[512,1408]{1,0:T(8,128)S(1)} fusion(bf16[512,2048]{1,0:T(8,128)(2,1)S(1)} %copy-done.5, bf16[2048,1408]{1,0:T(8,128)(2,1)} %get-tuple-element.55.wd_all), kind=kOutput, calls=%fused_computation.98 | convolution fusion | flops 2952790016 | bytes 10747904 | tf_op jit(solution)/shard_map/dot_general | solution.py:1677
  196.7 0.0 copy-done
  196.7 0.0 copy-done.1
  196.7 0.0 copy-start.15
  196.7 0.8 multiply_reduce_fusion
  197.5 1.7 slice_convert_fusion
  199.3 1.1 multiply_convert_fusion.normed_two
  200.3 0.0 copy-start.2
  200.3 0.0 copy-done.15
  200.3 0.0 slice-start.1
  200.3 3.4 fusion.31
  203.8 0.0 copy-done.2
  203.8 0.0 slice-done
  203.8 0.0 slice-done.1
  203.8 5.2 %multiply_convert_fusion.1 = (bf16[512,1408]{1,0:T(8,128)(2,1)}, bf16[512,1408]{1,0:T(8,128)(2,1)S(1)}, bf16[512,1408]{1,0:T(8,128)(2,1)S(1)}) fusion(f32[512,1408]{1,0:T(8,128)S(1)} %fusion.31, f32[512,1408]{1,0:T(8,128)S(1)} %fusion.30, bf16[512,2048]{1,0:T(8,128)(2,1)S(1)} %multiply_convert_fusion.normed_two, bf16[2048,1408]{1,0:T(8,128)(2,1)S(1)} %bitcast.32), kind=kOutput, calls=%fused_computation.5 | convolution fusion | flops 2963603456 | bytes 17956864 | tf_op jit(solution)/shard_map/dot_general | solution.py:1673
  209.0 3.4 fusion.32
  212.5 0.0 copy-done.9
  212.5 0.0 copy-done.10
  212.5 4.7 %add_convert_fusion.part = bf16[512,2048]{1,0:T(8,128)(2,1)} fusion(f32[512,2048]{1,0:T(8,128)S(1)} %fusion.32, bf16[512,1408]{1,0:T(8,128)(2,1)S(1)} %get-tuple-element.113.d_up, bf16[2048,1408]{1,0:T(8,128)(2,1)S(1)} %bitcast.32), kind=kOutput, calls=%fused_computation | convolution fusion | flops 2954887168 | bytes 13500416 | tf_op jit(solution)/shard_map/dot_general | solution.py:1681
  217.2 114.9 %backward.1 = (f32[256,1408]{1,0:T(8,128)}, f32[256,1408]{1,0:T(8,128)}, bf16[2048,1408]{1,0:T(8,128)(2,1)}, f32[128,2048]{1,0:T(8,128)}, bf16[2048,512]{1,0:T(8...) custom-call(bf16[512,2048]{1,0:T(8,128)(2,1)} %add_convert_fusion.part, ...), custom_call_target="tpu_custom_call" | custom-call | tf_op jit(solution)/shard_map/backward/pallas_call | solution.py:1445
  332.1 10.7 %finish_attention.1 = (bf16[512,2048]{1,0:T(8,128)(2,1)}, bf16[2048,640]{1,0:T(8,128)(2,1)}, f32[64,256]{1,0:T(8,128)}) custom-call(bf16[8,64,512]{2,1,0:T(8,128)(2,1)} %get-tuple-element.64.dq_t, f32[512,128]{1,0:T(8,128)} %get-tuple-element.65.dkv, f32[32,512]{1,0:T(8,128)} %get-tuple-element.127.cos_t, f32[32,512]{1,0:T(8,128)} %get-tuple-element.126.sin_t, ...), custom_call_target="tpu_custom_call" | custom-call | flops 2684354560 | bytes 8388608 | tf_op jit(solution)/shard_map/finish_attention/pallas_call | solution.py:1509
  342.8 62.9 %scatter_last.1 = (f32[128,2048]{1,0:T(8,128)}, f32[256,512]{1,0:T(8,128)}, bf16[4,256,128]{2,1,0:T(8,128)(2,1)}, f32[256,512]{1,0:T(8,128)}, f32[256,1408]{1,0:T(8,128)}, /*index=5*/f32[8,256]{1,0:T(8,128)}) custom-call(bf16[512,2048]{1,0:T(8,128)(2,1)} %get-tuple-element.68.part, bf16[2048,640]{1,0:T(8,128)(2,1)} %get-tuple-element.69.dwqkv, ...), custom_call_target="tpu_custom_call" | custom-call | tf_op jit(solution)/shard_map/scatter_last/pallas_call | solution.py:1588
  405.8 1.0 constant_dynamic-slice_fusion.3
  406.8 0.0 copy-start.3
  406.8 0.0 copy-start.4
  406.8 0.0 copy-start.14
  406.8 0.2 slice_bitcast_fusion
  407.0 0.2 copy.27
  407.2 0.8 copy.29
  408.1 0.2 copy.28
  408.3 0.8 copy.30
  409.1 0.0 copy-done.3
  409.1 0.0 copy-done.4
  409.1 0.0 copy-done.14
  409.1 0.3 fusion.3
  409.4 0.0 copy-done.11
  409.4 0.0 copy-start.12
  409.5 0.0 copy-start.7
  409.5 3.0 fusion.9
  412.5 1.4 fusion.29
  413.9 0.8 copy.36
  414.6 0.8 copy.37
  415.4 1.1 copy.38
  416.5 0.0 copy-done.8
  416.5 1.1 copy.39
  417.7 1.1 copy.40
  (26 shorter events, 0.2 us)
Async XLA Ops:
  119.2 71.6 %copy-start.5 = (bf16[512,2048]{1,0:T(8,128)(2,1)S(1)}, bf16[512,2048]{1,0:T(8,128)(2,1)}, u32[]{:S(2)}) copy-start(bf16[512,2048]{1,0:T(8,128)(2,1)} %get-tuple-element.54.cot_all) | copy-start | bytes 6291460
  190.8 5.9 %copy-start = (bf16[512,2048]{1,0:T(8,128)(2,1)S(1)}, bf16[512,2048]{1,0:T(8,128)(2,1)}, u32[]{:S(2)}) copy-start(bf16[512,2048]{1,0:T(8,128)(2,1)} %get-tuple-element.46.tok.tok_all) | copy-start | bytes 6291460
  190.8 5.9 %copy-start.1 = (bf16[512,2048]{1,0:T(8,128)(2,1)S(1)}, bf16[512,2048]{1,0:T(8,128)(2,1)}, u32[]{:S(2)}) copy-start(bf16[512,2048]{1,0:T(8,128)(2,1)} %get-tuple-element.53.branch) | copy-start | bytes 6291460
  196.7 3.6 copy-start.15
  199.3 4.5 %slice-start = ((s8[5767168]{0:T(1024)(128)(4,1)}), s8[4194304]{0:T(1024)(128)(4,1)S(1)}, s32[]{:S(2)}) async-start(s8[5767168]{0:T(1024)(128)(4,1)} %bitcast.31), calls=%async_computation | async-start | bytes 8388608
  200.3 3.5 copy-start.2
  200.3 3.5 slice-start.1
  209.0 3.5 copy-start.9
  209.0 3.5 copy-start.10
  406.8 2.3 copy-start.3
  406.8 2.3 copy-start.4
  406.8 2.3 copy-start.14
  408.1 1.4 copy-start.11
  409.4 4.5 %copy-start.13 = (f32[256,512]{1,0:T(8,128)S(1)}, f32[256,512]{1,0:T(8,128)}, u32[]{:S(2)}) copy-start(f32[256,512]{1,0:T(8,128)} %get-tuple-element.147) | copy-start | bytes 1572868
  409.4 5.2 %copy-start.12 = (f32[256,512]{1,0:T(8,128)S(1)}, f32[256,512]{1,0:T(8,128)}, u32[]{:S(2)}) copy-start(f32[256,512]{1,0:T(8,128)} %get-tuple-element.150) | copy-start | bytes 1572868
  409.5 6.0 %copy-start.7 = (f32[256,1408]{1,0:T(8,128)S(1)}, f32[256,1408]{1,0:T(8,128)}, u32[]{:S(2)}) copy-start(f32[256,1408]{1,0:T(8,128)} %get-tuple-element.151) | copy-start | bytes 4325380
  412.5 4.1 copy-start.8
  415.4 2.2 copy-start.6

commit v4 on v3

--- a/solution.py
+++ b/solution.py
@@ -2,6 +2,7 @@
 
 import jax
 import jax.numpy as jnp
+import numpy as np
 from jax import lax
 from jax.experimental import pallas as pl
 from jax.experimental.pallas import tpu as pltpu
@@ -563,6 +564,11 @@
             self.step()
         self.now = max(self.now, until)
 
+    def until(self, *flags):
+        while not all(flag.up for flag in flags):
+            self.now = max(self.now, self.next_at())
+            self.step()
+
     def finish(self):
         while self.waiting:
             self.step()
@@ -591,7 +597,12 @@
     Order(*tasks).finish()
 
 
-def z_gather(me, src, dst, unit, begin=0.0):
+class Flag:
+    def __init__(self):
+        self.up = False
+
+
+def z_gather(me, src, dst, unit, begin=0.0, done=None):
     rows = src.shape[0]
     z = me.z
 
@@ -600,105 +611,117 @@
 
     ups = [me.slot() for _ in range(3)]
     downs = [me.slot() for _ in range(3)]
-    if begin:
+    own = me.local(src, block(z))
+
+    def up(j):
+        return me.again(ups[j], src if j == 0 else block(z - j), block(z - j), me.up())
+
+    def down(j):
+        return me.again(downs[j], src if j == 0 else block(z + j), block(z + j), me.down())
+
+    def steps():
         yield begin
 
-    @pl.when(z < 3)
-    def _():
-        me.again(ups[0], src, block(z), me.up()).start()
-
-    @pl.when(z > 0)
-    def _():
-        me.again(downs[0], src, block(z), me.down()).start()
-
-    own = me.local(src, block(z))
-    own.start()
-    for j in (1, 2, 3):
-        yield begin + unit * j
-
-        @pl.when(z >= j)
+        @pl.when(z < 3)
         def _():
-            me.again(ups[j - 1], block(z - j), block(z - j), me.up()).wait_recv()
-
-        if j < 3:
+            up(0).start()
+
+        @pl.when(z > 0)
+        def _():
+            down(0).start()
+
+        own.start()
+        for j in (1, 2, 3):
+            yield begin + unit * j
+
+            @pl.when(z >= j)
+            def _():
+                up(j - 1).wait_recv()
+
+            if j < 3:
+
+                @pl.when((z >= j) & (z < 3))
+                def _():
+                    up(j).start()
+
+            @pl.when(z <= 3 - j)
+            def _():
+                down(j - 1).wait_recv()
+
+            if j < 3:
+
+                @pl.when((z <= 3 - j) & (z > 0))
+                def _():
+                    down(j).start()
+
+        own.wait()
+        if done is not None:
+            done.up = True
+        yield begin + unit * 3 + 1.0
+        for j in (0, 1, 2):
 
             @pl.when((z >= j) & (z < 3))
             def _():
-                me.again(ups[j], block(z - j), block(z - j), me.up()).start()
-
-        @pl.when(z <= 3 - j)
-        def _():
-            me.again(downs[j - 1], block(z + j), block(z + j), me.down()).wait_recv()
-
-        if j < 3:
+                up(j).wait_send()
 
             @pl.when((z <= 3 - j) & (z > 0))
             def _():
-                me.again(downs[j], block(z + j), block(z + j), me.down()).start()
-
-    yield begin + unit * 3.2
-    own.wait()
-    for j in (0, 1, 2):
-
-        @pl.when((z >= j) & (z < 3))
-        def _():
-            me.again(ups[j], block(z - j), block(z - j), me.up()).wait_send()
-
-        @pl.when((z <= 3 - j) & (z > 0))
-        def _():
-            me.again(downs[j], block(z + j), block(z + j), me.down()).wait_send()
-
-
-def plane_gather(me, src, dst, unit, begin=0.0):
+                down(j).wait_send()
+
+    return steps()
+
+
+def plane_gather(me, src, dst, unit, begin=0.0, done=None):
     rows = src.shape[0]
     half = rows // 2
 
+    def part(i, h):
+        return dst.at[pl.ds(pl.multiple_of(me.number(i) * rows + h * half, half), half)]
+
     def block(i):
         return dst.at[pl.ds(pl.multiple_of(me.number(i) * rows, rows), rows)]
 
-    def part(i, h):
-        return dst.at[pl.ds(pl.multiple_of(me.number(i) * rows + h * half, half), half)]
-
-    if begin:
-        yield begin
-    heads = src.at[pl.ds(0, half)], src.at[pl.ds(half, half)]
-    x_in, y_in = [], []
-    for h in (0, 1):
-        x_in.append(me.copy(heads[h], part(0, h), me.plane(2)))
-        x_in[h].start()
-        y_in.append(me.copy(heads[1 - h], part(0, 1 - h), me.plane(4)))
-        y_in[h].start()
+    halves = src.at[pl.ds(0, half)], src.at[pl.ds(half, half)]
+    x_in = [me.copy(halves[h], part(0, h), me.plane(2)) for h in (0, 1)]
+    y_in = [me.copy(halves[h], part(0, h), me.plane(4)) for h in (1, 0)]
     to_c = me.copy(src, block(0), me.plane(1))
     own = me.local(src, block(0))
-    to_c.start()
-    own.start()
-    yield begin + unit * 0.5
-    x_in[0].wait_recv()
     x_on = me.copy(part(2, 0), part(2, 0), me.plane(4))
-    x_on.start()
-    y_in[0].wait_recv()
     y_on = me.copy(part(4, 1), part(4, 1), me.plane(2))
-    y_on.start()
-    yield begin + unit
-    x_in[1].wait_recv()
     x_core = me.copy(block(2), block(2), me.plane(1))
-    x_core.start()
-    y_in[1].wait_recv()
     y_core = me.copy(block(4), block(4), me.plane(1))
-    y_core.start()
-    yield begin + unit * 1.5
-    x_on.wait_recv()
-    d0_core = me.copy(part(6, 0), part(6, 0), me.plane(1))
-    d0_core.start()
-    y_on.wait_recv()
-    d1_core = me.copy(part(6, 1), part(6, 1), me.plane(1))
-    d1_core.start()
-    yield begin + unit * 1.5 + 2.0
-    own.wait()
-    for copy in (to_c, x_core, y_core, d0_core, d1_core):
-        copy.wait_recv()
-    for copy in (*x_in, *y_in, to_c, x_on, x_core, y_on, y_core, d0_core, d1_core):
-        copy.wait_send()
+    far = [me.copy(part(6, h), part(6, h), me.plane(1)) for h in (0, 1)]
+
+    def steps():
+        yield begin
+        for copy in (x_in[0], y_in[0], x_in[1], y_in[1], to_c, own):
+            copy.start()
+        yield begin + unit * 0.5
+        x_in[0].wait_recv()
+        x_on.start()
+        y_in[0].wait_recv()
+        y_on.start()
+        yield begin + unit
+        x_in[1].wait_recv()
+        x_core.start()
+        y_in[1].wait_recv()
+        y_core.start()
+        yield begin + unit * 1.5
+        x_on.wait_recv()
+        far[0].start()
+        y_on.wait_recv()
+        far[1].start()
+        yield begin + unit * 1.5 + 2.0
+        own.wait()
+        for copy in (to_c, x_core, y_core, *far):
+            copy.wait_recv()
+        if done is not None:
+            done.up = True
+        yield begin + unit * 1.5 + 2.5
+        for copy in (*x_in, *y_in, to_c, x_on, x_core, y_on, y_core, *far):
+            copy.wait_send()
+
+    return steps()
 
 
 def add_rows(dst, a, b, step=32):
@@ -980,31 +1003,6 @@
     return jax.ShapeDtypeStruct(dims, kind)
 
 
-def first_kernel(tok, wqkv, gains, tok_all, wqkv_all, gains_all, ss, rs):
-    me = Here(ss, rs)
-    me.enter((1, 2, 4))
-    drive(
-        z_gather(me, tok, tok_all, 11.3),
-        plane_gather(me, gains, gains_all, 2.0),
-        plane_gather(me, wqkv, wqkv_all, 7.0),
-    )
-
-
-def first(tok, wqkv, gains):
-    def grown(a, n):
-        return shape((a.shape[0] * n,) + a.shape[1:])
-
-    return pl.pallas_call(
-        first_kernel,
-        out_shape=(grown(tok, 4), grown(wqkv, 8), grown(gains, 8)),
-        in_specs=[VM] * 3,
-        out_specs=[HB] * 3,
-        scratch_shapes=dma_sems(64),
-        compiler_params=params(1),
-        name="gather_first",
-    )(tok, wqkv, gains)
-
-
 def alone(flops, vmem=60 * 2**20):
     return dict(
         compiler_params=pltpu.CompilerParams(vmem_limit_bytes=vmem),
@@ -1013,9 +1011,7 @@
 
 
 def gain_row(gains, which):
-    return jnp.concatenate(
-        [gains[i * 32 : i * 32 + 16, :].astype(f32)[which : which + 1] for i in range(8)], axis=1
-    )
+    return jnp.concatenate([gains[i * 16 + which : i * 16 + which + 1, :] for i in range(8)], axis=1)
 
 
 def rotate_heads(values, cos, sin, inverse=False):
@@ -1030,177 +1026,184 @@
     return jnp.concatenate(out, axis=0)
 
 
-def project_kernel(tok, wqkv, gains, cos_t, sin_t, normed, q_t, q_n, kv_own):
-    heads = q_t.shape[0]
-    wide = heads * HD
-    gain = gain_row(gains, 0)
-
-    def body(i, _):
+def block_positions(order_ref, number, stretch_rows):
+    row = lax.broadcasted_iota(jnp.int32, (stretch_rows, 128), 0)
+    return jnp.concatenate(
+        [row + order_ref[number * 2 + i] * stretch_rows for i in range(2)], axis=0
+    )
+
+
+def forward_kernel(
+    order_ref, tok, w_query, w_key, w_value, gains, frequency, wo, cot, wg, wu, wd,
+    tok_all, wqkv_all, gains_all, wo_all, wg_all, wu_all, wd_all, cot_all, kv_all, branch,
+    normed, q_t, q_n, out_t, attended, log_sum, key_pos, query_pos, cos_t, sin_t,
+    wqkv, gain_src, toks, wqkvs, wos, kv_own, kv, v_t, att_t, part, total, inbox, across, ss, rs
+):
+    me = Here(ss, rs)
+    z = me.z
+    heads, hd, rows = q_t.shape
+    wide = heads * hd
+    keys = kv.shape[0]
+    wqkv[:, :wide] = w_query[...]
+    for j in range(4):
+
+        @pl.when(z == j)
+        def _():
+            wqkv[:, wide : wide + hd] = w_key[:, j * hd : (j + 1) * hd]
+            wqkv[:, wide + hd :] = w_value[:, j * hd : (j + 1) * hd]
+
+    gain_src[...] = jnp.concatenate([gains[...], jnp.zeros((14, gains.shape[1]), f32)], axis=0)
+    me.enter((1, 2, 3, 4))
+    have_tok, have_gains, have_wqkv, have_wo = Flag(), Flag(), Flag(), Flag()
+    progress = Progress(0)
+    order = Order(
+        z_gather(me, tok, toks, 11.3, 0.0, have_tok),
+        plane_gather(me, gain_src, gains_all, 2.0, 0.0, have_gains),
+        plane_gather(me, wqkv, wqkvs, 7.0, 0.1, have_wqkv),
+        plane_gather(me, wo, wos, 6.0, 8.0, have_wo),
+        plane_gather(me, wg, wg_all, 15.5, 17.0),
+        z_gather(me, cot, cot_all, 11.3, 23.5),
+    )
+    c_number = me.x * 2 + me.c
+    for i in range(4):
+        x = 1 - me.x if i & 2 else me.x
+        c = 1 - me.c if i & 1 else me.c
+        key_pos[i * rows : (i + 1) * rows, :] = block_positions(order_ref, x * 2 + c, rows // 2)
+    lane = lax.broadcasted_iota(jnp.int32, (hd // 2, rows // 2), 1)
+    for i in range(2):
+        span = slice(i * rows // 2, (i + 1) * rows // 2)
+        position = lane + order_ref[c_number * 2 + i] * (rows // 2)
+        query_pos[:, span] = position[:8]
+        freq = jnp.concatenate([frequency[...]] * (rows // 256), axis=1)
+        angle = position.astype(f32) * freq
+        cos_t[:, span] = jnp.cos(angle)
+        sin_t[:, span] = jnp.sin(angle)
+    order.until(have_tok, have_gains, have_wqkv)
+    saves = [me.local(toks, tok_all), me.local(wqkvs, wqkv_all)]
+    for save in saves:
+        save.start()
+    gain = gain_row(gains_all, 0)
+
+    def project(i):
         at = pl.ds(pl.multiple_of(i * 128, 128), 128)
-        x = tok[at, :].astype(f32)
+        x = toks[at, :].astype(f32)
         inv = lax.rsqrt(jnp.mean(x * x, axis=1, keepdims=True) + norm_epsilon)
         low = (x * inv * gain).astype(bf16)
         normed[at, :] = low
-        lin = jnp.dot(low, wqkv[...], preferred_element_type=f32).T
+        lin = jnp.dot(low, wqkvs[...], preferred_element_type=f32).T
         cos, sin = cos_t[:, at], sin_t[:, at]
-        turned = rotate_heads(lin[: wide + HD], cos, sin)
-        query = turned[:wide].astype(bf16) * bf16(1.0 / math.sqrt(HD))
-        for h in range(heads):
-            q_t[h, :, at] = query[h * HD : (h + 1) * HD]
+        turned = rotate_heads(lin[: wide + hd], cos, sin)
+        query = turned[:wide].astype(bf16) * bf16(1.0 / math.sqrt(hd))
         natural = query.astype(f32).T
         for h in range(heads):
-            q_n[h, at, :] = natural[:, h * HD : (h + 1) * HD].astype(bf16)
-        kv_own[at, :] = jnp.concatenate([turned[wide:], lin[wide + HD :]], axis=0).T.astype(bf16)
-        return 0
-
-    lax.fori_loop(0, tok.shape[0] // 128, body, 0)
-
-
-def project(tok, wqkv, gains, cos_t, sin_t):
-    rows = tok.shape[0]
-    heads = (wqkv.shape[1] - 2 * HD) // HD
-    return pl.pallas_call(
-        project_kernel,
-        out_shape=(
-            shape(tok.shape),
-            shape((heads, HD, rows)),
-            shape((heads, rows, HD)),
-            shape((rows, 2 * HD)),
-        ),
-        in_specs=[VM] * 5,
-        out_specs=[VM] * 4,
-        name="project",
-        **alone(2 * rows * wqkv.shape[0] * wqkv.shape[1]),
-    )(tok, wqkv, gains, cos_t, sin_t)
-
-
-def attention_forward(me, q_t, kv_own, kv, v_t, key_pos, query_pos, out_t, attended, log_sum, kv_all, per):
-    heads, hd, rows = q_t.shape
-    blocks = kv.shape[0] // rows
+            q_t[h, :, at] = query[h * hd : (h + 1) * hd]
+            q_n[h, at, :] = natural[:, h * hd : (h + 1) * hd].astype(bf16)
+        kv_own[at, :] = jnp.concatenate([turned[wide:], lin[wide + hd :]], axis=0).T.astype(bf16)
+
+    order.loop(rows // 128, 1.9, project)
 
     def block(i):
         return kv.at[pl.ds(i * rows, rows)]
 
     copies = [me.copy(kv_own, block(i), me.plane(i)) for i in (1, 2, 3)]
-    for copy in copies:
+    own = me.local(kv_own, block(0))
+    for copy in (*copies, own):
         copy.start()
-    own = me.local(kv_own, block(0))
-    own.start()
-    yield 0.2
+    order.pump(order.now + 4.0)
+    order.add(plane_gather(me, wu, wu_all, 15.5, order.now))
+    order.add(plane_gather(me, wd, wd_all, 15.5, order.now + 16.0))
     own.wait()
     for copy in copies:
         copy.wait_recv()
     save = me.local(kv, kv_all)
     save.start()
-    for i in range(blocks):
-        v_t[:, i * rows : (i + 1) * rows] = kv[i * rows : (i + 1) * rows, :].astype(f32).T[hd:, :].astype(bf16)
-
-    def one_head(h):
-        q = q_t[h]
-        limit = query_pos[0:1, :]
-
-        def step(i, state):
-            top, total, acc = state
-            at = pl.ds(pl.multiple_of(i * rows, rows), rows)
-            s = jnp.dot(kv[at, 0:hd], q, preferred_element_type=f32)
-            pos = key_pos[at, :]
-            pos = jnp.concatenate([pos] * (rows // 128), axis=1)
-            s = jnp.where(pos <= limit, s, masked_value)
-            new = jnp.maximum(top, jnp.max(s, axis=0, keepdims=True))
-            p = jnp.exp(s - new)
-            factor = jnp.exp(top - new)
-            total = total * factor + jnp.sum(p, axis=0, keepdims=True)
-            acc = acc * factor + jnp.dot(v_t[:, at], p.astype(bf16), preferred_element_type=f32)
-            return new, total, acc
-
-        top, total, acc = lax.fori_loop(
-            0,
-            blocks,
-            step,
-            (
-                jnp.full((1, rows), masked_value, f32),
-                jnp.zeros((1, rows), f32),
-                jnp.zeros((hd, rows), f32),
-            ),
-        )
-        acc = acc / total
-        out_t[h] = acc
-        log_sum[h] = top + jnp.log(total)
-        return acc
-
-    for h in range(0, heads, 2):
-        yield 6.0 + per * h
-        pair = jnp.concatenate([one_head(h), one_head(h + 1)], axis=0)
-        attended[:, h * hd : (h + 2) * hd] = pair.T.astype(bf16)
-    yield 6.0 + per * heads
-    save.wait()
+    for i in range(keys // rows):
+        span = slice(i * rows, (i + 1) * rows)
+        v_t[:, span] = kv[span, :].astype(f32).T[hd:, :].astype(bf16)
+    order.until(have_wo)
+    save_wo = me.local(wos, wo_all)
+    save_wo.start()
+    order.add(
+        z_reduce_all(me, part, total, inbox, across, branch, 45.0, 16, progress, order.now)
+    )
+
+    def item(i):
+        r, h = i // heads, i % heads
+        at = pl.ds(pl.multiple_of(r * 128, 128), 128)
+        s = jnp.dot(kv[:, 0:hd], q_t[h, :, at], preferred_element_type=f32)
+        s = jnp.where(key_pos[...] <= query_pos[0:1, at], s, masked_value)
+        top = jnp.max(s, axis=0, keepdims=True)
+        p = jnp.exp(s - top)
+        norm = jnp.sum(p, axis=0, keepdims=True)
+        o = jnp.dot(v_t[...], p.astype(bf16), preferred_element_type=f32) / norm
+        out_t[h, :, at] = o
+        log_sum[h, :, at] = top + jnp.log(norm)
+        att_t[pl.ds(pl.multiple_of(h * hd, hd), hd), :] = o
+
+        @pl.when(h == heads - 1)
+        def _():
+            natural = att_t[...].T.astype(bf16)
+            attended[at, :] = natural
+            part[at, :] = contract_last_dims(natural, wos[...]).astype(bf16)
+
+    def before(k):
+        progress.parts = k // heads * 4
+        return False
+
+    order.loop(heads * rows // 128, 0.75, item, before)
+    progress.parts = 16
+    order.finish()
     for copy in copies:
         copy.wait_send()
-
-
-def second_kernel(
-    q_t, kv_own, key_pos, query_pos, cot, wo, wu,
-    out_t, attended, log_sum, kv_all, cot_all, wo_all, wu_all, kv, v_t, ss, rs
-):
-    me = Here(ss, rs)
-    me.enter((1, 2, 3, 4))
-    drive(
-        attention_forward(
-            me, q_t, kv_own, kv, v_t, key_pos, query_pos, out_t, attended, log_sum, kv_all, 4.0
+    for copy in (save, save_wo, *saves):
+        copy.wait()
+
+
+def forward(stretch_order, tok, w_query, w_key, w_value, gains, frequency, wo, cot, wg, wu, wd):
+    rows = tok.shape[0] * 4
+    width = tok.shape[1]
+    heads = w_query.shape[1] // HD
+    keys = rows * 4
+    qkv = (w_query.shape[0], w_query.shape[1] + 2 * HD)
+
+    def grown(a, n=8):
+        return shape((a.shape[0] * n,) + a.shape[1:], a.dtype)
+
+    def room(a):
+        return pltpu.VMEM(a.shape, a.dtype)
+
+    gain_block = shape((16, gains.shape[1]), f32)
+    wqkv = shape(qkv)
+    block = shape((rows, width))
+    return pl.pallas_call(
+        forward_kernel,
+        out_shape=(
+            block, grown(wqkv), grown(gain_block), grown(wo), grown(wg), grown(wu), grown(wd), block,
+            shape((keys, 2 * HD)), block,
+            block,
+            shape((heads, HD, rows)),
+            shape((heads, rows, HD)),
+            shape((heads, HD, rows), f32),
+            shape((rows, heads * HD)),
+            shape((heads, 1, rows), f32),
+            shape((keys, 128), jnp.int32),
+            shape((8, rows), jnp.int32),
+            shape((HD // 2, rows), f32),
+            shape((HD // 2, rows), f32),
         ),
-        z_gather(me, cot, cot_all, 11.3, 0.1),
-        plane_gather(me, wo, wo_all, 6.0, 0.3),
-        plane_gather(me, wu, wu_all, 15.5, 6.0),
-    )
-
-
-def second(q_t, kv_own, key_pos, query_pos, cot, wo, wu):
-    heads, hd, rows = q_t.shape
-    keys = key_pos.shape[0]
-    return pl.pallas_call(
-        second_kernel,
-        out_shape=(
-            shape((heads, hd, rows), f32),
-            shape((rows, heads * hd)),
-            shape((heads, 1, rows), f32),
-            shape((keys, 2 * hd)),
-            shape((cot.shape[0] * 4, cot.shape[1])),
-            shape((wo.shape[0] * 8, wo.shape[1])),
-            shape((wu.shape[0] * 8, wu.shape[1])),
-        ),
-        in_specs=[VM] * 7,
-        out_specs=[VM] * 3 + [HB] * 4,
-        scratch_shapes=[pltpu.VMEM((keys, 2 * hd), bf16), pltpu.VMEM((hd, keys), bf16)] + dma_sems(64),
-        compiler_params=params(2),
-        name="attention_forward",
-    )(q_t, kv_own, key_pos, query_pos, cot, wo, wu)
-
-
-def third_kernel(part, wg, wd, total_out, wg_all, wd_all, total, inbox, across, ss, rs):
-    me = Here(ss, rs)
-    me.enter((1, 2, 4))
-    drive(
-        z_reduce_all(me, part, total, inbox, across, total_out, 45.0, 16, Progress(16)),
-        plane_gather(me, wg, wg_all, 15.5, 0.1),
-        plane_gather(me, wd, wd_all, 15.5, 15.0),
-    )
-
-
-def third(part, wg, wd):
-    rows = pltpu.VMEM(part.shape, bf16)
-
-    def grown(a):
-        return shape((a.shape[0] * 8, a.shape[1]))
-
-    return pl.pallas_call(
-        third_kernel,
-        out_shape=(shape(part.shape), grown(wg), grown(wd)),
-        in_specs=[VM] * 3,
-        out_specs=[HB] * 3,
-        scratch_shapes=[rows] * 3 + dma_sems(96),
-        compiler_params=params(3),
-        name="sum_branch",
-    )(part, wg, wd)
+        in_specs=[pl.BlockSpec(memory_space=pltpu.SMEM)] + [VM] * 7 + [HB] * 4,
+        out_specs=[HB, HB, VM] + [HB] * 7 + [VM] * 10,
+        scratch_shapes=[
+            room(wqkv), room(gain_block), room(block), room(grown(wqkv)), room(grown(wo)),
+            pltpu.VMEM((rows, 2 * HD), bf16),
+            pltpu.VMEM((keys, 2 * HD), bf16),
+            pltpu.VMEM((HD, keys), bf16),
+            pltpu.VMEM((heads * HD, 128), f32),
+            room(block), room(block), room(block), room(block),
+        ] + dma_sems(192),
+        compiler_params=params(1),
+        name="forward",
+    )(stretch_order, tok, w_query, w_key, w_value, gains, frequency, wo, cot, wg, wu, wd)
 
 
 def contract_rows(left, right):
@@ -1620,52 +1623,26 @@
 ):
     row_count, width = tokens.shape
     groups = 4
-    head_rows = row_count * groups
-    stretch_rows = head_rows // 2
     cols = width // 8
     contract_last = (((1,), (1,)), ((), ()))
     z = lax.axis_index("head")
-    b = lax.axis_index("blk")
     own_first = z * row_count
 
     def own_rows(values):
         return lax.dynamic_slice_in_dim(values, own_first, row_count, 0)
 
-    query_positions = stretch_positions(stretch_order, b * head_rows, head_rows, stretch_rows)
-    key_positions = jnp.concatenate(
-        [
-            stretch_positions(stretch_order, jnp.bitwise_xor(b, i) * head_rows, head_rows, stretch_rows)
-            for i in range(4)
-        ]
-    )
-    key_pos = jnp.broadcast_to(key_positions[:, None], (key_positions.shape[0], 128))
-    query_pos = jnp.broadcast_to(query_positions[None, :], (8, head_rows))
-    half = HD // 2
-    frequency = rope_base ** (-(jnp.arange(half, dtype=f32) * (2.0 / HD)))
-    angles = frequency[:, None] * query_positions.astype(f32)[None, :]
-    cos_t, sin_t = jnp.cos(angles), jnp.sin(angles)
-
-    slot_first = z * HD
-    w_qkv = jnp.concatenate(
-        [
-            w_query,
-            lax.dynamic_slice_in_dim(w_key, slot_first, HD, 1),
-            lax.dynamic_slice_in_dim(w_value, slot_first, HD, 1),
-        ],
-        axis=1,
-    )
-    gains = jnp.concatenate([gain_attn[None], gain_mlp[None], jnp.zeros((30, cols), bf16)])
-    tok_all, wqkv_all, gains_all = first(tokens, w_qkv, gains)
-    normed, q_t, q_n, kv_own = project(tok_all, wqkv_all, gains_all, cos_t, sin_t)
-    out_t, attended, log_sum, kv_all, cot_all, wo_all, wu_all = second(
-        q_t, kv_own, key_pos, query_pos, cotangent, w_out, w_up
-    )
-    branch_part = lax.dot_general(attended, wo_all, contract_last, preferred_element_type=f32).astype(bf16)
-    branch, wg_all, wd_all = third(branch_part, w_gate, w_down)
-
-    gain_rows = gains_all.reshape(8, 32, cols)
-    gain_one = gain_rows[:, 0].reshape(width).astype(f32)
-    gain_two = gain_rows[:, 1].reshape(width).astype(f32)
+    frequency = rope_base ** (-(np.arange(HD // 2, dtype=np.float32) * np.float32(2.0 / HD)))
+    frequency = jnp.asarray(np.broadcast_to(frequency.astype(np.float32)[:, None], (HD // 2, 128)))
+    gains = jnp.concatenate([gain_attn[None], gain_mlp[None]]).astype(f32)
+    (
+        tok_all, wqkv_all, gains_all, wo_all, wg_all, wu_all, wd_all, cot_all, kv_all, branch,
+        normed, q_t, q_n, out_t, attended, log_sum, key_pos, query_pos, cos_t, sin_t,
+    ) = forward(
+        stretch_order, tokens, w_query, w_key, w_value, gains, frequency, w_out, cotangent, w_gate, w_up, w_down
+    )
+    gain_rows = gains_all.reshape(8, 16, cols)
+    gain_one = gain_rows[:, 0].reshape(width)
+    gain_two = gain_rows[:, 1].reshape(width)
     hidden_rows = tok_all.astype(f32) + branch.astype(f32)
     inv_mlp = lax.rsqrt(jnp.mean(hidden_rows * hidden_rows, axis=-1, keepdims=True) + norm_epsilon)
     normed_two = (hidden_rows * inv_mlp * gain_two).astype(bf16)

time: 420 us -> 387 us (0.921)
  Pallas kernels: 366 us -> 343 us
  matrix products: 27 us -> 20.2 us
    pallas_call x4 -> x1, Pallas kernels: 177 us -> 155 us  [forward(): pl.pallas_call(forward_kernel, out_shape=(block, grown(wqkv), grown(gain_...]
    dot_general x1 -> x0, matrix products: 4.35 us -> none  [local_fast(): lax.dot_general(attended, wo_all, contract_last, preferred_element_type=f32)]
where the time goes in v4:
time: 387 us
  Pallas kernels  343 us (89%)
  matrix products  20.2 us (5%)
  local copies, waits for them, and re-layouts  14.6 us (4%)
  other arithmetic  8.11 us (2%)
    pallas_call x1, Pallas kernels, forward(): pl.pallas_call(forward_kernel, out_shape=(block, grown(wqkv), grown(gain_...  155 us
    pallas_call x1, Pallas kernels, backward(): pl.pallas_call(backward_kernel, out_shape=(shape(own, f32), shape(own, f3...  113 us
    pallas_call x1, Pallas kernels, sixth(): pl.pallas_call(sixth_kernel, out_shape=(shape((part.shape[0] // 4, part.s...  64.5 us
    pallas_call x1, Pallas kernels, finish(): pl.pallas_call(finish_kernel, out_shape=(shape(tok.shape), shape(wqkv.sha...  10.7 us

profile of v4, /device:TPU:0, one launch (start us, length us, event | category | flops | bytes accessed | tf_op | source)
XLA Modules:
  0.0 386.6 jit_solution(14812663795195672914)
XLA Ops:
  0.6 0.7 broadcast_in_dim.10
  1.3 0.7 broadcast_in_dim.4
  2.0 0.6 maximum_convert_fusion.1.gains
  2.5 1.3 jit_solution_.3.frequency
  3.9 154.8 %forward.1 = (bf16[512,2048]{1,0:T(8,128)(2,1)}, bf16[2048,640]{1,0:T(8,128)(2,1)}, f32[128,256]{1,0:T(8,128)}, bf16[2048,512]{1,0:T(8,128)(2,1)}, bf16[2048,140...) custom-call(s32[8]{0:T(128)} %order_ref.1, ...), custom_call_target="tpu_custom_call" | custom-call | tf_op jit(solution)/shard_map/forward/pallas_call | solution.py:1178
  158.7 0.0 copy-start
  158.7 0.0 copy-start.1
  158.7 0.0 copy-start.15
  158.7 3.1 multiply_reduce_fusion
  161.8 2.2 fusion.11
  164.1 0.0 copy-done
  164.1 0.0 copy-done.1
  164.1 0.0 slice-start
  164.1 1.0 multiply_convert_fusion.normed_two
  165.1 0.0 copy-start.2
  165.2 0.0 copy-done.15
  165.2 0.0 slice-start.1
  165.2 0.0 copy-start.5
  165.2 0.0 slice-start.2
  165.2 3.4 fusion.14
  168.6 0.0 slice-start.3
  168.6 0.0 slice-done
  168.6 0.0 slice-done.1
  168.7 0.2 copy-done.5
  168.8 3.4 fusion.13
  172.3 0.0 copy-done.2
  172.3 0.0 slice-done.2
  172.3 0.0 slice-done.3
  172.3 5.2 %multiply_convert_fusion.1 = (bf16[512,1408]{1,0:T(8,128)(2,1)}, bf16[512,1408]{1,0:T(8,128)(2,1)S(1)}, bf16[512,1408]{1,0:T(8,128)(2,1)S(1)}) fusion(f32[512,1408]{1,0:T(8,128)S(1)} %fusion.14, f32[512,1408]{1,0:T(8,128)S(1)} %fusion.13, bf16[512,2048]{1,0:T(8,128)(2,1)S(1)} %multiply_convert_fusion.normed_two, bf16[2048,1408]{1,0:T(8,128)(2,1)S(1)} %bitcast.32), kind=kOutput, calls=%fused_computation.4 | convolution fusion | flops 2963603456 | bytes 17956864 | tf_op jit(solution)/shard_map/dot_general | solution.py:1650
  177.5 3.4 fusion.15
  180.9 0.0 copy-done.9
  180.9 0.0 copy-done.10
  181.0 4.7 %add_convert_fusion.part = bf16[512,2048]{1,0:T(8,128)(2,1)} fusion(f32[512,2048]{1,0:T(8,128)S(1)} %fusion.15, bf16[512,1408]{1,0:T(8,128)(2,1)S(1)} %get-tuple-element.102.d_up, bf16[2048,1408]{1,0:T(8,128)(2,1)S(1)} %bitcast.32), kind=kOutput, calls=%fused_computation | convolution fusion | flops 2954887168 | bytes 13500416 | tf_op jit(solution)/shard_map/dot_general | solution.py:1658
  185.7 112.7 %backward.1 = (f32[256,1408]{1,0:T(8,128)}, f32[256,1408]{1,0:T(8,128)}, bf16[2048,1408]{1,0:T(8,128)(2,1)}, f32[128,2048]{1,0:T(8,128)}, bf16[2048,512]{1,0:T(8...) custom-call(bf16[512,2048]{1,0:T(8,128)(2,1)} %add_convert_fusion.part, ...), custom_call_target="tpu_custom_call" | custom-call | tf_op jit(solution)/shard_map/backward/pallas_call | solution.py:1448
  298.4 10.7 %finish_attention.1 = (bf16[512,2048]{1,0:T(8,128)(2,1)}, bf16[2048,640]{1,0:T(8,128)(2,1)}, f32[64,256]{1,0:T(8,128)}) custom-call(bf16[8,64,512]{2,1,0:T(8,128)(2,1)} %get-tuple-element.67.dq_t, f32[512,128]{1,0:T(8,128)} %get-tuple-element.68.dkv, f32[32,512]{1,0:T(8,128)} %get-tuple-element.69.cos_t, f32[32,512]{1,0:T(8,128)} %get-tuple-element.70.sin_t, ...), custom_call_target="tpu_custom_call" | custom-call | flops 2684354560 | bytes 8388608 | tf_op jit(solution)/shard_map/finish_attention/pallas_call | solution.py:1512
  309.0 64.5 %scatter_last.1 = (f32[128,2048]{1,0:T(8,128)}, f32[256,512]{1,0:T(8,128)}, bf16[4,256,128]{2,1,0:T(8,128)(2,1)}, f32[256,512]{1,0:T(8,128)}, f32[256,1408]{1,0:T(8,128)}, /*index=5*/f32[8,256]{1,0:T(8,128)}) custom-call(bf16[512,2048]{1,0:T(8,128)(2,1)} %get-tuple-element.74.part, bf16[2048,640]{1,0:T(8,128)(2,1)} %get-tuple-element.75.dwqkv, ...), custom_call_target="tpu_custom_call" | custom-call | tf_op jit(solution)/shard_map/scatter_last/pallas_call | solution.py:1591
  373.7 1.0 constant_dynamic-slice_fusion.3
  374.6 0.0 copy-start.3
  374.6 0.0 copy-start.4
  374.6 0.0 copy-start.14
  374.7 0.2 slice_bitcast_fusion
  374.9 0.2 copy.24
  375.1 0.8 copy.26
  375.9 0.2 copy.25
  376.1 0.8 copy.27
  377.0 0.0 copy-done.3
  377.0 0.0 copy-done.4
  377.0 0.0 copy-done.14
  377.0 0.3 fusion.3
  377.3 0.0 copy-done.11
  377.3 0.0 copy-start.12
  377.3 0.0 copy-start.7
  377.3 3.0 fusion.9
  380.3 1.4 fusion.12
  381.7 0.0 copy-done.13
  381.7 0.8 copy.33
  382.5 0.0 copy-done.12
  382.5 0.8 copy.34
  383.3 0.0 copy-done.7
  383.3 1.1 copy.35
  384.4 0.0 copy-done.8
  384.4 1.1 copy.36
  385.5 0.0 copy-done.6
  385.5 1.1 copy.37
  (11 shorter events, 0.1 us)
Async XLA Ops:
  158.7 5.4 %copy-start = (bf16[512,2048]{1,0:T(8,128)(2,1)S(1)}, bf16[512,2048]{1,0:T(8,128)(2,1)}, u32[]{:S(2)}) copy-start(bf16[512,2048]{1,0:T(8,128)(2,1)} %get-tuple-element.49.branch) | copy-start | bytes 6291460
  158.7 5.4 %copy-start.1 = (bf16[512,2048]{1,0:T(8,128)(2,1)S(1)}, bf16[512,2048]{1,0:T(8,128)(2,1)}, u32[]{:S(2)}) copy-start(bf16[512,2048]{1,0:T(8,128)(2,1)} %get-tuple-element.52.tok_all.tok) | copy-start | bytes 6291460
  158.7 6.5 %copy-start.15 = (bf16[2048,1408]{1,0:T(8,128)(2,1)S(1)}, bf16[2048,1408]{1,0:T(8,128)(2,1)}, u32[]{:S(2)}) copy-start(bf16[2048,1408]{1,0:T(8,128)(2,1)} %get-tuple-element.55) | copy-start | bytes 17301508
  164.1 4.6 %slice-start = ((s8[5767168]{0:T(1024)(128)(4,1)}), s8[1572864]{0:T(1024)(128)(4,1)S(1)}, s32[]{:S(2)}) async-start(s8[5767168]{0:T(1024)(128)(4,1)} %bitcast.21), calls=%async_computation | async-start | bytes 3145728
  165.1 7.1 %copy-start.2 = (bf16[512,2048]{1,0:T(8,128)(2,1)}, bf16[512,2048]{1,0:T(8,128)(2,1)S(1)}, u32[]{:S(2)}) copy-start(bf16[512,2048]{1,0:T(8,128)(2,1)S(1)} %multiply_convert_fusion.normed_two) | copy-start | bytes 6291460
  165.2 3.5 slice-start.1
  165.2 3.6 copy-start.5
  165.2 7.1 %slice-start.2 = ((s8[5767168]{0:T(1024)(128)(4,1)}), s8[4194304]{0:T(1024)(128)(4,1)S(1)}, s32[]{:S(2)}) async-start(s8[5767168]{0:T(1024)(128)(4,1)} %bitcast.31), calls=%async_computation.2 | async-start | bytes 8388608
  168.6 3.6 slice-start.3
  177.5 3.5 copy-start.9
  177.5 3.5 copy-start.10
  374.6 2.3 copy-start.3
  374.6 2.3 copy-start.4
  374.6 2.3 copy-start.14
  375.9 1.4 copy-start.11
  377.3 4.4 %copy-start.13 = (f32[256,512]{1,0:T(8,128)S(1)}, f32[256,512]{1,0:T(8,128)}, u32[]{:S(2)}) copy-start(f32[256,512]{1,0:T(8,128)} %get-tuple-element.130) | copy-start | bytes 1572868
  377.3 5.2 %copy-start.12 = (f32[256,512]{1,0:T(8,128)S(1)}, f32[256,512]{1,0:T(8,128)}, u32[]{:S(2)}) copy-start(f32[256,512]{1,0:T(8,128)} %get-tuple-element.133) | copy-start | bytes 1572868
  377.3 6.0 %copy-start.7 = (f32[256,1408]{1,0:T(8,128)S(1)}, f32[256,1408]{1,0:T(8,128)}, u32[]{:S(2)}) copy-start(f32[256,1408]{1,0:T(8,128)} %get-tuple-element.134) | copy-start | bytes 4325380
  380.3 4.1 %copy-start.8 = (f32[256,1408]{1,0:T(8,128)S(1)}, f32[256,1408]{1,0:T(8,128)}, u32[]{:S(2)}) copy-start(f32[256,1408]{1,0:T(8,128)} %get-tuple-element.135) | copy-start | bytes 4325380
  383.3 2.2 copy-start.6

commit v5 on v4

--- a/solution.py
+++ b/solution.py
@@ -512,6 +512,22 @@
         self.used += 1
         return pltpu.make_async_copy(src, dst, self.send_sem.at[k])
 
+    def free_in_plane(self, sem):
+        for i in (1, 2, 4):
+            pl.semaphore_signal(sem, inc=1, device_id=self.plane(i), device_id_type=MESH)
+
+    def free_along_z(self, sem):
+        @pl.when(self.z > 0)
+        def _():
+            pl.semaphore_signal(sem, inc=1, device_id=self.down(), device_id_type=MESH)
+
+        @pl.when(self.z < 3)
+        def _():
+            pl.semaphore_signal(sem, inc=1, device_id=self.up(), device_id_type=MESH)
+
+    def wait_along_z(self, sem):
+        pl.semaphore_wait(sem, jnp.where(self.z > 0, 1, 0) + jnp.where(self.z < 3, 1, 0))
+
     def enter(self, offsets, along_z=True, all_z=False):
         bar = pltpu.get_barrier_semaphore()
         for i in offsets:
@@ -602,76 +618,84 @@
         self.up = False
 
 
-def z_gather(me, src, dst, unit, begin=0.0, done=None):
+def z_gather(me, src, dst, unit, begin=0.0, done=None, issue=None):
     rows = src.shape[0]
+    half = rows // 2
     z = me.z
 
-    def block(j):
-        return dst.at[pl.ds(pl.multiple_of(j * rows, rows), rows)]
-
-    ups = [me.slot() for _ in range(3)]
-    downs = [me.slot() for _ in range(3)]
-    own = me.local(src, block(z))
-
-    def up(j):
-        return me.again(ups[j], src if j == 0 else block(z - j), block(z - j), me.up())
-
-    def down(j):
-        return me.again(downs[j], src if j == 0 else block(z + j), block(z + j), me.down())
+    def block(j, h):
+        return dst.at[pl.ds(pl.multiple_of(j * rows + h * half, half), half)]
+
+    ups = [me.slot() for _ in range(6)]
+    downs = [me.slot() for _ in range(6)]
+    own = me.local(src, dst.at[pl.ds(pl.multiple_of(z * rows, rows), rows)])
+
+    def up(j, h):
+        mine = src.at[pl.ds(h * half, half)] if j == 0 else block(z - j, h)
+        return me.again(ups[2 * j + h], mine, block(z - j, h), me.up())
+
+    def down(j, h):
+        mine = src.at[pl.ds(h * half, half)] if j == 0 else block(z + j, h)
+        return me.again(downs[2 * j + h], mine, block(z + j, h), me.down())
 
     def steps():
-        yield begin
+        yield begin if issue is None else issue
 
         @pl.when(z < 3)
         def _():
-            up(0).start()
+            up(0, 0).start()
+            up(0, 1).start()
 
         @pl.when(z > 0)
         def _():
-            down(0).start()
+            down(0, 0).start()
+            down(0, 1).start()
 
         own.start()
         for j in (1, 2, 3):
-            yield begin + unit * j
-
-            @pl.when(z >= j)
-            def _():
-                up(j - 1).wait_recv()
-
-            if j < 3:
-
-                @pl.when((z >= j) & (z < 3))
+            for h in (0, 1):
+                yield begin + unit * (j - 0.5 + h * 0.5) + 1.8 + 0.4 * j
+
+                @pl.when(z >= j)
                 def _():
-                    up(j).start()
-
-            @pl.when(z <= 3 - j)
-            def _():
-                down(j - 1).wait_recv()
-
-            if j < 3:
-
-                @pl.when((z <= 3 - j) & (z > 0))
+                    up(j - 1, h).wait_recv()
+
+                if j < 3:
+
+                    @pl.when((z >= j) & (z < 3))
+                    def _():
+                        up(j, h).start()
+
+                @pl.when(z <= 3 - j)
                 def _():
-                    down(j).start()
+                    down(j - 1, h).wait_recv()
+
+                if j < 3:
+
+                    @pl.when((z <= 3 - j) & (z > 0))
+                    def _():
+                        down(j, h).start()
 
         own.wait()
         if done is not None:
             done.up = True
-        yield begin + unit * 3 + 1.0
+        yield begin + unit * 3 + 15.0
         for j in (0, 1, 2):
 
             @pl.when((z >= j) & (z < 3))
             def _():
-                up(j).wait_send()
+                up(j, 0).wait_send()
+                up(j, 1).wait_send()
 
             @pl.when((z <= 3 - j) & (z > 0))
             def _():
-                down(j).wait_send()
+                down(j, 0).wait_send()
+                down(j, 1).wait_send()
 
     return steps()
 
 
-def plane_gather(me, src, dst, unit, begin=0.0, done=None):
+def plane_gather(me, src, dst, unit, begin=0.0, done=None, issue=None):
     rows = src.shape[0]
     half = rows // 2
 
@@ -693,32 +717,53 @@
     far = [me.copy(part(6, h), part(6, h), me.plane(1)) for h in (0, 1)]
 
     def steps():
-        yield begin
+        yield begin if issue is None else issue
         for copy in (x_in[0], y_in[0], x_in[1], y_in[1], to_c, own):
             copy.start()
-        yield begin + unit * 0.5
+        yield begin + unit * 0.5 + 2.0
         x_in[0].wait_recv()
         x_on.start()
         y_in[0].wait_recv()
         y_on.start()
-        yield begin + unit
+        yield begin + unit + 2.5
         x_in[1].wait_recv()
         x_core.start()
         y_in[1].wait_recv()
         y_core.start()
-        yield begin + unit * 1.5
+        yield begin + unit * 1.5 + 4.5
         x_on.wait_recv()
         far[0].start()
         y_on.wait_recv()
         far[1].start()
-        yield begin + unit * 1.5 + 2.0
+        yield begin + unit * 1.5 + 6.5
         own.wait()
         for copy in (to_c, x_core, y_core, *far):
             copy.wait_recv()
         if done is not None:
             done.up = True
-        yield begin + unit * 1.5 + 2.5
+        yield begin + unit * 1.5 + 15.0
         for copy in (*x_in, *y_in, to_c, x_on, x_core, y_on, y_core, *far):
+            copy.wait_send()
+
+    return steps()
+
+
+def plane_direct(me, src, dst, done):
+    rows = src.shape[0]
+    place = dst.at[pl.ds(pl.multiple_of(me.number(0) * rows, rows), rows)]
+    copies = [me.copy(src, place, me.plane(i)) for i in range(1, 8)]
+    own = me.local(src, place)
+
+    def steps():
+        for copy in (*copies, own):
+            copy.start()
+        yield 5.0
+        own.wait()
+        for copy in copies:
+            copy.wait_recv()
+        done.up = True
+        yield 15.0
+        for copy in copies:
             copy.wait_send()
 
     return steps()
@@ -737,16 +782,20 @@
 
 class Progress:
     def __init__(self, parts):
-        self.parts, self.whole = parts, 0
+        self.parts, self.entered, self.crossed, self.left = parts, 0, 0, 0
+        self.sent_in, self.sent_out = Flag(), Flag()
+
+    def whole(self):
+        return min(self.crossed, self.left)
 
 
 def z_reduce_all(me, part, total, inbox, across, out, unit, chunks, progress, begin=0.0):
     rows = part.shape[0] // chunks
-    end, middle = me.end, me.middle
     first = [me.slot() for _ in range(chunks)]
     second = [me.slot() for _ in range(chunks)]
     third = [me.slot() for _ in range(chunks)]
     store = [me.slot() for _ in range(chunks)]
+    hop = unit / chunks
 
     def at(ref, k):
         return ref.at[pl.ds(k * rows, rows)]
@@ -761,68 +810,97 @@
         return me.again(third[k], at(total, k), at(total, k), me.outward)
 
     def put(k):
-        if out is not None:
-            return pltpu.make_async_copy(at(total, k), at(out, k), me.send_sem.at[store[k]])
-
-    yield begin
-    hop = unit / chunks
-    time, sent = begin, 0
-    for k in range(chunks + 2):
-        while min(k, chunks - 1) >= progress.parts:
-            time += 1.0
+        return pltpu.make_async_copy(at(total, k), at(out, k), me.send_sem.at[store[k]])
+
+    def entering():
+        yield begin
+        time, sent = begin, 0
+        for k in range(chunks):
+            while k >= progress.parts:
+                time += 0.5
+                yield time
+            new, sent = range(sent, progress.parts), progress.parts
+            if len(new):
+
+                @pl.when(me.end)
+                def _():
+                    for j in new:
+                        send_in(j).start()
+
+            time = max(time, begin + 2.0) + hop
             yield time
-        new = range(sent, min(progress.parts, chunks))
-        sent = max(sent, min(progress.parts, chunks))
-        if len(new):
-
-            @pl.when(end)
+
+            @pl.when(me.middle)
             def _():
-                for j in new:
-                    send_in(j).start()
-
-        time = max(time + hop, begin + hop * (k + 1) + 2.0)
-        yield time
-
-        @pl.when(middle)
-        def _():
-            if k < chunks:
                 send_in(k).wait_recv()
                 add_rows(at(inbox, k), at(part, k), at(inbox, k))
                 send_across(k).start()
-            if 1 <= k <= chunks:
-                send_across(k - 1).wait_recv()
-                add_rows(at(total, k - 1), at(inbox, k - 1), at(across, k - 1))
-                send_out(k - 1).start()
+
+            progress.entered = k + 1
+        yield time + 20.0
+
+        @pl.when(me.end)
+        def _():
+            for k in range(chunks):
+                send_in(k).wait_send()
+
+        progress.sent_in.up = True
+
+    def crossing():
+        yield begin
+        time = begin
+        for k in range(chunks):
+            while k >= progress.entered:
+                time += 0.5
+                yield time
+            time = max(time, begin + 4.0 + hop) + hop
+            yield time
+
+            @pl.when(me.middle)
+            def _():
+                send_across(k).wait_recv()
+                add_rows(at(total, k), at(inbox, k), at(across, k))
+                send_out(k).start()
                 if out is not None:
-                    put(k - 1).start()
-
-        @pl.when(end)
+                    put(k).start()
+
+            progress.crossed = k + 1
+        yield time + 10.0
+
+        @pl.when(me.middle)
         def _():
-            if k >= 2:
-                send_out(k - 2).wait_recv()
+            for k in range(chunks):
+                send_across(k).wait_send()
+                send_out(k).wait_send()
+
+        progress.sent_out.up = True
+
+    def leaving():
+        yield begin
+        time = begin
+        for k in range(chunks):
+            while k >= progress.crossed:
+                time += 0.5
+                yield time
+            time = max(time, begin + 6.0 + 2 * hop) + hop
+            yield time
+
+            @pl.when(me.end)
+            def _():
+                send_out(k).wait_recv()
                 if out is not None:
-                    put(k - 2).start()
-
-        progress.whole = max(0, k - 1)
-    yield time + 1.0
-
-    @pl.when(end)
-    def _():
-        for k in range(chunks):
-            send_in(k).wait_send()
-
-    @pl.when(middle)
-    def _():
-        for k in range(chunks):
-            send_across(k).wait_send()
-            send_out(k).wait_send()
-
-    if out is not None:
-        for k in range(chunks):
-            put(k).wait()
-
-
-def z_reduce_scatter(me, part, from_below, from_above, own, unit, begin=0.0):
+                    put(k).start()
+
+            progress.left = k + 1
+        if out is not None:
+            yield time + 2.0
+            for k in range(chunks):
+                put(k).wait()
+
+    return entering(), crossing(), leaving()
+
+
+def z_reduce_scatter(me, part, from_below, from_above, own, unit, begin=0.0, done=None):
     rows = part.shape[0] // 4
     z = me.z
     ups = [me.slot() for _ in range(4)]
@@ -899,6 +977,9 @@
                 if i < j:
                     down(i, part).wait_send()
 
+    if done is not None:
+        done.up = True
+
 
 def offsets_of(me, j):
     dx, dy, dc = 1 - (j % 4) // 2, 1 - j % 2, 1 - j // 4
@@ -922,6 +1003,7 @@
 
 class PlaneScatter:
     def __init__(self, me, scratch):
+        self.me = me
         self.blocks, self.other, self.over_x, self.over_y, self.last_y, self.last_x = scratch
         blocks, rows = self.blocks, self.blocks.shape[1]
         half = rows // 2
@@ -935,7 +1017,7 @@
         self.to_y = me.copy(blocks.at[6, first], self.last_y, me.plane(4))
         self.to_x = me.copy(blocks.at[5, second], self.last_x, me.plane(2))
 
-    def steps(self, out, unit, begin):
+    def steps(self, out, unit, begin, done, free=None):
         blocks, half, first, second = self.blocks, self.half, self.first, self.second
         for j in range(4):
             yield begin + 0.3 * j
@@ -970,27 +1052,9 @@
         lax.fori_loop(0, half // 32, body, 0)
         for copy in (*self.core, self.far_x, self.far_y, self.near_x, self.near_y, self.to_y, self.to_x):
             copy.wait_send()
-
-
-def plane_scatter(me, src, out, scratch, unit, begin=0.0):
-    scatter = PlaneScatter(me, scratch)
-    rows = out.shape[0]
-    loads = [
-        me.local(
-            src.at[pl.ds(pl.multiple_of(offsets_of(me, j) * rows, rows), rows)], scatter.blocks.at[j]
-        )
-        for j in range(8)
-    ]
-    yield begin
-    for load in loads:
-        load.start()
-    for j in range(4):
-        loads[j].wait()
-        scatter.core[j].start()
-    yield begin + 1.0
-    for j in range(4, 8):
-        loads[j].wait()
-    yield from scatter.steps(out, unit, begin + 2.5)
+        done.up = True
+        if free is not None:
+            self.me.free_in_plane(free)
 
 
 def params(number, vmem=60 * 2**20):
@@ -1011,7 +1075,7 @@
 
 
 def gain_row(gains, which):
-    return jnp.concatenate([gains[i * 16 + which : i * 16 + which + 1, :] for i in range(8)], axis=1)
+    return jnp.concatenate([gains[i * 8 + which : i * 8 + which + 1, :] for i in range(8)], axis=1)
 
 
 def rotate_heads(values, cos, sin, inverse=False):
@@ -1052,17 +1116,18 @@
             wqkv[:, wide : wide + hd] = w_key[:, j * hd : (j + 1) * hd]
             wqkv[:, wide + hd :] = w_value[:, j * hd : (j + 1) * hd]
 
-    gain_src[...] = jnp.concatenate([gains[...], jnp.zeros((14, gains.shape[1]), f32)], axis=0)
-    me.enter((1, 2, 3, 4))
+    gain_src[...] = jnp.concatenate([gains[...], jnp.zeros((6, gains.shape[1]), f32)], axis=0)
+    me.enter(tuple(range(1, 8)))
+    lanes = att_t.shape[1]
     have_tok, have_gains, have_wqkv, have_wo = Flag(), Flag(), Flag(), Flag()
     progress = Progress(0)
     order = Order(
         z_gather(me, tok, toks, 11.3, 0.0, have_tok),
-        plane_gather(me, gain_src, gains_all, 2.0, 0.0, have_gains),
-        plane_gather(me, wqkv, wqkvs, 7.0, 0.1, have_wqkv),
-        plane_gather(me, wo, wos, 6.0, 8.0, have_wo),
-        plane_gather(me, wg, wg_all, 15.5, 17.0),
-        z_gather(me, cot, cot_all, 11.3, 23.5),
+        plane_direct(me, gain_src, gains_all, have_gains),
+        plane_gather(me, wqkv, wqkvs, 7.0, 0.5, have_wqkv, 0.0),
+        plane_gather(me, wo, wos, 6.0, 11.0, have_wo, 7.5),
+        plane_gather(me, wg, wg_all, 15.5, 20.0, None, 17.0),
+        z_gather(me, cot, cot_all, 11.3, 37.0, None, 27.0),
     )
     c_number = me.x * 2 + me.c
     for i in range(4):
@@ -1100,7 +1165,7 @@
             q_n[h, at, :] = natural[:, h * hd : (h + 1) * hd].astype(bf16)
         kv_own[at, :] = jnp.concatenate([turned[wide:], lin[wide + hd :]], axis=0).T.astype(bf16)
 
-    order.loop(rows // 128, 1.9, project)
+    order.loop(rows // 128, 1.0, project)
 
     def block(i):
         return kv.at[pl.ds(i * rows, rows)]
@@ -1111,7 +1176,7 @@
         copy.start()
     order.pump(order.now + 4.0)
     order.add(plane_gather(me, wu, wu_all, 15.5, order.now))
-    order.add(plane_gather(me, wd, wd_all, 15.5, order.now + 16.0))
+    order.add(plane_gather(me, wd, wd_all, 15.5, order.now + 24.0, None, order.now + 14.0))
     own.wait()
     for copy in copies:
         copy.wait_recv()
@@ -1123,15 +1188,15 @@
     order.until(have_wo)
     save_wo = me.local(wos, wo_all)
     save_wo.start()
-    order.add(
-        z_reduce_all(me, part, total, inbox, across, branch, 45.0, 16, progress, order.now)
-    )
+    for task in z_reduce_all(me, part, total, inbox, across, branch, 45.0, 16, progress, order.now):
+        order.add(task)
 
     def item(i):
         r, h = i // heads, i % heads
-        at = pl.ds(pl.multiple_of(r * 128, 128), 128)
+        at = pl.ds(pl.multiple_of(r * lanes, lanes), lanes)
         s = jnp.dot(kv[:, 0:hd], q_t[h, :, at], preferred_element_type=f32)
-        s = jnp.where(key_pos[...] <= query_pos[0:1, at], s, masked_value)
+        pos = jnp.concatenate([key_pos[...]] * (lanes // 128), axis=1)
+        s = jnp.where(pos <= query_pos[0:1, at], s, masked_value)
         top = jnp.max(s, axis=0, keepdims=True)
         p = jnp.exp(s - top)
         norm = jnp.sum(p, axis=0, keepdims=True)
@@ -1147,10 +1212,10 @@
             part[at, :] = contract_last_dims(natural, wos[...]).astype(bf16)
 
     def before(k):
-        progress.parts = k // heads * 4
+        progress.parts = k // heads * (lanes // 32)
         return False
 
-    order.loop(heads * rows // 128, 0.75, item, before)
+    order.loop(heads * rows // lanes, 1.2, item, before)
     progress.parts = 16
     order.finish()
     for copy in copies:
@@ -1172,7 +1237,7 @@
     def room(a):
         return pltpu.VMEM(a.shape, a.dtype)
 
-    gain_block = shape((16, gains.shape[1]), f32)
+    gain_block = shape((8, gains.shape[1]), f32)
     wqkv = shape(qkv)
     block = shape((rows, width))
     return pl.pallas_call(
@@ -1198,9 +1263,9 @@
             pltpu.VMEM((rows, 2 * HD), bf16),
             pltpu.VMEM((keys, 2 * HD), bf16),
             pltpu.VMEM((HD, keys), bf16),
-            pltpu.VMEM((heads * HD, 128), f32),
+            pltpu.VMEM((heads * HD, 256), f32),
             room(block), room(block), room(block), room(block),
-        ] + dma_sems(192),
+        ] + dma_sems(224),
         compiler_params=params(1),
         name="forward",
     )(stretch_order, tok, w_query, w_key, w_value, gains, frequency, wo, cot, wg, wu, wd)
@@ -1214,30 +1279,89 @@
     return lax.dot_general(left, right, (((1,), (1,)), ((), ())), preferred_element_type=f32)
 
 
+def gain_sums(me, src, out, came, mine, came_z):
+    def block(i):
+        return pl.ds(pl.multiple_of(me.number(i) * 8, 8), 8)
+
+    own = block(0)
+    copies = [me.copy(src.at[block(i)], came.at[i - 1], me.plane(i)) for i in range(1, 8)]
+    again = [
+        me.copy(mine, came_z.at[d - 1], {"head": (me.z + d) % 4}) for d in (1, 2, 3)
+    ]
+
+    def steps(begin):
+        for copy in copies:
+            copy.start()
+        yield begin + 6.0
+        value = src[own, :]
+        for i, copy in enumerate(copies):
+            copy.wait_recv()
+            value = value + came[i]
+        mine[...] = value
+        for copy in again:
+            copy.start()
+        yield begin + 35.0
+        value = mine[...]
+        for d, copy in enumerate(again):
+            copy.wait_recv()
+            value = value + came_z[d]
+        out[...] = value
+        for copy in copies + again:
+            copy.wait_send()
+
+    return steps
+
+
 def backward_kernel(
     part, cot_all, hidden, normed_two, d_gate, d_up, wd_all, tok_all, branch, gains, wo_all,
-    out_t_all, attended_all, q_t_all, q_n_all, kv_all, log_sum, key_pos, query_pos,
-    dwd_own, dwg_own, dwu, out_own, dwo, own, gain_part, dq_t, dkv_own,
-    total, inbox, across, cot, out_part, below, above, q_t, q_n, kv, k_t, came, *rest
+    out_t_all, attended_all, q_t_all, q_n_all, kv_all, wqkv_all, normed_all, log_sum, key_pos, query_pos, cos_t, sin_t,
+    dwd_own, dwg_own, dwu_own, dw_own, dwkv_all, out_own, own, grad_one, gains_out,
+    total, inbox, across, cot, out_part, below, above, q_t, q_n, kv, k_t, came, dq_t,
+    gain_two, gain_parts, came_gain, gain_mine, gain_z, dwkv_own, came_kv, *rest
 ):
-    scratch_d, scratch_g, (ss, rs) = rest[:6], rest[6:12], rest[12:]
+    scratch_d, scratch_g = rest[:6], rest[6:12]
+    free_d, free_g, free_z, ss, rs = rest[12:]
     me = Here(ss, rs)
-    me.enter((1, 2, 3, 4))
+    me.enter(tuple(range(1, 8)), all_z=True)
     z = me.z
     rows, width = part.shape
     heads, hd, _ = q_t.shape
+    wide = heads * hd
+    lin_cols = wide + 2 * hd
     keys = kv.shape[0]
     cols = width // 8
     progress = Progress(16)
-    order = Order(z_reduce_all(me, part, total, inbox, across, None, 45.0, 16, progress))
+    order = Order(*z_reduce_all(me, part, total, inbox, across, None, 45.0, 16, progress))
     down, gate = PlaneScatter(me, scratch_d), PlaneScatter(me, scratch_g)
+    up = PlaneScatter(me, scratch_d)
+    narrow = [ref.at[(slice(None),) * (len(ref.shape) - 1) + (pl.ds(0, lin_cols + wide),)] for ref in scratch_g]
+    both = PlaneScatter(me, narrow)
+    down_done, gate_done, up_done, both_done, out_done, one_done = (Flag() for _ in range(6))
     cot_load = me.local(cot_all, cot)
     cot_load.start()
     later = [me.local(src, dst) for src, dst in ((kv_all, kv), (q_t_all, q_t), (q_n_all, q_n))]
-    stores = [me.slot() for _ in range(4)]
-
-    def weights(left, right_h, right_g, right_u, stage, wd):
-        pairs = ((hidden, right_h), (normed_two, left), (d_gate, right_g), (d_up, right_u))
+    stores = [me.slot() for _ in range(5)]
+    back = [
+        me.copy(kv.at[pl.ds(i * rows, rows)], came.at[i - 1], me.plane(i)) for i in (1, 2, 3)
+    ]
+    kv_sends = [
+        me.copy(dwkv_own, came_kv.at[d - 1], {"head": (z + d) % 4}) for d in (1, 2, 3)
+    ]
+
+    gains_steps = gain_sums(me, gain_parts, gains_out, came_gain, gain_mine, gain_z)
+
+    def columns(j):
+        return pl.ds(pl.multiple_of(offsets_of(me, j) * cols, cols), cols)
+
+    def send(scatter, j):
+        for k in range(4):
+
+            @pl.when(j == k)
+            def _():
+                scatter.core[k].start()
+
+    def weights(left, right_h, right_g, wd):
+        pairs = ((hidden, right_h), (normed_two, left), (d_gate, right_g))
         loads = [me.local(src, dst) for src, dst in pairs]
         for load in loads:
             load.start()
@@ -1247,22 +1371,12 @@
         loads[0].wait()
         order.pump(2.0)
 
-        def columns(j):
-            return pl.ds(pl.multiple_of(offsets_of(me, j) * cols, cols), cols)
-
-        def send(scatter, j):
-            for k in range(4):
-
-                @pl.when(j == k)
-                def _():
-                    scatter.core[k].start()
-
         def down_item(j):
             down.blocks[j] = contract_rows(cot[:, columns(j)], right_h[...]).astype(bf16)
             send(down, j)
 
-        order.loop(8, 0.9, down_item)
-        order.add(down.steps(dwd_own, 15.5, order.now + 0.1))
+        order.loop(8, 0.65, down_item)
+        order.add(down.steps(dwd_own, 16.5, order.now + 0.1, down_done, free_d))
         loads[1].wait()
         loads[2].wait()
 
@@ -1270,25 +1384,8 @@
             gate.blocks[j] = contract_rows(left[:, columns(j)], right_g[...]).astype(bf16)
             send(gate, j)
 
-        order.loop(8, 0.9, gate_item)
-        order.add(gate.steps(dwg_own, 15.5, order.now + 15.0))
-        loads[3].wait()
-
-        def put(j):
-            at = pl.ds(pl.multiple_of(j * cols, cols), cols)
-            return pltpu.make_async_copy(stage.at[j % 2], dwu.at[at], ss.at[stores[0]])
-
-        def up_item(j):
-            @pl.when(j >= 1)
-            def _():
-                put(j - 1).wait()
-
-            at = pl.ds(pl.multiple_of(j * cols, cols), cols)
-            stage[j % 2] = contract_rows(left[:, at], right_u[...]).astype(bf16)
-            put(j).start()
-
-        order.loop(8, 0.9, up_item)
-        put(7).wait()
+        order.loop(8, 0.75, gate_item)
+        order.add(gate.steps(dwg_own, 16.5, order.now + 19.0, gate_done, free_g))
 
         def fetch(j):
             at = pl.ds(pl.multiple_of(j * cols, cols), cols)
@@ -1306,11 +1403,11 @@
             at = pl.ds(pl.multiple_of(j * cols, cols), cols)
             out_part[:, at] = contract_last_dims(right_h[...], wd[j % 2]).astype(bf16)
 
-        order.loop(8, 0.7, out_item)
+        order.loop(8, 1.2, out_item)
 
     units = pltpu.VMEM(hidden.shape, bf16)
     weight = pltpu.VMEM((2, cols, hidden.shape[1]), bf16)
-    pl.run_scoped(weights, pltpu.VMEM(part.shape, bf16), units, units, units, weight, weight)
+    pl.run_scoped(weights, pltpu.VMEM(part.shape, bf16), units, units, weight)
 
     def attention(tok, summed, wo, out_t, attended, g_t, g_n, delta, dk, dv):
         gain = gain_row(gains, 1)
@@ -1339,7 +1436,7 @@
             k_t[:, span] = kv[span, :].astype(f32).T[:hd, :].astype(bf16)
         for load in loads:
             load.wait()
-        order.add(z_reduce_scatter(me, out_part, below, above, out_own, 11.3, 47.0), 47.0)
+        order.add(z_reduce_scatter(me, out_part, below, above, out_own, 12.0, 42.0, out_done), 42.0)
 
         def prepare(r):
             for copy in fetch(r):
@@ -1355,9 +1452,7 @@
             @pl.when(r == z)
             def _():
                 own[...] = grad
-                gain_part[...] = jnp.broadcast_to(
-                    jnp.sum(e * h * inv, axis=0, keepdims=True), gain_part.shape
-                )
+                gain_two[...] = jnp.broadcast_to(jnp.sum(e * h * inv, axis=0, keepdims=True), gain_two.shape)
 
             small = grad.astype(bf16)
             cot[at, :] = small
@@ -1393,31 +1488,21 @@
             dq_t[h, :, at] = (grad * (1.0 / math.sqrt(hd))).astype(bf16)
 
         def before(k):
-            return progress.whole < (k // heads + 1) * 4
-
-        order.loop(heads * rows // 128, 1.2, item, before)
+            return progress.whole() < (k // heads + 1) * 4
+
+        order.loop(heads * rows // 128, 1.25, item, before)
         for i in range(keys // rows):
             span = slice(i * rows, (i + 1) * rows)
             kv[span, :] = jnp.concatenate([dk[span, :], dv[span, :]], axis=1).astype(bf16)
-        copies = [
-            me.copy(kv.at[pl.ds(i * rows, rows)], came.at[i - 1], me.plane(i)) for i in (1, 2, 3)
-        ]
-        for copy in copies:
+        for copy in back:
             copy.start()
-
-        def out_item(i):
-            span = pl.ds(pl.multiple_of(i * cols, cols), cols)
-            dwo[span, :] = contract_rows(cot[:, span], attended[...]).astype(bf16)
-
-        order.loop(8, 0.4, out_item)
-        order.pump(order.now + 2.0)
-        value = kv[0:rows, :].astype(f32)
-        for i, copy in enumerate(copies):
-            copy.wait_recv()
-            value = value + came[i].astype(f32)
-        dkv_own[...] = value
-        for copy in copies:
-            copy.wait_send()
+        order.until(gate_done)
+        pl.semaphore_wait(free_g, 3)
+
+        def low_item(j):
+            both.blocks[j, :, lin_cols:] = contract_rows(cot[:, columns(j)], attended[...]).astype(bf16)
+
+        order.loop(8, 0.4, low_item)
 
     slots = pltpu.VMEM((128, width), bf16)
     pl.run_scoped(
@@ -1433,33 +1518,120 @@
         pltpu.VMEM((keys, hd), f32),
         pltpu.VMEM((keys, hd), f32),
     )
+
+    def last(left, right_u, wqkv, normed, lin, gain_one):
+        tok = cot
+        pairs = ((wqkv_all, wqkv), (normed_two, left), (d_up, right_u), (normed_all, normed), (tok_all, tok))
+        loads = [me.local(src, dst) for src, dst in pairs]
+        for load in loads:
+            load.start()
+        gain_one[...] = jnp.zeros_like(gain_one)
+        order.until(progress.sent_in, progress.sent_out, down_done)
+        pl.semaphore_wait(free_d, 3)
+        loads[1].wait()
+        loads[2].wait()
+
+        def up_item(j):
+            up.blocks[j] = contract_rows(left[:, columns(j)], right_u[...]).astype(bf16)
+            send(up, j)
+
+        order.loop(8, 0.75, up_item)
+        order.add(up.steps(dwu_own, 16.5, order.now + 0.1, up_done))
+        for copy in back:
+            copy.wait_recv()
+        mine = kv[0:rows, :].astype(f32)
+        for i in range(keys // rows - 1):
+            mine = mine + came[i].astype(f32)
+        for copy in back:
+            copy.wait_send()
+        kv[0:rows, :] = mine.astype(bf16)
+        for load in (loads[0], loads[3], loads[4]):
+            load.wait()
+
+        def finish_item(i):
+            at = pl.ds(pl.multiple_of(i * 128, 128), 128)
+            grads_kv = kv[at, :].astype(f32).T
+            grads = jnp.concatenate(
+                [dq_t[h, :, at].astype(f32) for h in range(heads)] + [grads_kv[:hd]], axis=0
+            )
+            grads = rotate_heads(grads, cos_t[:, at], sin_t[:, at], inverse=True)
+            natural = jnp.concatenate([grads, grads_kv[hd:]], axis=0).T.astype(bf16)
+            lin[at, :] = natural
+            one = contract_last_dims(natural, wqkv[...])
+            total[at, :] = one.astype(bf16)
+            x = tok[at, :].astype(f32)
+            inv = lax.rsqrt(jnp.mean(x * x, axis=1, keepdims=True) + norm_epsilon)
+            gain_one[0:1, :] += jnp.sum(one * x * inv, axis=0, keepdims=True)
+
+        order.loop(rows // 128, 2.0, finish_item)
+        for i in range(8):
+            span = slice(i * cols, (i + 1) * cols)
+            gain_parts[i * 8 : (i + 1) * 8, :] = jnp.concatenate(
+                [gain_one[0:1, span], gain_two[0:1, span], jnp.zeros((6, cols), f32)], axis=0
+            )
+        order.until(out_done)
+        me.free_along_z(free_z)
+        order.add(gains_steps(order.now))
+        order.step()
+        me.wait_along_z(free_z)
+        order.add(z_reduce_scatter(me, total, below, above, grad_one, 12.0, order.now, one_done), order.now)
+
+        def both_item(j):
+            both.blocks[j, :, :lin_cols] = contract_rows(normed[:, columns(j)], lin[...]).astype(bf16)
+            send(both, j)
+
+        order.loop(8, 0.5, both_item)
+        order.add(both.steps(dw_own, 13.0, order.now + 0.1, both_done))
+
+    pl.run_scoped(
+        last,
+        pltpu.VMEM(part.shape, bf16),
+        units,
+        pltpu.VMEM(wqkv_all.shape, bf16),
+        pltpu.VMEM(part.shape, bf16),
+        pltpu.VMEM((rows, lin_cols), bf16),
+        pltpu.VMEM((8, width), f32),
+    )
+    order.until(both_done)
+    dwkv_own[...] = dw_own[:, wide:lin_cols].astype(bf16)
+    for copy in kv_sends:
+        copy.start()
     order.finish()
+    for copy in kv_sends:
+        copy.wait_recv()
+    dwkv_all[0] = dwkv_own[...]
+    for d in (1, 2, 3):
+        dwkv_all[d] = came_kv[d - 1]
+    for copy in kv_sends:
+        copy.wait_send()
 
 
 def backward(
     part, cot_all, hidden, normed_two, d_gate, d_up, wd_all, tok_all, branch, gains, wo_all,
-    out_t, attended, q_t, q_n, kv_all, log_sum, key_pos, query_pos
+    out_t, attended, q_t, q_n, kv_all, wqkv_all, normed, log_sum, key_pos, query_pos, cos_t, sin_t
 ):
     heads, hd, rows = q_t.shape
     keys = key_pos.shape[0]
     width = part.shape[1]
+    cols = width // 8
     whole = pltpu.VMEM(part.shape, bf16)
     own = (wd_all.shape[0] // 8, wd_all.shape[1])
+    narrow = wqkv_all.shape[1] + wo_all.shape[1]
     return pl.pallas_call(
         backward_kernel,
         out_shape=(
-            shape(own, f32),
-            shape(own, f32),
-            shape(wd_all.shape),
+            shape(own),
+            shape(own),
+            shape(own),
+            shape((own[0], narrow), f32),
+            shape((4, own[0], 2 * hd)),
             shape((rows // 4, width), f32),
-            shape(wo_all.shape),
             shape((rows // 4, width), f32),
-            shape((8, width), f32),
-            shape((heads, hd, rows)),
-            shape((rows, 2 * hd), f32),
+            shape((rows // 4, width), f32),
+            shape((8, cols), f32),
         ),
-        in_specs=[VM] + [HB] * 8 + [VM] + [HB] * 6 + [VM] * 3,
-        out_specs=[VM, VM, HB] + [VM] * 6,
+        in_specs=[VM] + [HB] * 8 + [VM] + [HB] * 8 + [VM] * 5,
+        out_specs=[VM] * 9,
         scratch_shapes=[whole] * 7
         + [
             pltpu.VMEM(q_t.shape, bf16),
@@ -1467,155 +1639,24 @@
             pltpu.VMEM((keys, 2 * hd), bf16),
             pltpu.VMEM((hd, keys), bf16),
             pltpu.VMEM((keys // rows - 1, rows, 2 * hd), bf16),
+            pltpu.VMEM(q_t.shape, bf16),
+            pltpu.VMEM((8, width), f32),
+            pltpu.VMEM((64, cols), f32),
+            pltpu.VMEM((7, 8, cols), f32),
+            pltpu.VMEM((8, cols), f32),
+            pltpu.VMEM((3, 8, cols), f32),
+            pltpu.VMEM((own[0], 2 * hd), bf16),
+            pltpu.VMEM((3, own[0], 2 * hd), bf16),
         ]
         + plane_scatter_scratch(*own) * 2
-        + dma_sems(160),
+        + [pltpu.SemaphoreType.REGULAR] * 3
+        + dma_sems(224),
         compiler_params=params(4, 67043328),
         name="backward",
     )(
         part, cot_all, hidden, normed_two, d_gate, d_up, wd_all, tok_all, branch, gains, wo_all,
-        out_t, attended, q_t, q_n, kv_all, log_sum, key_pos, query_pos
-    )
-
-
-def finish_kernel(dq_t, dkv, cos_t, sin_t, wqkv, normed, tok, gain_two, one_part, dwqkv, gain_parts, lin):
-    heads = dq_t.shape[0]
-    wide = heads * HD
-    width = tok.shape[1]
-    cols = width // 8
-
-    def body(i, total):
-        at = pl.ds(pl.multiple_of(i * 128, 128), 128)
-        cos, sin = cos_t[:, at], sin_t[:, at]
-        kv = dkv[at, :].astype(bf16).astype(f32).T
-        grads = jnp.concatenate([dq_t[h, :, at].astype(f32) for h in range(heads)] + [kv[:HD]], axis=0)
-        grads = rotate_heads(grads, cos, sin, inverse=True)
-        natural = jnp.concatenate([grads, kv[HD:]], axis=0).T.astype(bf16)
-        lin[at, :] = natural
-        one = contract_last_dims(natural, wqkv[...])
-        one_part[at, :] = one.astype(bf16)
-        x = tok[at, :].astype(f32)
-        inv = lax.rsqrt(jnp.mean(x * x, axis=1, keepdims=True) + norm_epsilon)
-        return total + jnp.sum(one * x * inv, axis=0, keepdims=True)
-
-    total = lax.fori_loop(0, tok.shape[0] // 128, body, jnp.zeros((1, width), f32))
-    for i in range(8):
-        span = slice(i * cols, (i + 1) * cols)
-        gain_parts[i * 8 : (i + 1) * 8, :] = jnp.concatenate(
-            [total[:, span], gain_two[0:1, span], jnp.zeros((6, cols), f32)], axis=0
-        )
-        dwqkv[span, :] = contract_rows(normed[:, span], lin[...]).astype(bf16)
-
-
-def finish(dq_t, dkv, cos_t, sin_t, wqkv, normed, tok, gain_two):
-    width = tok.shape[1]
-    return pl.pallas_call(
-        finish_kernel,
-        out_shape=(shape(tok.shape), shape(wqkv.shape), shape((64, width // 8), f32)),
-        in_specs=[VM] * 8,
-        out_specs=[VM] * 3,
-        scratch_shapes=[pltpu.VMEM((tok.shape[0], wqkv.shape[1]), bf16)],
-        name="finish_attention",
-        **alone(4 * tok.shape[0] * width * wqkv.shape[1]),
-    )(dq_t, dkv, cos_t, sin_t, wqkv, normed, tok, gain_two)
-
-
-def gain_sums(me, src, out, came, mine, came_z):
-    def block(i):
-        return pl.ds(pl.multiple_of(me.number(i) * 8, 8), 8)
-
-    copies = [me.copy(src.at[block(i)], came.at[i - 1], me.plane(i)) for i in range(1, 8)]
-    for copy in copies:
-        copy.start()
-    yield 4.0
-    value = src[block(0), :]
-    for i, copy in enumerate(copies):
-        copy.wait_recv()
-        value = value + came[i]
-    mine[...] = value
-    again = [
-        me.copy(mine, came_z.at[d - 1], {"head": (me.z + d) % 4}) for d in (1, 2, 3)
-    ]
-    for copy in again:
-        copy.start()
-    yield 20.0
-    for d, copy in enumerate(again):
-        copy.wait_recv()
-        value = value + came_z[d]
-    out[...] = value
-    for copy in copies + again:
-        copy.wait_send()
-
-
-def sixth_kernel(
-    part, dwqkv, dwo, dwu, gains,
-    own, dwq_own, dwkv_all, dwo_own, dwu_own, gains_out,
-    below, above, dwqkv_own, dwkv_own, came_kv, came, mine, came_z, *rest
-):
-    *scratch, ss, rs = rest
-    me = Here(ss, rs)
-    me.enter(tuple(range(1, 8)), all_z=True)
-    wide = dwq_own.shape[1]
-
-    def weights():
-        yield from plane_scatter(me, dwqkv, dwqkv_own, scratch[:6], 7.0, 18.0)
-        dwq_own[...] = dwqkv_own[:, :wide]
-        dwkv_own[...] = dwqkv_own[:, wide:].astype(bf16)
-        copies = [
-            me.copy(dwkv_own, came_kv.at[d - 1], {"head": (me.z + d) % 4}) for d in (1, 2, 3)
-        ]
-        for copy in copies:
-            copy.start()
-        yield 45.0
-        for copy in copies:
-            copy.wait_recv()
-        dwkv_all[0] = dwkv_own[...]
-        for d in (1, 2, 3):
-            dwkv_all[d] = came_kv[d - 1]
-        for copy in copies:
-            copy.wait_send()
-
-    drive(
-        gain_sums(me, gains, gains_out, came, mine, came_z),
-        z_reduce_scatter(me, part, below, above, own, 11.3),
-        plane_scatter(me, dwu, dwu_own, scratch[12:], 15.5, 0.1),
-        plane_scatter(me, dwo, dwo_own, scratch[6:12], 8.0, 9.0),
-        weights(),
-    )
-
-
-def sixth(part, dwqkv, dwo, dwu, gains):
-    rows, cols = dwqkv.shape[0] // 8, dwqkv.shape[1]
-    wide = dwo.shape[1]
-    whole = pltpu.VMEM(part.shape, bf16)
-    return pl.pallas_call(
-        sixth_kernel,
-        out_shape=(
-            shape((part.shape[0] // 4, part.shape[1]), f32),
-            shape((rows, wide), f32),
-            shape((4, rows, cols - wide)),
-            shape((rows, wide), f32),
-            shape((rows, dwu.shape[1]), f32),
-            shape((8, gains.shape[1]), f32),
-        ),
-        in_specs=[VM, HB, HB, HB, VM],
-        out_specs=[VM] * 6,
-        scratch_shapes=[
-            whole, whole,
-            pltpu.VMEM((rows, cols), f32),
-            pltpu.VMEM((rows, cols - wide), bf16),
-            pltpu.VMEM((3, rows, cols - wide), bf16),
-            pltpu.VMEM((7, 8, gains.shape[1]), f32),
-            pltpu.VMEM((8, gains.shape[1]), f32),
-            pltpu.VMEM((3, 8, gains.shape[1]), f32),
-        ]
-        + plane_scatter_scratch(rows, cols)
-        + plane_scatter_scratch(rows, wide)
-        + plane_scatter_scratch(rows, dwu.shape[1])
-        + dma_sems(96),
-        compiler_params=params(6),
-        name="scatter_last",
-    )(part, dwqkv, dwo, dwu, gains)
+        out_t, attended, q_t, q_n, kv_all, wqkv_all, normed, log_sum, key_pos, query_pos, cos_t, sin_t
+    )
 
 
 def local_fast(
@@ -1640,7 +1681,7 @@
     ) = forward(
         stretch_order, tokens, w_query, w_key, w_value, gains, frequency, w_out, cotangent, w_gate, w_up, w_down
     )
-    gain_rows = gains_all.reshape(8, 16, cols)
+    gain_rows = gains_all.reshape(8, 8, cols)
     gain_one = gain_rows[:, 0].reshape(width)
     gain_two = gain_rows[:, 1].reshape(width)
     hidden_rows = tok_all.astype(f32) + branch.astype(f32)
@@ -1656,15 +1697,10 @@
     d_up = (grad_hidden * gate_silu).astype(bf16)
     two_part = lax.dot_general(d_gate, wg_all, contract_last, preferred_element_type=f32)
     two_part = two_part + lax.dot_general(d_up, wu_all, contract_last, preferred_element_type=f32)
-    dwd_own, dwg_own, dwu, out_own, dwo, grad_hidden_own, gain_two_part, dq_t, dkv = backward(
+    dwd_own, dwg_own, dwu_own, dw_own, dwkv_all, out_own, grad_hidden_own, grad_one, gain_grads = backward(
         two_part.astype(bf16), cot_all, hidden, normed_two, d_gate, d_up, wd_all, tok_all, branch,
-        gains_all, wo_all, out_t, attended, q_t, q_n, kv_all, log_sum, key_pos, query_pos,
-    )
-    one_part, dwqkv, gain_parts = finish(
-        dq_t, dkv, cos_t, sin_t, wqkv_all, normed, tok_all, gain_two_part
-    )
-    grad_one, dwq_own, dwkv_all, dwo_own, dwu_own, gain_grads = sixth(
-        one_part, dwqkv, dwo, dwu, gain_parts
+        gains_all, wo_all, out_t, attended, q_t, q_n, kv_all, wqkv_all, normed, log_sum, key_pos, query_pos,
+        cos_t, sin_t,
     )
 
     x_own = tokens.astype(f32)
@@ -1679,13 +1715,13 @@
     return (
         layer_low,
         grad_tokens,
-        dwq_own,
+        dw_own[:, : w_query.shape[1]],
         grad_key,
         grad_value,
-        dwo_own,
-        dwg_own,
-        dwu_own,
-        dwd_own,
+        dw_own[:, w_query.shape[1] + 2 * HD :],
+        dwg_own.astype(f32),
+        dwu_own.astype(f32),
+        dwd_own.astype(f32),
         gain_grads[0],
         gain_grads[1],
     )

time: 387 us -> 339 us (0.88)
  Pallas kernels: 343 us -> 293 us
  other arithmetic: 8.11 us -> 12.8 us
    pallas_call x3 -> x1, Pallas kernels: 188 us -> 152 us  [backward(): pl.pallas_call(backward_kernel, out_shape=(shape(own), shape(own), shape(...]
    pallas_call x1, Pallas kernels: 155 us -> 141 us  [forward(): pl.pallas_call(forward_kernel, out_shape=(block, grown(wqkv), grown(gain_...]
    unnamed x47 -> x38, local copies, waits for them, and re-layouts: 6.81 us -> 1.91 us
    convert_element_type x0 -> x3, other arithmetic: none -> 4.78 us  [the longest x1 2.39 us: local_fast(): dwu_own.astype(f32)]
where the time goes in v5:
time: 339 us; the launch traced here: 338 us
  Pallas kernels  293 us (86%)
  matrix products  20.4 us (6%)
  other arithmetic  12.8 us (4%)
  local copies, waits for them, and re-layouts  10.8 us (3%)
    pallas_call x1, Pallas kernels, backward(): pl.pallas_call(backward_kernel, out_shape=(shape(own), shape(own), shape(...  152 us
    pallas_call x1, Pallas kernels, forward(): pl.pallas_call(forward_kernel, out_shape=(block, grown(wqkv), grown(gain_...  141 us

profile of v5, /device:TPU:0, one launch (start us, length us, event | category | flops | bytes accessed | tf_op | source)
XLA Modules:
  0.0 338.4 jit_solution(13417087442070584406)
XLA Ops:
  0.6 0.7 broadcast_in_dim.10
  1.3 0.7 broadcast_in_dim.4
  2.0 0.6 maximum_convert_fusion.1.gains
  2.5 1.3 jit_solution_.3.frequency
  3.9 141.4 %forward.1 = (bf16[512,2048]{1,0:T(8,128)(2,1)}, bf16[2048,640]{1,0:T(8,128)(2,1)}, f32[64,256]{1,0:T(8,128)}, bf16[2048,512]{1,0:T(8,128)(2,1)}, bf16[2048,1408...) custom-call(s32[8]{0:T(128)} %order_ref.1, ...), custom_call_target="tpu_custom_call" | custom-call | tf_op jit(solution)/shard_map/forward/pallas_call | solution.py:1243
  145.3 0.0 copy-start
  145.3 0.0 copy-start.1
  145.3 0.0 copy-start.13
  145.3 3.1 multiply_reduce_fusion
  148.5 2.2 fusion.12
  150.7 0.0 copy-done
  150.7 0.0 copy-done.1
  150.7 0.0 slice-start
  150.7 1.0 multiply_convert_fusion.normed_two
  151.8 0.0 copy-start.2
  151.8 0.0 copy-done.13
  151.8 0.0 slice-start.1
  151.8 0.0 copy-start.5
  151.8 0.0 slice-start.2
  151.8 3.4 %fusion.15 = f32[512,1408]{1,0:T(8,128)S(1)} fusion(bf16[512,2048]{1,0:T(8,128)(2,1)S(1)} %multiply_convert_fusion.normed_two, bf16[2048,1408]{1,0:T(8,128)(2,1)S(1)} %copy-done.13), kind=kOutput, calls=%fused_computation.38 | convolution fusion | flops 2952790016 | bytes 10747904 | tf_op jit(solution)/shard_map/dot_general | solution.py:1690
  155.3 0.0 slice-start.3
  155.3 0.0 slice-done
  155.3 0.0 slice-done.1
  155.3 0.2 copy-done.5
  155.5 3.4 %fusion.14 = f32[512,1408]{1,0:T(8,128)S(1)} fusion(bf16[512,2048]{1,0:T(8,128)(2,1)S(1)} %copy-done.5, bf16[2048,1408]{1,0:T(8,128)(2,1)S(1)} %bitcast.22), kind=kOutput, calls=%fused_computation.37 | convolution fusion | flops 2952790016 | bytes 10747904 | tf_op jit(solution)/shard_map/dot_general | solution.py:1695
  158.9 0.0 copy-done.2
  158.9 0.0 slice-done.2
  158.9 0.0 slice-done.3
  158.9 5.4 %multiply_convert_fusion.1 = (bf16[512,1408]{1,0:T(8,128)(2,1)}, bf16[512,1408]{1,0:T(8,128)(2,1)S(1)}, bf16[512,1408]{1,0:T(8,128)(2,1)S(1)}) fusion(f32[512,1408]{1,0:T(8,128)S(1)} %fusion.15, f32[512,1408]{1,0:T(8,128)S(1)} %fusion.14, bf16[512,2048]{1,0:T(8,128)(2,1)S(1)} %multiply_convert_fusion.normed_two, bf16[2048,1408]{1,0:T(8,128)(2,1)S(1)} %bitcast.32), kind=kOutput, calls=%fused_computation.4 | convolution fusion | flops 2963603456 | bytes 17956864 | tf_op jit(solution)/shard_map/dot_general | solution.py:1691
  164.3 0.0 copy-start.6
  164.3 0.0 copy-start.7
  164.3 3.4 %fusion.16 = f32[512,2048]{1,0:T(8,128)S(1)} fusion(bf16[512,1408]{1,0:T(8,128)(2,1)S(1)} %get-tuple-element.83.d_gate, bf16[2048,1408]{1,0:T(8,128)(2,1)S(1)} %copy-done.13), kind=kOutput, calls=%fused_computation.39 | convolution fusion | flops 2952790016 | bytes 11403264 | tf_op jit(solution)/shard_map/dot_general | solution.py:1698
  167.8 0.0 copy-done.6
  167.8 0.0 copy-done.7
  167.8 4.7 %add_convert_fusion.part = bf16[512,2048]{1,0:T(8,128)(2,1)} fusion(f32[512,2048]{1,0:T(8,128)S(1)} %fusion.16, bf16[512,1408]{1,0:T(8,128)(2,1)S(1)} %get-tuple-element.84.d_up, bf16[2048,1408]{1,0:T(8,128)(2,1)S(1)} %bitcast.32), kind=kOutput, calls=%fused_computation | convolution fusion | flops 2954887168 | bytes 13500416 | tf_op jit(solution)/shard_map/dot_general | solution.py:1699
  172.5 152.0 %backward.1 = (bf16[256,1408]{1,0:T(8,128)(2,1)}, bf16[256,1408]{1,0:T(8,128)(2,1)}, bf16[256,1408]{1,0:T(8,128)(2,1)}, f32[256,1152]{1,0:T(8,128)}, bf16[4,256,...) custom-call(bf16[512,2048]{1,0:T(8,128)(2,1)} %add_convert_fusion.pa, ...), custom_call_target="tpu_custom_call" | custom-call | tf_op jit(solution)/shard_map/backward/pallas_call | solution.py:1620
  324.6 1.0 constant_dynamic-slice_fusion.3
  325.6 0.0 copy-start.11
  325.7 0.2 slice_bitcast_fusion
  325.9 0.2 copy.24
  326.1 0.8 copy.26
  326.9 0.0 copy-start.10
  326.9 0.2 copy.25
  327.1 0.8 copy.27
  327.9 0.0 copy-done.11
  327.9 0.0 copy-start.3
  327.9 0.0 copy-start.4
  327.9 0.0 copy-start.12
  327.9 1.2 convert_element_type.61
  329.1 0.0 copy-start.8
  329.1 2.4 convert_element_type.62
  331.5 0.0 copy-done.10
  331.5 1.2 convert_element_type.63
  332.7 0.0 copy-done.3
  332.7 0.0 copy-done.4
  332.7 0.0 copy-done.12
  332.7 0.3 fusion.3
  333.0 0.0 copy-done.8
  333.1 0.0 copy-start.9
  333.1 2.9 fusion.9
  336.0 0.0 copy-done.9
  336.0 1.1 fusion.11
  337.1 1.3 fusion.13
  (5 shorter events, 0.1 us)
Async XLA Ops:
  145.3 5.4 %copy-start = (bf16[512,2048]{1,0:T(8,128)(2,1)S(1)}, bf16[512,2048]{1,0:T(8,128)(2,1)}, u32[]{:S(2)}) copy-start(bf16[512,2048]{1,0:T(8,128)(2,1)} %get-tuple-element.40.branch) | copy-start | bytes 6291460
  145.3 5.4 %copy-start.1 = (bf16[512,2048]{1,0:T(8,128)(2,1)S(1)}, bf16[512,2048]{1,0:T(8,128)(2,1)}, u32[]{:S(2)}) copy-start(bf16[512,2048]{1,0:T(8,128)(2,1)} %get-tuple-element.43.tok_all) | copy-start | bytes 6291460
  145.3 6.5 %copy-start.13 = (bf16[2048,1408]{1,0:T(8,128)(2,1)S(1)}, bf16[2048,1408]{1,0:T(8,128)(2,1)}, u32[]{:S(2)}) copy-start(bf16[2048,1408]{1,0:T(8,128)(2,1)} %get-tuple-element.46) | copy-start | bytes 17301508
  150.7 4.6 %slice-start = ((s8[5767168]{0:T(1024)(128)(4,1)}), s8[1572864]{0:T(1024)(128)(4,1)S(1)}, s32[]{:S(2)}) async-start(s8[5767168]{0:T(1024)(128)(4,1)} %bitcast.21), calls=%async_computation | async-start | bytes 3145728
  151.8 7.1 %copy-start.2 = (bf16[512,2048]{1,0:T(8,128)(2,1)}, bf16[512,2048]{1,0:T(8,128)(2,1)S(1)}, u32[]{:S(2)}) copy-start(bf16[512,2048]{1,0:T(8,128)(2,1)S(1)} %multiply_convert_fusion.normed_two) | copy-start | bytes 6291460
  151.8 3.5 %slice-start.1 = ((s8[5767168]{0:T(1024)(128)(4,1)}), s8[4194304]{0:T(1024)(128)(4,1)S(1)}, s32[]{:S(2)}) async-start(s8[5767168]{0:T(1024)(128)(4,1)} %bitcast.21), calls=%async_computation.1 | async-start | bytes 8388608
  151.8 3.6 %copy-start.5 = (bf16[512,2048]{1,0:T(8,128)(2,1)S(1)}, bf16[512,2048]{1,0:T(8,128)(2,1)}, u32[]{:S(2)}) copy-start(bf16[512,2048]{1,0:T(8,128)(2,1)} %get-tuple-element.41.cot_all) | copy-start | bytes 6291460
  151.8 7.1 %slice-start.2 = ((s8[5767168]{0:T(1024)(128)(4,1)}), s8[4194304]{0:T(1024)(128)(4,1)S(1)}, s32[]{:S(2)}) async-start(s8[5767168]{0:T(1024)(128)(4,1)} %bitcast.31), calls=%async_computation.2 | async-start | bytes 8388608
  155.3 3.6 %slice-start.3 = ((s8[5767168]{0:T(1024)(128)(4,1)}), s8[1572864]{0:T(1024)(128)(4,1)S(1)}, s32[]{:S(2)}) async-start(s8[5767168]{0:T(1024)(128)(4,1)} %bitcast.31), calls=%async_computation.3 | async-start | bytes 3145728
  164.3 3.5 %copy-start.6 = (bf16[512,1408]{1,0:T(8,128)(2,1)}, bf16[512,1408]{1,0:T(8,128)(2,1)S(1)}, u32[]{:S(2)}) copy-start(bf16[512,1408]{1,0:T(8,128)(2,1)S(1)} %get-tuple-element.83.d_gate) | copy-start | bytes 4325380
  164.3 3.5 %copy-start.7 = (bf16[512,1408]{1,0:T(8,128)(2,1)}, bf16[512,1408]{1,0:T(8,128)(2,1)S(1)}, u32[]{:S(2)}) copy-start(bf16[512,1408]{1,0:T(8,128)(2,1)S(1)} %get-tuple-element.84.d_up) | copy-start | bytes 4325380
  325.6 2.3 copy-start.11
  326.9 4.6 %copy-start.10 = (bf16[256,1408]{1,0:T(8,128)(2,1)S(1)}, bf16[256,1408]{1,0:T(8,128)(2,1)}, u32[]{:S(2)}) copy-start(bf16[256,1408]{1,0:T(8,128)(2,1)} %get-tuple-element.67) | copy-start | bytes 2162692
  327.9 4.8 %copy-start.3 = (bf16[128,2048]{1,0:T(8,128)(2,1)S(1)}, bf16[128,2048]{1,0:T(8,128)(2,1)}, u32[]{:S(2)}) copy-start(bf16[128,2048]{1,0:T(8,128)(2,1)} %tok.1) | copy-start | bytes 1572868
  327.9 4.8 %copy-start.4 = (f32[128,2048]{1,0:T(8,128)S(1)}, f32[128,2048]{1,0:T(8,128)}, u32[]{:S(2)}) copy-start(f32[128,2048]{1,0:T(8,128)} %get-tuple-element.62) | copy-start | bytes 3145732
  327.9 4.8 %copy-start.12 = (f32[8,1,256]{2,1,0:T(1,128)S(1)}, f32[8,1,256]{2,1,0:T(1,128)}, u32[]{:S(2)}) copy-start(f32[8,1,256]{2,1,0:T(1,128)} %get-tuple-element.95) | copy-start | bytes 24580
  329.1 3.9 %copy-start.8 = (f32[128,2048]{1,0:T(8,128)S(1)}, f32[128,2048]{1,0:T(8,128)}, u32[]{:S(2)}) copy-start(f32[128,2048]{1,0:T(8,128)} %get-tuple-element.60) | copy-start | bytes 3145732
  333.1 2.9 copy-start.9

commit v6 on v5

--- a/solution.py
+++ b/solution.py
@@ -789,7 +789,7 @@
         return min(self.crossed, self.left)
 
 
-def z_reduce_all(me, part, total, inbox, across, out, unit, chunks, progress, begin=0.0):
+def z_reduce_all(me, part, total, inbox, across, out, unit, chunks, progress, begin=0.0, lag=0.0):
     rows = part.shape[0] // chunks
     first = [me.slot() for _ in range(chunks)]
     second = [me.slot() for _ in range(chunks)]
@@ -827,7 +827,7 @@
                     for j in new:
                         send_in(j).start()
 
-            time = max(time, begin + 2.0) + hop
+            time = max(time, begin + lag + 2.0) + hop
             yield time
 
             @pl.when(me.middle)
@@ -853,7 +853,7 @@
             while k >= progress.entered:
                 time += 0.5
                 yield time
-            time = max(time, begin + 4.0 + hop) + hop
+            time = max(time, begin + lag + 4.0 + hop) + hop
             yield time
 
             @pl.when(me.middle)
@@ -882,7 +882,7 @@
             while k >= progress.crossed:
                 time += 0.5
                 yield time
-            time = max(time, begin + 6.0 + 2 * hop) + hop
+            time = max(time, begin + lag + 6.0 + 2 * hop) + hop
             yield time
 
             @pl.when(me.end)
@@ -1099,9 +1099,11 @@
 
 def forward_kernel(
     order_ref, tok, w_query, w_key, w_value, gains, frequency, wo, cot, wg, wu, wd,
-    tok_all, wqkv_all, gains_all, wo_all, wg_all, wu_all, wd_all, cot_all, kv_all, branch,
-    normed, q_t, q_n, out_t, attended, log_sum, key_pos, query_pos, cos_t, sin_t,
-    wqkv, gain_src, toks, wqkvs, wos, kv_own, kv, v_t, att_t, part, total, inbox, across, ss, rs
+    tok_all, wqkv_all, gains_all, wo_all, wd_all, cot_all, kv_all, branch,
+    normed_all, q_t_all, q_n_all, out_t_all, attended_all, log_sum, key_pos, query_pos, cos_t, sin_t,
+    normed_two, hidden, d_gate, d_up, two_part,
+    normed, q_t, q_n, out_t, attended, wqkv, gain_src, toks, wqkvs, wos, kv_own, kv, v_t, att_t, part, total, inbox, across,
+    wgs, wus, wds, cots, two, ss, rs
 ):
     me = Here(ss, rs)
     z = me.z
@@ -1120,14 +1122,15 @@
     me.enter(tuple(range(1, 8)))
     lanes = att_t.shape[1]
     have_tok, have_gains, have_wqkv, have_wo = Flag(), Flag(), Flag(), Flag()
+    have_wg, have_wu, have_wd, have_cot = Flag(), Flag(), Flag(), Flag()
     progress = Progress(0)
     order = Order(
         z_gather(me, tok, toks, 11.3, 0.0, have_tok),
         plane_direct(me, gain_src, gains_all, have_gains),
         plane_gather(me, wqkv, wqkvs, 7.0, 0.5, have_wqkv, 0.0),
         plane_gather(me, wo, wos, 6.0, 11.0, have_wo, 7.5),
-        plane_gather(me, wg, wg_all, 15.5, 20.0, None, 17.0),
-        z_gather(me, cot, cot_all, 11.3, 37.0, None, 27.0),
+        plane_gather(me, wg, wgs, 15.5, 20.0, have_wg, 17.0),
+        z_gather(me, cot, cots, 11.3, 37.0, have_cot, 27.0),
     )
     c_number = me.x * 2 + me.c
     for i in range(4):
@@ -1175,8 +1178,8 @@
     for copy in (*copies, own):
         copy.start()
     order.pump(order.now + 4.0)
-    order.add(plane_gather(me, wu, wu_all, 15.5, order.now))
-    order.add(plane_gather(me, wd, wd_all, 15.5, order.now + 24.0, None, order.now + 14.0))
+    order.add(plane_gather(me, wu, wus, 15.5, order.now, have_wu))
+    order.add(plane_gather(me, wd, wds, 15.5, order.now + 24.0, have_wd, order.now + 14.0))
     own.wait()
     for copy in copies:
         copy.wait_recv()
@@ -1188,7 +1191,9 @@
     order.until(have_wo)
     save_wo = me.local(wos, wo_all)
     save_wo.start()
-    for task in z_reduce_all(me, part, total, inbox, across, branch, 45.0, 16, progress, order.now):
+    for task in z_reduce_all(
+        me, part, total, inbox, across, branch, 45.0, 16, progress, order.now, 18.0
+    ):
         order.add(task)
 
     def item(i):
@@ -1217,10 +1222,58 @@
 
     order.loop(heads * rows // lanes, 1.2, item, before)
     progress.parts = 16
+    early = ((normed, normed_all), (q_t, q_t_all), (q_n, q_n_all), (out_t, out_t_all), (attended, attended_all))
+    early = [me.local(*pair) for pair in early]
+    for copy in early:
+        copy.start()
+    late = [me.local(wds, wd_all), me.local(cots, cot_all)]
+    order.until(have_wg, have_wu, have_wd, have_cot)
+    for copy in late:
+        copy.start()
+    gain_mlp = gain_row(gains_all, 1)
+    half = rows // 2
+
+    def norm_two(first):
+        def body(i, _):
+            at = pl.ds(pl.multiple_of(first + i * 64, 64), 64)
+            h = toks[at, :].astype(f32) + total[at, :].astype(f32)
+            inv = lax.rsqrt(jnp.mean(h * h, axis=1, keepdims=True) + norm_epsilon)
+            normed_two[at, :] = (h * inv * gain_mlp).astype(bf16)
+            return 0
+
+        lax.fori_loop(0, half // 64, body, 0)
+
+    def feed(at, span):
+        gate = jnp.dot(normed_two[at, :], wgs[:, span], preferred_element_type=f32)
+        up = jnp.dot(normed_two[at, :], wus[:, span], preferred_element_type=f32)
+        grad = jnp.dot(cots[at, :], wds[:, span], preferred_element_type=f32)
+        sigmoid = jax.nn.sigmoid(gate)
+        silu = gate * sigmoid
+        hidden[at, span] = (silu * up).astype(bf16)
+        grad_gate = (grad * up * sigmoid * (1.0 + gate * (1.0 - sigmoid))).astype(bf16)
+        grad_up = (grad * silu).astype(bf16)
+        d_gate[at, span] = grad_gate
+        d_up[at, span] = grad_up
+        return contract_last_dims(grad_gate, wgs[:, span]) + contract_last_dims(grad_up, wus[:, span])
+
+    def feed_item(j):
+        @pl.when(j == 0)
+        def _():
+            norm_two(0)
+            two[...] = jnp.zeros_like(two)
+
+        two[...] += feed(slice(0, half), pl.ds(pl.multiple_of(j * 128, 128), 128))
+
+    order.loop(hidden.shape[1] // 128, 1.8, feed_item, lambda k: progress.whole() < 8)
+    two_part[:half, :] = two[...].astype(bf16)
+    while progress.whole() < 16:
+        order.step()
+    norm_two(half)
+    two_part[half:, :] = feed(slice(half, rows), slice(None)).astype(bf16)
     order.finish()
     for copy in copies:
         copy.wait_send()
-    for copy in (save, save_wo, *saves):
+    for copy in (save, save_wo, *saves, *early, *late):
         copy.wait()
 
 
@@ -1240,10 +1293,11 @@
     gain_block = shape((8, gains.shape[1]), f32)
     wqkv = shape(qkv)
     block = shape((rows, width))
+    units = shape((rows, wg.shape[1]))
     return pl.pallas_call(
         forward_kernel,
         out_shape=(
-            block, grown(wqkv), grown(gain_block), grown(wo), grown(wg), grown(wu), grown(wd), block,
+            block, grown(wqkv), grown(gain_block), grown(wo), grown(wd), block,
             shape((keys, 2 * HD)), block,
             block,
             shape((heads, HD, rows)),
@@ -1255,18 +1309,25 @@
             shape((8, rows), jnp.int32),
             shape((HD // 2, rows), f32),
             shape((HD // 2, rows), f32),
+            block, units, units, units, block,
         ),
         in_specs=[pl.BlockSpec(memory_space=pltpu.SMEM)] + [VM] * 7 + [HB] * 4,
-        out_specs=[HB, HB, VM] + [HB] * 7 + [VM] * 10,
+        out_specs=[HB, HB, VM] + [HB] * 10 + [VM] * 10,
         scratch_shapes=[
+            room(block),
+            pltpu.VMEM((heads, HD, rows), bf16),
+            pltpu.VMEM((heads, rows, HD), bf16),
+            pltpu.VMEM((heads, HD, rows), f32),
+            pltpu.VMEM((rows, heads * HD), bf16),
             room(wqkv), room(gain_block), room(block), room(grown(wqkv)), room(grown(wo)),
             pltpu.VMEM((rows, 2 * HD), bf16),
             pltpu.VMEM((keys, 2 * HD), bf16),
             pltpu.VMEM((HD, keys), bf16),
             pltpu.VMEM((heads * HD, 256), f32),
             room(block), room(block), room(block), room(block),
+            room(grown(wg)), room(grown(wu)), room(grown(wd)), room(block), pltpu.VMEM((rows // 2, width), f32),
         ] + dma_sems(224),
-        compiler_params=params(1),
+        compiler_params=params(1, 67043328),
         name="forward",
     )(stretch_order, tok, w_query, w_key, w_value, gains, frequency, wo, cot, wg, wu, wd)
 
@@ -1676,29 +1737,16 @@
     frequency = jnp.asarray(np.broadcast_to(frequency.astype(np.float32)[:, None], (HD // 2, 128)))
     gains = jnp.concatenate([gain_attn[None], gain_mlp[None]]).astype(f32)
     (
-        tok_all, wqkv_all, gains_all, wo_all, wg_all, wu_all, wd_all, cot_all, kv_all, branch,
+        tok_all, wqkv_all, gains_all, wo_all, wd_all, cot_all, kv_all, branch,
         normed, q_t, q_n, out_t, attended, log_sum, key_pos, query_pos, cos_t, sin_t,
+        normed_two, hidden, d_gate, d_up, two_part,
     ) = forward(
         stretch_order, tokens, w_query, w_key, w_value, gains, frequency, w_out, cotangent, w_gate, w_up, w_down
     )
     gain_rows = gains_all.reshape(8, 8, cols)
     gain_one = gain_rows[:, 0].reshape(width)
-    gain_two = gain_rows[:, 1].reshape(width)
-    hidden_rows = tok_all.astype(f32) + branch.astype(f32)
-    inv_mlp = lax.rsqrt(jnp.mean(hidden_rows * hidden_rows, axis=-1, keepdims=True) + norm_epsilon)
-    normed_two = (hidden_rows * inv_mlp * gain_two).astype(bf16)
-    gate = jnp.dot(normed_two, wg_all, preferred_element_type=f32)
-    up = jnp.dot(normed_two, wu_all, preferred_element_type=f32)
-    gate_sigmoid = jax.nn.sigmoid(gate)
-    gate_silu = gate * gate_sigmoid
-    hidden = (gate_silu * up).astype(bf16)
-    grad_hidden = jnp.dot(cot_all, wd_all, preferred_element_type=f32)
-    d_gate = (grad_hidden * up * gate_sigmoid * (1.0 + gate * (1.0 - gate_sigmoid))).astype(bf16)
-    d_up = (grad_hidden * gate_silu).astype(bf16)
-    two_part = lax.dot_general(d_gate, wg_all, contract_last, preferred_element_type=f32)
-    two_part = two_part + lax.dot_general(d_up, wu_all, contract_last, preferred_element_type=f32)
     dwd_own, dwg_own, dwu_own, dw_own, dwkv_all, out_own, grad_hidden_own, grad_one, gain_grads = backward(
-        two_part.astype(bf16), cot_all, hidden, normed_two, d_gate, d_up, wd_all, tok_all, branch,
+        two_part, cot_all, hidden, normed_two, d_gate, d_up, wd_all, tok_all, branch,
         gains_all, wo_all, out_t, attended, q_t, q_n, kv_all, wqkv_all, normed, log_sum, key_pos, query_pos,
         cos_t, sin_t,
     )

time: 339 us -> 322 us (0.950)
  matrix products: 20.4 us -> 0 us
  Pallas kernels: 293 us -> 304 us
  other arithmetic: 12.8 us -> 7.45 us
    dot_general x5 -> x0, matrix products: 20.4 us -> none  [the longest x1 5.41 us: local_fast(): up = jnp.dot(normed_two, wu_all, preferred_element_type=f32)]
    pallas_call x1, Pallas kernels: 141 us -> 151 us  [forward(): pl.pallas_call(forward_kernel, out_shape=(block, grown(wqkv), grown(gain_...]
where the time goes in v6:
time: 322 us
  Pallas kernels  304 us (94%)
  local copies, waits for them, and re-layouts  9.16 us (3%)
  other arithmetic  7.45 us (2%)
    pallas_call x1, Pallas kernels, backward(): pl.pallas_call(backward_kernel, out_shape=(shape(own), shape(own), shape(...  153 us
    pallas_call x1, Pallas kernels, forward(): pl.pallas_call(forward_kernel, out_shape=(block, grown(wqkv), grown(gain_...  151 us

profile of v6, /device:TPU:0, one launch (start us, length us, event | category | flops | bytes accessed | tf_op | source)
XLA Modules:
  0.0 321.6 jit_solution(14600747376505676514)
XLA Ops:
  0.6 0.7 broadcast_in_dim.8
  1.3 0.7 broadcast_in_dim.9
  2.0 0.6 maximum_convert_fusion.1.gains
  2.5 1.3 jit_solution_.3.frequency
  3.9 151.5 %forward.1 = (bf16[512,2048]{1,0:T(8,128)(2,1)}, bf16[2048,640]{1,0:T(8,128)(2,1)}, f32[64,256]{1,0:T(8,128)}, bf16[2048,512]{1,0:T(8,128)(2,1)}, bf16[2048,1408...) custom-call(s32[8]{0:T(128)} %order_ref.1, ...), custom_call_target="tpu_custom_call" | custom-call | tf_op jit(solution)/shard_map/forward/pallas_call | solution.py:1297
  155.4 152.7 %backward.1 = (bf16[256,1408]{1,0:T(8,128)(2,1)}, bf16[256,1408]{1,0:T(8,128)(2,1)}, bf16[256,1408]{1,0:T(8,128)(2,1)}, f32[256,1152]{1,0:T(8,128)}, bf16[4,256,...) custom-call(bf16[512,2048]{1,0:T(8,128)(2,1)} %get-tuple-element.44., ...), custom_call_target="tpu_custom_call" | custom-call | tf_op jit(solution)/shard_map/backward/pallas_call | solution.py:1681
  308.1 1.0 constant_dynamic-slice_fusion.3
  309.1 0.0 copy-start.6
  309.2 0.2 slice_bitcast_fusion
  309.4 0.2 copy.24
  309.5 0.0 copy-start.5
  309.6 0.8 copy.26
  310.4 0.2 copy.25
  310.6 0.8 copy.27
  311.4 0.0 copy-done.6
  311.4 0.0 copy-start.4
  311.4 1.2 convert_element_type.33
  312.6 0.0 copy-done.5
  312.6 0.0 copy-start
  312.6 0.0 copy-start.1
  312.6 1.2 convert_element_type.34
  313.8 0.0 copy-start.2
  313.8 0.0 copy-done.4
  313.8 1.2 convert_element_type.35
  315.0 0.8 slice.28
  315.9 0.0 copy-done
  315.9 0.0 copy-done.1
  315.9 0.3 fusion.2
  316.2 0.0 copy-done.2
  316.2 0.0 copy-start.3
  316.2 2.9 fusion.8
  319.1 0.0 copy-done.3
  319.1 1.1 fusion.10
  320.2 1.3 fusion.11
  (2 shorter events, 0.1 us)
Async XLA Ops:
  309.1 2.3 copy-start.6
  309.5 3.1 copy-start.5
  311.4 2.4 copy-start.4
  312.6 3.2 %copy-start = (bf16[128,2048]{1,0:T(8,128)(2,1)S(1)}, bf16[128,2048]{1,0:T(8,128)(2,1)}, u32[]{:S(2)}) copy-start(bf16[128,2048]{1,0:T(8,128)(2,1)} %tok.1) | copy-start | bytes 1572868
  312.6 3.2 %copy-start.1 = (f32[128,2048]{1,0:T(8,128)S(1)}, f32[128,2048]{1,0:T(8,128)}, u32[]{:S(2)}) copy-start(f32[128,2048]{1,0:T(8,128)} %get-tuple-element.68) | copy-start | bytes 3145732
  313.8 2.4 copy-start.2
  316.2 2.9 copy-start.3

commit v7 on v6

--- a/solution.py
+++ b/solution.py
@@ -1353,7 +1353,7 @@
     def steps(begin):
         for copy in copies:
             copy.start()
-        yield begin + 6.0
+        yield begin + 13.0
         value = src[own, :]
         for i, copy in enumerate(copies):
             copy.wait_recv()
@@ -1361,7 +1361,7 @@
         mine[...] = value
         for copy in again:
             copy.start()
-        yield begin + 35.0
+        yield begin + 40.0
         value = mine[...]
         for d, copy in enumerate(again):
             copy.wait_recv()
@@ -1587,17 +1587,7 @@
         for load in loads:
             load.start()
         gain_one[...] = jnp.zeros_like(gain_one)
-        order.until(progress.sent_in, progress.sent_out, down_done)
-        pl.semaphore_wait(free_d, 3)
-        loads[1].wait()
-        loads[2].wait()
-
-        def up_item(j):
-            up.blocks[j] = contract_rows(left[:, columns(j)], right_u[...]).astype(bf16)
-            send(up, j)
-
-        order.loop(8, 0.75, up_item)
-        order.add(up.steps(dwu_own, 16.5, order.now + 0.1, up_done))
+        order.until(progress.sent_in, progress.sent_out)
         for copy in back:
             copy.wait_recv()
         mine = kv[0:rows, :].astype(f32)
@@ -1637,6 +1627,17 @@
         me.wait_along_z(free_z)
         order.add(z_reduce_scatter(me, total, below, above, grad_one, 12.0, order.now, one_done), order.now)
 
+        order.until(down_done)
+        pl.semaphore_wait(free_d, 3)
+        loads[1].wait()
+        loads[2].wait()
+
+        def up_item(j):
+            up.blocks[j] = contract_rows(left[:, columns(j)], right_u[...]).astype(bf16)
+            send(up, j)
+
+        order.loop(8, 0.75, up_item)
+        order.add(up.steps(dwu_own, 16.5, order.now + 0.1, up_done))
         def both_item(j):
             both.blocks[j, :, :lin_cols] = contract_rows(normed[:, columns(j)], lin[...]).astype(bf16)
             send(both, j)

time: 322 us -> 330 us (1.025)
  Pallas kernels: 304 us -> 312 us
    pallas_call x1, Pallas kernels: 153 us -> 160 us  [backward(): pl.pallas_call(backward_kernel, out_shape=(shape(own), shape(own), shape(...]
where the time goes in v7:
time: 330 us; the launch traced here: 329 us
  Pallas kernels  312 us (95%)
  local copies, waits for them, and re-layouts  9.16 us (3%)
  other arithmetic  7.45 us (2%)
    pallas_call x1, Pallas kernels, backward(): pl.pallas_call(backward_kernel, out_shape=(shape(own), shape(own), shape(...  160 us
    pallas_call x1, Pallas kernels, forward(): pl.pallas_call(forward_kernel, out_shape=(block, grown(wqkv), grown(gain_...  151 us

profile of v7, /device:TPU:0, one launch (start us, length us, event | category | flops | bytes accessed | tf_op | source)
XLA Modules:
  0.0 329.3 jit_solution(16140192589374886313)
XLA Ops:
  0.6 0.7 broadcast_in_dim.8
  1.3 0.7 broadcast_in_dim.9
  2.0 0.6 maximum_convert_fusion.1.gains
  2.5 1.3 jit_solution_.3.frequency
  3.9 151.5 %forward.1 = (bf16[512,2048]{1,0:T(8,128)(2,1)}, bf16[2048,640]{1,0:T(8,128)(2,1)}, f32[64,256]{1,0:T(8,128)}, bf16[2048,512]{1,0:T(8,128)(2,1)}, bf16[2048,1408...) custom-call(s32[8]{0:T(128)} %order_ref.1, ...), custom_call_target="tpu_custom_call" | custom-call | tf_op jit(solution)/shard_map/forward/pallas_call | solution.py:1297
  155.4 160.3 %backward.1 = (bf16[256,1408]{1,0:T(8,128)(2,1)}, bf16[256,1408]{1,0:T(8,128)(2,1)}, bf16[256,1408]{1,0:T(8,128)(2,1)}, f32[256,1152]{1,0:T(8,128)}, bf16[4,256,...) custom-call(bf16[512,2048]{1,0:T(8,128)(2,1)} %get-tuple-element.44., ...), custom_call_target="tpu_custom_call" | custom-call | tf_op jit(solution)/shard_map/backward/pallas_call | solution.py:1682
  315.8 1.0 constant_dynamic-slice_fusion.3
  316.8 0.0 copy-start.6
  316.8 0.2 slice_bitcast_fusion
  317.0 0.2 copy.24
  317.2 0.0 copy-start.5
  317.2 0.8 copy.26
  318.1 0.2 copy.25
  318.3 0.8 copy.27
  319.1 0.0 copy-done.6
  319.1 0.0 copy-start.4
  319.1 1.2 convert_element_type.33
  320.3 0.0 copy-done.5
  320.3 0.0 copy-start
  320.3 0.0 copy-start.1
  320.3 1.2 convert_element_type.34
  321.5 0.0 copy-start.2
  321.5 0.0 copy-done.4
  321.5 1.2 convert_element_type.35
  322.7 0.8 slice.28
  323.5 0.0 copy-done
  323.5 0.0 copy-done.1
  323.6 0.3 fusion.2
  323.9 0.0 copy-done.2
  323.9 0.0 copy-start.3
  323.9 2.9 fusion.8
  326.8 0.0 copy-done.3
  326.8 1.1 fusion.10
  327.9 1.3 fusion.11
  (2 shorter events, 0.1 us)
Async XLA Ops:
  316.8 2.3 copy-start.6
  317.2 3.1 copy-start.5
  319.1 2.4 copy-start.4
  320.3 3.2 copy-start
  320.3 3.2 copy-start.1
  321.5 2.4 copy-start.2
  323.9 2.9 copy-start.3

commit v8 on v6

--- a/solution.py
+++ b/solution.py
@@ -1353,7 +1353,7 @@
     def steps(begin):
         for copy in copies:
             copy.start()
-        yield begin + 6.0
+        yield begin + 13.0
         value = src[own, :]
         for i, copy in enumerate(copies):
             copy.wait_recv()
@@ -1361,7 +1361,7 @@
         mine[...] = value
         for copy in again:
             copy.start()
-        yield begin + 35.0
+        yield begin + 40.0
         value = mine[...]
         for d, copy in enumerate(again):
             copy.wait_recv()

time: 322 us -> 320 us (level)
  no operation moved by 1% of the time
where the time goes in v8:
time: 320 us; the launch traced here: 319 us
  Pallas kernels  302 us (94%)
  local copies, waits for them, and re-layouts  9.16 us (3%)
  other arithmetic  7.45 us (2%)
    pallas_call x1, Pallas kernels, forward(): pl.pallas_call(forward_kernel, out_shape=(block, grown(wqkv), grown(gain_...  151 us
    pallas_call x1, Pallas kernels, backward(): pl.pallas_call(backward_kernel, out_shape=(shape(own), shape(own), shape(...  150 us

profile of v8, /device:TPU:0, one launch (start us, length us, event | category | flops | bytes accessed | tf_op | source)
XLA Modules:
  0.0 319.3 jit_solution(17597614314118894757)
XLA Ops:
  0.6 0.7 broadcast_in_dim.8
  1.3 0.7 broadcast_in_dim.9
  2.0 0.6 maximum_convert_fusion.1.gains
  2.5 1.3 jit_solution_.3.frequency
  3.9 151.5 %forward.1 = (bf16[512,2048]{1,0:T(8,128)(2,1)}, bf16[2048,640]{1,0:T(8,128)(2,1)}, f32[64,256]{1,0:T(8,128)}, bf16[2048,512]{1,0:T(8,128)(2,1)}, bf16[2048,1408...) custom-call(s32[8]{0:T(128)} %order_ref.1, ...), custom_call_target="tpu_custom_call" | custom-call | tf_op jit(solution)/shard_map/forward/pallas_call | solution.py:1297
  155.4 150.4 %backward.1 = (bf16[256,1408]{1,0:T(8,128)(2,1)}, bf16[256,1408]{1,0:T(8,128)(2,1)}, bf16[256,1408]{1,0:T(8,128)(2,1)}, f32[256,1152]{1,0:T(8,128)}, bf16[4,256,...) custom-call(bf16[512,2048]{1,0:T(8,128)(2,1)} %get-tuple-element.44., ...), custom_call_target="tpu_custom_call" | custom-call | tf_op jit(solution)/shard_map/backward/pallas_call | solution.py:1681
  305.9 1.0 constant_dynamic-slice_fusion.3
  306.9 0.0 copy-start.6
  306.9 0.2 slice_bitcast_fusion
  307.1 0.2 copy.24
  307.3 0.0 copy-start.5
  307.3 0.8 copy.26
  308.1 0.2 copy.25
  308.3 0.8 copy.27
  309.2 0.0 copy-done.6
  309.2 0.0 copy-start.4
  309.2 1.2 convert_element_type.33
  310.4 0.0 copy-done.5
  310.4 0.0 copy-start
  310.4 0.0 copy-start.1
  310.4 1.2 convert_element_type.34
  311.6 0.0 copy-start.2
  311.6 0.0 copy-done.4
  311.6 1.2 convert_element_type.35
  312.8 0.8 slice.28
  313.6 0.0 copy-done
  313.6 0.0 copy-done.1
  313.6 0.3 fusion.2
  313.9 0.0 copy-done.2
  313.9 0.0 copy-start.3
  313.9 2.9 fusion.8
  316.9 0.0 copy-done.3
  316.9 1.1 fusion.10
  318.0 1.3 fusion.11
  (2 shorter events, 0.1 us)
Async XLA Ops:
  306.9 2.3 copy-start.6
  307.3 3.1 copy-start.5
  309.2 2.4 copy-start.4
  310.4 3.2 %copy-start = (bf16[128,2048]{1,0:T(8,128)(2,1)S(1)}, bf16[128,2048]{1,0:T(8,128)(2,1)}, u32[]{:S(2)}) copy-start(bf16[128,2048]{1,0:T(8,128)(2,1)} %tok.1) | copy-start | bytes 1572868
  310.4 3.2 %copy-start.1 = (f32[128,2048]{1,0:T(8,128)S(1)}, f32[128,2048]{1,0:T(8,128)}, u32[]{:S(2)}) copy-start(f32[128,2048]{1,0:T(8,128)} %get-tuple-element.68) | copy-start | bytes 3145732
  311.6 2.4 copy-start.2
  313.9 2.9 copy-start.3
